TPU v7x, 32 devices: a 4x4x1 block of a 4x4x8 slice. The times are simulated.
32 devices in a mesh: pod: 1 (over z), data: 4 (over y), stage: 8 (over x, core).
Axes of the slice: x: 4, y: 4, z: 1, core: 2. Of those that a mesh axis runs over, the one named last changes fastest.
The devices are a block of a 4x4x8 slice.
Arguments:
- x_last: bfloat16 [16384, 768], P(('pod', 'data', 'stage'))
- w_head: bfloat16 [50304, 768], P('stage')
- labels: int32 [16384], P(('pod', 'data'))
- loss_mask: int32 [16384], P(('pod', 'data'))
- w_embed: bfloat16 [50304, 768], P('stage')
- tok_ids: int32 [16384], P(('pod', 'data'))
- act_in: bfloat16 [131072, 768], P(('pod', 'data', 'stage'))
- w_up: bfloat16 [8, 768, 3072], P('stage')
- w_down: bfloat16 [8, 3072, 768], P('stage')
Outputs:
- output 1: float32 [1], P('pod')
- output 2: float32 [16384, 768], P(('pod', 'data', 'stage'))
- output 3: bfloat16 [50304, 768], P(('pod', 'stage'))
- output 4: bfloat16 [16384, 768], P(('pod', 'data', 'stage'))
- output 5: bfloat16 [131072, 768], P(('pod', 'data', 'stage'))
All inputs are finite; a program needn't handle non-finite values.
Results may differ from a plain program's by a relative error of at most 0.001.
Values are sent between devices in bfloat16 or wider.
A program may use at most 768 MiB of HBM per device.

v0:
```python
import jax
import jax.numpy as jnp
from jax import lax
from jax.sharding import PartitionSpec as P


def solution(mesh):
    n_data = mesh.shape['data']
    tok_spec = P(('pod', 'data', 'stage'), None)
    rep_spec = P(('pod', 'data'))
    vocab_spec = P('stage', None)
    layer_spec = P('stage', None, None)

    def local_step(x_rows, w_head, labels, loss_mask, w_embed, tok_ids, act_in, w_up, w_down):
        stage_idx = lax.axis_index('stage')
        slice_rows = w_head.shape[0]
        offset = stage_idx * slice_rows
        x_full = lax.all_gather(x_rows, 'stage', axis=0, tiled=True)
        logits = jnp.einsum('td,vd->tv', x_full, w_head, preferred_element_type=jnp.float32)
        loc_max = jnp.max(logits, axis=1)
        shifted = jnp.exp(logits - loc_max[:, None])
        loc_sum = jnp.sum(shifted, axis=1)
        col_ids = lax.broadcasted_iota(jnp.int32, (1, slice_rows), 1) + offset
        is_label = labels[:, None] == col_ids
        loc_target = jnp.sum(jnp.where(is_label, logits, 0.0), axis=1)
        glob_max = lax.pmax(loc_max, 'stage')
        rescale = jnp.exp(loc_max - glob_max)
        stat_sums = lax.psum(jnp.stack([loc_sum * rescale, loc_target]), 'stage')
        total_sum = stat_sums[0]
        target = stat_sums[1]
        weights = loss_mask.astype(jnp.float32)
        loss_denom = jnp.maximum(jnp.sum(weights), 1.0)
        rep_loss = jnp.sum(weights * (jnp.log(total_sum) + glob_max - target)) / loss_denom
        mean_loss = lax.psum(rep_loss, 'data') / n_data
        soft_probs = shifted * (rescale / total_sum)[:, None]
        row_scale = (weights / loss_denom)[:, None]
        grad_logits = (jnp.where(is_label, soft_probs - 1.0, soft_probs) * row_scale).astype(jnp.bfloat16)
        dx_part = jnp.dot(grad_logits, w_head, preferred_element_type=jnp.float32)
        grad_x = lax.psum_scatter(dx_part, 'stage', scatter_dimension=0, tiled=True)
        dw_part = jnp.einsum('tv,td->vd', grad_logits, x_full, preferred_element_type=jnp.float32)
        grad_head = (lax.psum(dw_part, 'data') / n_data).astype(jnp.bfloat16)
        local_ids = tok_ids - offset
        in_slice = (local_ids >= 0) & (local_ids < slice_rows)
        rows_emb = jnp.take(w_embed, jnp.clip(local_ids, 0, slice_rows - 1), axis=0)
        emb_part = jnp.where(in_slice[:, None], rows_emb, jnp.zeros_like(rows_emb))
        embed_out = lax.psum_scatter(emb_part, 'stage', scatter_dimension=0, tiled=True)
        hidden = jax.nn.gelu(jnp.dot(act_in, w_up[0], preferred_element_type=jnp.float32)).astype(jnp.bfloat16)
        mlp_f32 = act_in.astype(jnp.float32) + jnp.dot(hidden, w_down[0], preferred_element_type=jnp.float32)
        return mean_loss.reshape(1), grad_x, grad_head, embed_out, mlp_f32.astype(jnp.bfloat16)

    return jax.shard_map(local_step, mesh=mesh, in_specs=(tok_spec, vocab_spec, rep_spec, rep_spec, vocab_spec, rep_spec, tok_spec, layer_spec, layer_spec), out_specs=(P('pod'), tok_spec, P(('pod', 'stage'), None), tok_spec, tok_spec), check_vma=False)
```

profile of v0, /device:TPU:97, one launch (start us, length us, event | category | flops | bytes accessed | tf_op | source)
XLA Modules:
  0.0 737.5 jit_solution(7403523519024867974)
XLA Ops:
  7.2 0.1 all-gather.2.cloned.1.call-start
  7.2 0.7 all-gather.2.cloned.1.call-update
  8.0 0.1 all-reduce.2.cloned.1.call-start
  8.1 0.0 copy-start
  8.1 43.9 %all-gather.2.cloned.1.call-done = bf16[4096,768]{1,0:T(8,128)(2,1)} async-done(((bf16[512,768]{1,0:T(8,128)(2,1)}), bf16[4096,768]{1,0:T(8,128)(2,1)}) %all-gather.2.cloned.1.call-update) | async-done | bytes 6291472 | tf_op jit(solution)/shard_map/all_gather | solution.py:18
  52.0 51.6 %fusion.29 = (f32[4096]{0:T(1024)S(1)}, f32[4096,6288]{0,1:T(8,128)}) fusion(bf16[4096,768]{1,0:T(8,128)(2,1)} %all-gather.2.cloned.1.call-done, bf16[6288,768]{1,0:T(8,128)(2,1)} %param.10), kind=kOutput, calls=%fused_computation.41 | convolution fusion | flops 39586426880 | bytes 118988800 | tf_op jit(solution)/shard_map/td,vd->tv/dot_general | solution.py:19
  103.6 20.8 %pmax.7 = f32[4096]{0:T(1024)S(1)} all-reduce(f32[4096]{0:T(1024)S(1)} %get-tuple-element.14), channel_id=1, replica_groups=mesh['pod'=1,'data'=4,'stage'=8] {'stage'}, use_global_device_ids=true, to_apply=%region_2.3 | all-reduce | flops 4096 | bytes 32768 | tf_op jit(solution)/shard_map/pmax | solution.py:26
  124.4 0.0 copy-done
  124.4 0.0 copy-start.1
  124.4 33.1 %fusion.3 = (f32[4096]{0:T(1024)S(1)}, f32[4096]{0:T(1024)S(1)}) fusion(f32[4096,6288]{0,1:T(8,128)} %get-tuple-element.15, f32[4096]{0:T(1024)S(1)} %get-tuple-element.14, s32[6288]{0:T(1024)S(1)} %iota_add_fusion, s32[4096]{0:T(1024)S(1)} %copy-done), kind=kLoop, calls=%fused_computation.7 | loop fusion | flops 128770048 | bytes 103113280 | tf_op jit(solution)/shard_map/reduce_sum | solution.py:22
  157.6 23.8 %psum.21 = f32[2,4096]{1,0:T(2,128)S(1)} all-reduce(f32[2,4096]{1,0:T(2,128)S(1)} %pad_maximum_fusion), channel_id=1, replica_groups=mesh['pod'=1,'data'=4,'stage'=8] {'stage'}, use_global_device_ids=true, to_apply=%region_4.5 | all-reduce | flops 8192 | bytes 65536 | tf_op jit(solution)/shard_map/psum | solution.py:28
  181.5 0.0 copy-done.1
  181.5 0.6 convert_reduce_fusion
  182.8 50.1 %fusion.2 = bf16[4096,6288]{0,1:T(8,128)(2,1)} fusion(f32[4096,6288]{0,1:T(8,128)} %get-tuple-element.15, f32[4096]{0:T(1024)S(1)} %convert_divide_fusion, f32[4096]{0:T(1024)S(1)} %get-tuple-element.9, s32[4096]{0:T(1024)S(1)} %copy-done, f32[4096]{0:T(1024)S(1)} %get-tuple-element.14, s32[6288]{0:T(1024)S(1)} %iota_add_fusion), kind=kLoop, calls=%fused_computation.5 | loop fusion | flops 180289536 | bytes 154624576 | tf_op jit(solution)/shard_map/convert_element_type | solution.py:37
  232.8 48.5 %fusion.31 = f32[6288,768]{1,0:T(8,128)} fusion(bf16[4096,6288]{0,1:T(8,128)(2,1)} %fusion.2, bf16[4096,768]{1,0:T(8,128)(2,1)} %all-gather.2.cloned.1.call-done), kind=kOutput, calls=%fused_computation.43 | convolution fusion | flops 39560675328 | bytes 77119488 | tf_op jit(solution)/shard_map/tv,td->vd/dot_general | solution.py:40
  281.4 0.0 copy-start.2
  281.4 0.1 all-reduce.2.cloned.1.call-update
  281.4 0.1 reduce-scatter.5.cloned.1.call-start
  281.5 0.6 copy-done.2
  282.1 24.0 %gather_fusion = bf16[4096,768]{1,0:T(8,128)(2,1)} fusion(bf16[6288,768]{1,0:T(8,128)(2,1)} %param.13, s32[4096]{0:T(1024)S(1)} %fusion.21), kind=kCustom, calls=%fused_computation | custom fusion | bytes 12599296 | tf_op jit(solution)/shard_map/jit(_take)/gather | solution.py:44
  306.2 8.0 %select_select_fusion = bf16[4096,768]{1,0:T(8,128)(2,1)} fusion(bf16[4096,768]{1,0:T(8,128)(2,1)} %gather_fusion, pred[4096]{0:T(1024)(128)(4,1)S(1)} %get-tuple-element.13, pred[4096]{0:T(1024)(128)(4,1)S(1)} %get-tuple-element.12), kind=kLoop, calls=%fused_computation.21 | loop fusion | flops 6291456 | bytes 12591104 | tf_op jit(solution)/shard_map/jit(_where)/select_n | solution.py:45
  314.1 0.1 reduce-scatter.5.cloned.1.call-update
  314.2 0.3 reduce-scatter.3.cloned.1.call-start
  314.5 49.3 %fusion.30 = f32[4096,768]{1,0:T(8,128)} fusion(bf16[4096,6288]{0,1:T(8,128)(2,1)} %fusion.2, bf16[6288,768]{1,0:T(8,128)(2,1)} %param.10), kind=kOutput, calls=%fused_computation.42 | convolution fusion | flops 39560675328 | bytes 73752576 | tf_op jit(solution)/shard_map/dot_general | solution.py:38
  363.8 0.1 reduce-scatter.3.cloned.1.call-update
  363.9 36.9 %fusion.48 = bf16[4096,3072]{1,0:T(8,128)(2,1)} fusion(bf16[4096,768]{1,0:T(8,128)(2,1)} %param.15, bf16[1,768,3072]{2,1,0:T(8,128)(2,1)} %param.16), kind=kOutput, calls=%fused_computation.16.clone.clone.clone.clone.1 | convolution fusion | flops 19440599040 | bytes 36175872 | tf_op jit(solution)/shard_map/dot_general | solution.py:47
  401.5 27.2 %add_convert_fusion = bf16[4096,768]{1,0:T(8,128)(2,1)} fusion(bf16[4096,768]{1,0:T(8,128)(2,1)} %param.15, bf16[1,3072,768]{2,1,0:T(8,128)(2,1)} %param.17, bf16[4096,3072]{1,0:T(8,128)(2,1)} %fusion.48), kind=kOutput, calls=%fused_computation.19 | convolution fusion | flops 19336790016 | bytes 42467328 | tf_op jit(solution)/shard_map/dot_general | solution.py:48
  428.7 10.1 %psum.22 = f32[]{:T(128)} all-reduce(f32[]{:T(128)S(6)} %div.21), channel_id=1, replica_groups=mesh['pod'=1,'data'=4,'stage'=8] {'data'}, use_global_device_ids=true, to_apply=%region_7.8 | all-reduce | flops 1 | bytes 8 | tf_op jit(solution)/shard_map/psum | solution.py:34
  439.4 175.0 %all-reduce.2.cloned.1.call-done = f32[6288,768]{1,0:T(8,128)} async-done(((f32[6288,768]{1,0:T(8,128)}), f32[6288,768]{1,0:T(8,128)}) %all-reduce.2.cloned.1.call-update) | async-done | bytes 19316752 | tf_op jit(solution)/shard_map/psum | solution.py:41
  614.5 11.6 %multiply_convert_fusion = bf16[6288,768]{1,0:T(8,128)(2,1)} fusion(f32[6288,768]{1,0:T(8,128)} %all-reduce.2.cloned.1.call-done), kind=kLoop, calls=%fused_computation.18 | loop fusion | flops 9658368 | bytes 28975104 | tf_op jit(solution)/shard_map/convert_element_type | solution.py:41
  626.1 31.0 %reduce-scatter.5.cloned.1.call-done = bf16[512,768]{1,0:T(8,128)(2,1)} async-done(((bf16[4096,768]{1,0:T(8,128)(2,1)}), bf16[512,768]{1,0:T(8,128)(2,1)}) %reduce-scatter.5.cloned.1.call-update) | async-done | bytes 786448 | tf_op jit(solution)/shard_map/reduce_scatter | solution.py:46
  657.1 72.3 %reduce-scatter.3.cloned.1.call-done = f32[512,768]{1,0:T(8,128)} async-done(((f32[4096,768]{1,0:T(8,128)}), f32[512,768]{1,0:T(8,128)}) %reduce-scatter.3.cloned.1.call-update) | async-done | bytes 1572880 | tf_op jit(solution)/shard_map/reduce_scatter | solution.py:39
  (7 shorter events, 0.1 us)
Async XLA Ops:
  7.2 44.8 %all-gather.2.cloned.1.call-start = ((), (), s32[]{:S(2)}) async-start(), calls=%async_computation.2 | async-start | bytes 7077888 | tf_op jit(solution)/shard_map/all_gather | solution.py:18
  8.0 606.5 %all-reduce.2.cloned.1.call-start = ((), (), s32[]{:S(2)}) async-start(), calls=%async_computation.4 | async-start | bytes 38633472 | tf_op jit(solution)/shard_map/psum | solution.py:41
  8.1 116.4 %copy-start = (s32[4096]{0:T(1024)S(1)}, s32[4096]{0:T(1024)}, u32[]{:S(2)}) copy-start(s32[4096]{0:T(1024)} %param.11) | copy-start | bytes 49156
  124.4 57.0 %copy-start.1 = (s32[4096]{0:T(1024)S(1)}, s32[4096]{0:T(1024)}, u32[]{:S(2)}) copy-start(s32[4096]{0:T(1024)} %param.12) | copy-start | bytes 49156
  281.4 0.7 copy-start.2
  281.4 375.6 %reduce-scatter.5.cloned.1.call-start = ((), (), s32[]{:S(2)}) async-start(), calls=%async_computation.5 | async-start | bytes 7077888 | tf_op jit(solution)/shard_map/reduce_scatter | solution.py:46
  314.2 415.2 %reduce-scatter.3.cloned.1.call-start = ((), (), s32[]{:S(2)}) async-start(), calls=%async_computation.3 | async-start | bytes 14155776 | tf_op jit(solution)/shard_map/reduce_scatter | solution.py:39
Sparse Core Ops, SparseCore 0:
  9.6 42.3 all-gather.1
  281.6 332.8 all-reduce.1
  617.4 39.6 reduce-scatter.4
  659.8 69.5 reduce-scatter.2
where the time goes:
time: 744 us; the launch traced here: 738 us
  waiting for transfers between devices  323 us (43%)
  matrix products  214 us (29%)
  other arithmetic  103 us (14%)
  blocking collectives  54.8 us (7%)
  local copies, waits for them, and re-layouts  24.7 us (3%)
  between operations  17.4 us (2%)
    psum x1, waiting for transfers between devices, local_step(): grad_head = (lax.psum(dw_part, 'data') / n_data).astype(jnp.bfloat16)  175 us
    reduce_scatter x1, waiting for transfers between devices, local_step(): grad_x = lax.psum_scatter(dx_part, 'stage', scatter_dimension=0, tiled=True)  72.3 us
    dot_general x1, matrix products, local_step(): jnp.einsum('td,vd->tv', x_full, w_head, preferred_element_type=jnp.float32)  51.6 us
    convert_element_type x1, other arithmetic, local_step(): (jnp.where(is_label, soft_probs - 1.0, soft_probs) * row_scale).astype(jn...  50.1 us
    dot_general x1, matrix products, local_step(): dx_part = jnp.dot(grad_logits, w_head, preferred_element_type=jnp.float32)  49.3 us
    dot_general x1, matrix products, local_step(): jnp.einsum('tv,td->vd', grad_logits, x_full, preferred_element_type=jnp.f...  48.5 us
    all_gather x1, waiting for transfers between devices, local_step(): x_full = lax.all_gather(x_rows, 'stage', axis=0, tiled=True)  43.9 us
    dot_general x1, matrix products, local_step(): jnp.dot(act_in, w_up[0], preferred_element_type=jnp.float32)  36.9 us
  transfers between devices with their start and end apart: 4, of which 4 were waited for; matrix products, arithmetic and copies ran while one was open for 21% of the time, Pallas kernels for 0%

commit v1 on v0

v1 whole, which is shorter than its diff:
```python
import functools

import jax
import jax.numpy as jnp
from jax import lax
from jax.experimental import pallas as pl
from jax.experimental.pallas import tpu as pltpu
from jax.sharding import PartitionSpec as P

MESH = pl.DeviceIdType.MESH
F32 = jnp.float32
BF16 = jnp.bfloat16
N_TILE = 6
MLP_EIGHTHS = (2, 3, 3)
LOW = -1e30


def _params(mib=60, **kw):
    return pltpu.CompilerParams(vmem_limit_bytes=mib * 2**20, **kw)


def _cost(flops, nbytes, trans=0):
    return pl.CostEstimate(flops=int(flops), bytes_accessed=int(nbytes), transcendentals=int(trans))


def _mlp_body(a_ref, w1_ref, w2_ref, *rest, chunk):
    o_ref, u_ref = rest[-2:]
    ff = w1_ref.shape[1]
    for c in range(ff // chunk):
        cs = slice(c * chunk, (c + 1) * chunk)
        h = jnp.dot(a_ref[...], w1_ref[:, cs], preferred_element_type=F32)
        u_ref[:, cs] = jax.nn.gelu(h).astype(BF16)
    y = jnp.dot(u_ref[...], w2_ref[...], preferred_element_type=F32)
    o_ref[...] = (a_ref[...].astype(F32) + y).astype(BF16)


def mlp(a, w1, w2, out, first, count, tb=512):
    n, d = a.shape
    ff = w1.shape[1]
    extra = [] if out is None else [out]
    return pl.pallas_call(
        functools.partial(_mlp_body, chunk=512),
        grid=(count,),
        in_specs=[
            pl.BlockSpec((tb, d), lambda i: (first + i, 0)),
            pl.BlockSpec((d, ff), lambda i: (0, 0)),
            pl.BlockSpec((ff, d), lambda i: (0, 0)),
        ] + [pl.BlockSpec(memory_space=pl.ANY)] * len(extra),
        out_specs=pl.BlockSpec((tb, d), lambda i: (first + i, 0)),
        out_shape=jax.ShapeDtypeStruct((n, d), BF16),
        scratch_shapes=[pltpu.VMEM((tb, ff), BF16)],
        input_output_aliases={3: 0} if extra else {},
        compiler_params=_params(),
        cost_estimate=_cost(4 * count * tb * d * ff, 4 * count * tb * d + 4 * d * ff, count * tb * ff),
        name="mlp",
    )(a, w1, w2, *extra)


def _logits_body(lo_ref, lab_ref, x_ref, w_ref, z_ref, st_ref, *, vt):
    tb = x_ref.shape[0]
    lab8 = jnp.broadcast_to(lab_ref[0:1, :], (8, tb))
    sub = lax.broadcasted_iota(jnp.int32, (vt // 8, 8, tb), 0) * 8 + lax.broadcasted_iota(jnp.int32, (vt // 8, 8, tb), 1)
    m8 = s8 = t8 = None
    for v in range(w_ref.shape[0] // vt):
        vs = slice(v * vt, (v + 1) * vt)
        z = lax.dot_general(w_ref[vs, :], x_ref[...], (((1,), (1,)), ((), ())), preferred_element_type=F32)
        if v == 0:
            z = jnp.where(lax.broadcasted_iota(jnp.int32, (vt, tb), 0) >= lo_ref[0], z, LOW)
        z_ref[0, vs, :] = z
        zr = z_ref[0, vs, :].reshape(vt // 8, 8, tb)
        tile_max = jnp.max(zr, axis=0)
        m_new = tile_max if v == 0 else jnp.maximum(m8, tile_max)
        e_sum = jnp.sum(jnp.exp(zr - m_new[None]), axis=0)
        hit = jnp.sum(jnp.where(sub == (lab8 - v * vt)[None], zr, 0.0), axis=0)
        s8 = e_sum if v == 0 else s8 * jnp.exp(m8 - m_new) + e_sum
        t8 = hit if v == 0 else t8 + hit
        m8 = m_new
    m = jnp.max(m8, axis=0, keepdims=True)
    s = jnp.sum(s8 * jnp.exp(m8 - m), axis=0, keepdims=True)
    t = jnp.sum(t8, axis=0, keepdims=True)
    st_ref[...] = jnp.concatenate([m, s, t, jnp.zeros((5, tb), F32)], axis=0)


def logits(lo, lab, x, w, vt, tb=512):
    n, d = x.shape
    win = w.shape[0]
    return pl.pallas_call(
        functools.partial(_logits_body, vt=vt),
        grid=(n // tb,),
        in_specs=[
            pl.BlockSpec(memory_space=pltpu.SMEM),
            pl.BlockSpec((1, tb), lambda i: (0, i)),
            pl.BlockSpec((tb, d), lambda i: (i, 0)),
            pl.BlockSpec((win, d), lambda i: (0, 0)),
        ],
        out_specs=[
            pl.BlockSpec((1, win, tb), lambda i: (0, 0, i)),
            pl.BlockSpec((8, tb), lambda i: (0, i)),
        ],
        out_shape=[jax.ShapeDtypeStruct((1, win, n), F32), jax.ShapeDtypeStruct((8, n), F32)],
        compiler_params=_params(),
        cost_estimate=_cost(2 * n * d * win, 4 * n * win + 2 * d * (n + win), n * win),
        name="logits",
    )(lo, lab, x, w)


def _stats_body(mask_ref, sp_ref, so_ref, out_ref, got, mine, coef, send1, recv1, send2, recv2, *, n_stage):
    y, s = lax.axis_index("data"), lax.axis_index("stage")
    rows = sp_ref.shape[1] // n_stage
    peers = [(f, k) for f in range(2) for k in range(n_stage) if (f, k) != (0, 0)]

    def where_to(f, k):
        y_to = y if f == 0 else y + 1 - 2 * lax.rem(y, 2)
        return {"data": y_to, "stage": lax.rem(s + k, n_stage)}

    def cols(stage):
        return pl.ds(pl.multiple_of(stage * rows, rows), rows)

    barrier = pltpu.get_barrier_semaphore()
    for f, k in peers:
        pl.semaphore_signal(barrier, inc=1, device_id=where_to(f, k), device_id_type=MESH)
    pl.semaphore_wait(barrier, len(peers))

    first = []
    for f, k in peers:
        src = so_ref if f == 0 else sp_ref
        slot = f * n_stage + k
        c = pltpu.make_async_remote_copy(
            src_ref=src.at[:, cols(lax.rem(s + k, n_stage))],
            dst_ref=got.at[slot],
            send_sem=send1.at[slot],
            recv_sem=recv1.at[slot],
            device_id=where_to(f, k),
            device_id_type=MESH,
        )
        c.start()
        first.append(c)
    weight = mask_ref[...].astype(F32)
    denom = jnp.maximum(jnp.sum(weight), 1.0)
    mu = mask_ref[:, cols(s)].astype(F32)
    own = so_ref[:, cols(s)]
    for c in first:
        c.wait_recv()
    parts = [own] + [got[f * n_stage + k] for f, k in peers]
    m = functools.reduce(jnp.maximum, [p[0:1, :] for p in parts])
    z = sum(p[1:2, :] * jnp.exp(p[0:1, :] - m) for p in parts)
    t = sum(p[2:3, :] for p in parts)
    scale = mu / denom
    loss = scale * (jnp.log(z) + m - t)
    res = jnp.concatenate([m, scale / z, scale, loss, jnp.zeros((4, rows), F32)], axis=0)
    mine[...] = res
    second = []
    for f, k in peers:
        slot = f * n_stage + k
        c = pltpu.make_async_remote_copy(
            src_ref=mine,
            dst_ref=coef.at[1 - f, :, cols(s)],
            send_sem=send2.at[slot],
            recv_sem=recv2.at[slot],
            device_id=where_to(f, k),
            device_id_type=MESH,
        )
        c.start()
        second.append(c)
    coef[1, :, cols(s)] = res
    for c in first:
        c.wait_send()
    for c in second:
        c.wait_recv()
    out_ref[...] = coef[...]
    for c in second:
        c.wait_send()


def stats(mask, st_p, st_o, n_stage):
    n = st_p.shape[1]
    rows = n // n_stage
    vm = pl.BlockSpec(memory_space=pltpu.VMEM)
    slots = 2 * n_stage
    dma = pltpu.SemaphoreType.DMA((slots,))
    return pl.pallas_call(
        functools.partial(_stats_body, n_stage=n_stage),
        in_specs=[vm] * 3,
        out_specs=vm,
        out_shape=jax.ShapeDtypeStruct((2, 8, n), F32),
        scratch_shapes=[
            pltpu.VMEM((slots, 8, rows), F32),
            pltpu.VMEM((8, rows), F32),
            pltpu.VMEM((2, 8, n), F32),
            dma, dma, dma, dma,
        ],
        compiler_params=_params(32, collective_id=0, has_side_effects=True),
        cost_estimate=_cost(10**9, 10**7),
        name="stats",
    )(mask, st_p, st_o)


def _gdw_body(tile_ref, coef_ref, lab_ref, zp_ref, zo_ref, xp_ref, xo_ref, gin_ref, g_ref, dw_ref, gs, *, ch):
    del gin_ref
    t = pl.program_id(0)
    vt, tb = dw_ref.shape[0], coef_ref.shape[2]
    row0 = tile_ref[0] * vt
    sub = lax.broadcasted_iota(jnp.int32, (vt // 8, 8, ch), 0) * 8 + lax.broadcasted_iota(jnp.int32, (vt // 8, 8, ch), 1)

    def run(z_ref, x_ref, t_local):
        acc = None
        for c in range(tb // ch):
            cs = slice(c * ch, (c + 1) * ch)
            m8 = jnp.broadcast_to(coef_ref[0, 0:1, cs], (8, ch))
            c8 = jnp.broadcast_to(coef_ref[0, 1:2, cs], (8, ch))
            r8 = jnp.broadcast_to(coef_ref[0, 2:3, cs], (8, ch))
            lab8 = jnp.broadcast_to(lab_ref[0:1, cs], (8, ch)) - row0
            zr = z_ref[0, :, cs].reshape(vt // 8, 8, ch)
            e = jnp.exp(zr - m8[None]) * c8[None]
            g = jnp.where(sub == lab8[None], e - r8[None], e)
            gb = g.reshape(vt, ch).astype(BF16)
            g_ref[0, :, cs] = gb
            xb = x_ref[pl.ds(pl.multiple_of(t_local * tb + c * ch, ch), ch), :]
            d = jnp.dot(gb, xb, preferred_element_type=F32)
            acc = d if acc is None else acc + d
        dw_ref[...] = jnp.where(t == 0, 0.0, dw_ref[...]) + acc

    half = pl.num_programs(0) // 2

    @pl.when(t < half)
    def _():
        run(zp_ref, xp_ref, t)

    @pl.when(t >= half)
    def _():
        run(zo_ref, xo_ref, t - half)


def gdw(tile, coef, lab, z_p, z_o, x_p, x_o, g, vt, tb=2048, ch=512):
    n, d = x_p.shape
    win = z_p.shape[1]
    tb = min(tb, n)
    nt = n // tb
    spec = pltpu.PrefetchScalarGridSpec(
        num_scalar_prefetch=1,
        grid=(2 * nt,),
        in_specs=[
            pl.BlockSpec((1, 8, tb), lambda t, i: (t // nt, 0, t % nt)),
            pl.BlockSpec((1, tb), lambda t, i: (0, t)),
            pl.BlockSpec((1, vt, tb), lambda t, i: (0, i[0], jnp.minimum(t, nt - 1))),
            pl.BlockSpec((1, vt, tb), lambda t, i: (0, i[0], jnp.maximum(t - nt, 0))),
            pl.BlockSpec((n, d), lambda t, i: (0, 0), pipeline_mode=pl.Buffered(1)),
            pl.BlockSpec((n, d), lambda t, i: (0, 0), pipeline_mode=pl.Buffered(1)),
            pl.BlockSpec(memory_space=pl.ANY),
        ],
        out_specs=[
            pl.BlockSpec((1, vt, tb), lambda t, i: (t // nt, i[0], t % nt)),
            pl.BlockSpec((vt, d), lambda t, i: (0, 0)),
        ],
        scratch_shapes=[pltpu.VMEM((vt, ch), BF16)],
    )
    kw = {}
    args = [tile, coef, lab, z_p, z_o, x_p, x_o]
    if g is None:
        g = jnp.zeros((8, 128), BF16)
    else:
        kw["input_output_aliases"] = {7: 0}
    return pl.pallas_call(
        functools.partial(_gdw_body, ch=ch),
        grid_spec=spec,
        out_shape=[jax.ShapeDtypeStruct((2, win, n), BF16), jax.ShapeDtypeStruct((vt, d), F32)],
        compiler_params=_params(62),
        cost_estimate=_cost(4 * n * d * vt, 12 * n * vt + 4 * n * d, 2 * n * vt),
        name="gdw",
        **kw,
    )(*args, g)


def _dx_body(g_ref, w_ref, o_ref):
    o_ref[...] = lax.dot_general(g_ref[0], w_ref[...], (((0,), (0,)), ((), ())), preferred_element_type=F32)


def dx(g, w, role, tb=512):
    n = g.shape[2]
    win, d = w.shape
    return pl.pallas_call(
        _dx_body,
        grid=(n // tb,),
        in_specs=[
            pl.BlockSpec((1, win, tb), lambda i: (role, 0, i)),
            pl.BlockSpec((win, d), lambda i: (0, 0)),
        ],
        out_specs=pl.BlockSpec((tb, d), lambda i: (i, 0)),
        out_shape=jax.ShapeDtypeStruct((n, d), F32),
        compiler_params=_params(),
        cost_estimate=_cost(2 * n * d * win, 2 * n * win + 4 * n * d),
        name="dx",
    )(g, w)


def solution(mesh):
    n_data, n_stage = mesh.shape["data"], mesh.shape["stage"]
    tok_spec = P(("pod", "data", "stage"), None)
    rep_spec = P(("pod", "data"))
    vocab_spec = P("stage", None)
    layer_spec = P("stage", None, None)
    swap_a = [(i, i ^ 1) for i in range(n_data)]
    swap_b = [(i, n_data - 1 - i) for i in range(n_data)]

    def local_step(x_rows, w_head, labels, loss_mask, w_embed, tok_ids, act_in, w_up, w_down):
        y, s = lax.axis_index("data"), lax.axis_index("stage")
        shard, d = w_head.shape
        yh = y >> 1
        h = (y ^ yh) & 1
        vt = -(-shard // (2 * N_TILE * 16)) * 16
        win = N_TILE * vt
        first_row = shard - win
        lo = (2 * win - shard) * h

        def over_a(v):
            return lax.ppermute(v, "data", swap_a)

        def over_b(v):
            return lax.ppermute(v, "data", swap_b)

        w_win = lax.dynamic_slice(w_head, (h * first_row, 0), (win, d))
        lab_a = over_a(labels)
        x_a = over_a(x_rows)
        x_o = lax.all_gather(x_rows, "stage", axis=0, tiled=True)
        x_p = lax.all_gather(x_a, "stage", axis=0, tiled=True)

        def local(lab):
            lab = lab - (s * shard + h * first_row)
            return jnp.where(lab < lo, -1, lab)

        lab = jnp.concatenate([local(lab_a), local(labels)]).reshape(1, -1)
        lo_arr = lo.reshape(1)
        n_tok = labels.shape[0]
        mlp_out, done = None, 0
        for part in MLP_EIGHTHS:
            count = n_tok // 512 * part // 8
            mlp_out = mlp(act_in, w_up[0], w_down[0], mlp_out, done, count)
            done += count

        offset = s * shard
        local_ids = tok_ids - offset
        in_slice = (local_ids >= 0) & (local_ids < shard)
        rows_emb = jnp.take(w_embed, jnp.clip(local_ids, 0, shard - 1), axis=0)
        emb_part = jnp.where(in_slice[:, None], rows_emb, jnp.zeros_like(rows_emb))
        embed_out = lax.psum_scatter(emb_part, "stage", scatter_dimension=0, tiled=True)

        z_o, st_o = logits(lo_arr, lab[:, n_tok:], x_o, w_win, vt)
        z_p, st_p = logits(lo_arr, lab[:, :n_tok], x_p, w_win, vt)
        coef = stats(loss_mask.reshape(1, -1), st_p, st_o, n_stage)

        loss_two = jnp.sum(coef[:, 3, :], axis=1)
        loss_pair = loss_two[0] + loss_two[1]
        loss_far = over_b(loss_pair.reshape(1, 1))[0, 0]
        mean_loss = (loss_pair + loss_far) / n_data

        half = N_TILE // 2
        g = None
        sent, kept = [], []
        for j in range(half):
            tile = ((1 - yh) * half + j).reshape(1)
            g, dw = gdw(tile, coef, lab, z_p, z_o, x_p, x_o, g, vt)
            sent.append(over_b(dw))
        for j in range(half):
            tile = (yh * half + j).reshape(1)
            g, dw = gdw(tile, coef, lab, z_p, z_o, x_p, x_o, g, vt)
            kept.append(dw)

        dx_p = dx(g, w_win, 0)
        rs_p = lax.psum_scatter(dx_p, "stage", scatter_dimension=0, tiled=True)
        dx_o = dx(g, w_win, 1)
        rs_o = lax.psum_scatter(dx_o, "stage", scatter_dimension=0, tiled=True)
        gx_a = over_a(rs_p)
        grad_x = rs_o + gx_a

        grad_head = jnp.zeros((shard, d), BF16)
        for j in range(half):
            fin = lax.optimization_barrier(((kept[j] + sent[j]) / n_data).astype(BF16))
            fin_b = over_b(fin)
            fin_a = over_a(fin)
            fin_ab = over_a(fin_b)
            for v, hh, part in ((fin, h, yh), (fin_a, 1 - h, yh), (fin_b, h, 1 - yh), (fin_ab, 1 - h, 1 - yh)):
                row = hh * first_row + (part * half + j) * vt
                grad_head = lax.dynamic_update_slice(grad_head, v, (row, 0))

        return mean_loss.reshape(1), grad_x, grad_head, embed_out, mlp_out

    return jax.shard_map(
        local_step,
        mesh=mesh,
        in_specs=(tok_spec, vocab_spec, rep_spec, rep_spec, vocab_spec, rep_spec, tok_spec, layer_spec, layer_spec),
        out_specs=(P("pod"), tok_spec, P(("pod", "stage"), None), tok_spec, tok_spec),
        check_vma=False,
    )
```

time: 744 us -> 632 us (0.85)
  Pallas kernels: 0 us -> 310 us
  matrix products: 214 us -> 0 us
  waiting for transfers between devices: 323 us -> 126 us
  starting transfers between devices: 0.46 us -> 93.3 us
  other arithmetic: 103 us -> 18.5 us
  blocking collectives: 54.8 us -> 0 us
  local copies, waits for them, and re-layouts: 24.7 us -> 56.9 us
    pallas_call x0 -> x14, Pallas kernels: none -> 310 us  [the longest x6 115 us: gdw(): pl.pallas_call(functools.partial(_gdw_body, ch=ch), grid_spec=spec, out_s...]
    dot_general x5 -> x0, matrix products: 214 us -> none  [the longest x1 51.6 us: local_step(): jnp.einsum('td,vd->tv', x_full, w_head, preferred_element_type=jnp.float32)]
    psum x1 -> x0, waiting for transfers between devices: 175 us -> none  [local_step(): grad_head = (lax.psum(dw_part, 'data') / n_data).astype(jnp.bfloat16)]
    ppermute x0 -> x16, waiting for transfers between devices: none -> 102 us  [the longest x9 101 us: over_a(): return lax.ppermute(v, 'data', swap_a)]
    ppermute x0 -> x16, starting transfers between devices: none -> 93 us  [the longest x7 84.5 us: over_b(): return lax.ppermute(v, 'data', swap_b)]
    reduce_scatter x1 -> x2, waiting for transfers between devices: 72.3 us -> 0.01 us  [the longest x1 0.01 us: local_step(): rs_p = lax.psum_scatter(dx_p, 'stage', scatter_dimension=0, tiled=True)]
    convert_element_type x2 -> x3, other arithmetic: 61.7 us -> 6.07 us  [local_step(): fin = lax.optimization_barrier(((kept[j] + sent[j]) / n_data).astype(BF16))]
    psum x2 -> x0, blocking collectives: 34 us -> none  [the longest x1 23.8 us: local_step(): stat_sums = lax.psum(jnp.stack([loc_sum * rescale, loc_target]), 'stage')]
  transfers between devices with their start and end apart: 4 -> 21, of which waited for: 4 -> 8; matrix products, arithmetic and copies ran while one was open for 21% -> 12% of each run, Pallas kernels for 0% -> 19%
where the time goes in v1:
time: 632 us; the launch traced here: 622 us
  Pallas kernels  310 us (49%)
  waiting for transfers between devices  126 us (20%)
  starting transfers between devices  93.3 us (15%)
  local copies, waits for them, and re-layouts  56.9 us (9%)
  other arithmetic  18.5 us (3%)
  between operations  17.4 us (3%)
    pallas_call x6, Pallas kernels, gdw(): pl.pallas_call(functools.partial(_gdw_body, ch=ch), grid_spec=spec, out_s...  115 us
    ppermute x9, waiting for transfers between devices, over_a(): return lax.ppermute(v, 'data', swap_a)  101 us
    ppermute x7, starting transfers between devices, over_b(): return lax.ppermute(v, 'data', swap_b)  84.5 us
    pallas_call x2, Pallas kernels, logits(): pl.pallas_call(functools.partial(_logits_body, vt=vt), grid=(n // tb,), i...  67.3 us
    pallas_call x3, Pallas kernels, mlp(): pl.pallas_call(functools.partial(_mlp_body, chunk=512), grid=(count,), in...  57.4 us
    pallas_call x2, Pallas kernels, dx(): pl.pallas_call(_dx_body, grid=(n // tb,), in_specs=[pl.BlockSpec((1, win,...  55.1 us
    gather x1, local copies, waits for them, and re-layouts, local_step(): rows_emb = jnp.take(w_embed, jnp.clip(local_ids, 0, shard - 1), axis=0)  24.4 us
    dynamic_update_slice x12, local copies, waits for them, and re-layouts, local_step(): grad_head = lax.dynamic_update_slice(grad_head, v, (row, 0))  18.1 us
  transfers between devices with their start and end apart: 21, of which 8 were waited for; matrix products, arithmetic and copies ran while one was open for 12% of the time, Pallas kernels for 19%

profile of v1, /device:TPU:97, one launch (start us, length us, event | category | flops | bytes accessed | tf_op | source)
XLA Modules:
  0.0 621.7 jit_solution(5403987428669820635)
XLA Ops:
  8.1 2.8 collective-permute-start.1
  10.8 17.2 %collective-permute-done.1 = bf16[512,768]{1,0:T(8,128)(2,1)S(1)} collective-permute-done((bf16[512,768]{1,0:T(8,128)(2,1)}, bf16[512,768]{1,0:T(8,128)(2,1)S(1)}, u32[]{:S(2)}, u32[]{:S(2)}) %collective-permute-start.1) | collective-permute-done | bytes 786464 | tf_op jit(solution)/shard_map/ppermute | solution.py:316
  30.7 5.0 constant_dynamic-slice_fusion.w_ref
  36.5 15.8 %all-gather.5.cloned.1.call-done.x_ref.xo_ref = bf16[4096,768]{1,0:T(8,128)(2,1)} async-done(((bf16[512,768]{1,0:T(8,128)(2,1)}), bf16[4096,768]{1,0:T(8,128)(2,1)}) %all-gather.5.cloned.1.call-update) | async-done | bytes 6291472 | tf_op jit(solution)/shard_map/all_gather | solution.py:324
  52.3 33.6 %logits.3 = (f32[1,3168,4096]{2,1,0:T(8,128)}, f32[8,4096]{1,0:T(8,128)}) custom-call(s32[1]{0:T(128)} %bitcast.1.lo_ref, s32[1,4096]{1,0:T(1,128)} %get-tuple-element.37.lab_ref, bf16[4096,768]{1,0:T(8,128)(2,1)} %all-gather.5.cloned.1.call-done.x_ref.xo_ref, bf16[3168,768]{1,0:T(8,128)(2,1)} %constant_dynamic-slice_fusion.w_ref), custom_call_target="tpu_custom_call" | custom-call | flops 19931332608 | bytes 63062016 | tf_op jit(solution)/shard_map/logits/pallas_call | solution.py:87
  85.9 6.9 %all-gather.3.cloned.1.call-done.x_ref.xp_ref = bf16[4096,768]{1,0:T(8,128)(2,1)} async-done(((bf16[512,768]{1,0:T(8,128)(2,1)}), bf16[4096,768]{1,0:T(8,128)(2,1)}) %all-gather.3.cloned.1.call-update) | async-done | bytes 6291472 | tf_op jit(solution)/shard_map/all_gather | solution.py:325
  92.8 33.7 %logits.2 = (f32[1,3168,4096]{2,1,0:T(8,128)}, f32[8,4096]{1,0:T(8,128)}) custom-call(s32[1]{0:T(128)} %bitcast.1.lo_ref, s32[1,4096]{1,0:T(1,128)} %get-tuple-element.38.lab_ref, bf16[4096,768]{1,0:T(8,128)(2,1)} %all-gather.3.cloned.1.call-done.x_ref.xp_ref, bf16[3168,768]{1,0:T(8,128)(2,1)} %constant_dynamic-slice_fusion.w_ref), custom_call_target="tpu_custom_call" | custom-call | flops 19931332608 | bytes 63062016 | tf_op jit(solution)/shard_map/logits/pallas_call | solution.py:87
  127.4 14.9 %stats.1.coef_ref = f32[2,8,4096]{2,1,0:T(8,128)S(1)} custom-call(s32[1,4096]{1,0:T(1,128)S(1)} %bitcast.15, f32[8,4096]{1,0:T(8,128)S(1)} %copy-done.3, f32[8,4096]{1,0:T(8,128)S(1)} %copy-done.2), custom_call_target="tpu_custom_call" | custom-call | flops 1000000000 | bytes 10000000 | tf_op jit(solution)/shard_map/stats/pallas_call | solution.py:181
  143.6 19.0 %gdw.6 = (bf16[2,3168,4096]{2,1,0:T(8,128)(2,1)}, f32[528,768]{1,0:T(8,128)}) custom-call(s32[1]{0:T(128)} %bitcast.12.tile_ref, f32[2,8,4096]{2,1,0:T(8,128)} %copy-done, s32[1,8192]{1,0:T(1,128)} %bitcast.17, f32[1,3168,4096]{2,1,0:T(8,128)} %get-tuple-element.23.zp_ref, f32[1,3168,4096]{2,1,0:T(8,128)} %get-tuple-element.24.zo_ref, ...), custom_call_target="tpu_custom_call" | custom-call | flops 6643777536 | bytes 38535168 | tf_op jit(solution)/shard_map/gdw/pallas_call | solution.py:263
  162.6 19.2 %gdw.7 = (bf16[2,3168,4096]{2,1,0:T(8,128)(2,1)}, f32[528,768]{1,0:T(8,128)}) custom-call(s32[1]{0:T(128)} %bitcast.11.tile_ref, f32[2,8,4096]{2,1,0:T(8,128)} %copy-done, s32[1,8192]{1,0:T(1,128)} %bitcast.18, f32[1,3168,4096]{2,1,0:T(8,128)} %get-tuple-element.23.zp_ref, ...), custom_call_target="tpu_custom_call", output_to_operand_aliasing={{0}: (7, {})} | custom-call | flops 6643777536 | bytes 38535168 | tf_op jit(solution)/shard_map/gdw/pallas_call | solution.py:263
  181.9 19.1 %gdw.8 = (bf16[2,3168,4096]{2,1,0:T(8,128)(2,1)}, f32[528,768]{1,0:T(8,128)}) custom-call(s32[1]{0:T(128)} %bitcast.10.tile_ref, f32[2,8,4096]{2,1,0:T(8,128)} %copy-done, s32[1,8192]{1,0:T(1,128)} %bitcast.19, f32[1,3168,4096]{2,1,0:T(8,128)} %get-tuple-element.23.zp_ref, ...), custom_call_target="tpu_custom_call", output_to_operand_aliasing={{0}: (7, {})} | custom-call | flops 6643777536 | bytes 38535168 | tf_op jit(solution)/shard_map/gdw/pallas_call | solution.py:263
  200.9 19.5 %gdw.9 = (bf16[2,3168,4096]{2,1,0:T(8,128)(2,1)}, f32[528,768]{1,0:T(8,128)}) custom-call(s32[1]{0:T(128)} %bitcast.9.tile_ref, f32[2,8,4096]{2,1,0:T(8,128)} %copy-done, s32[1,8192]{1,0:T(1,128)} %bitcast.20, f32[1,3168,4096]{2,1,0:T(8,128)} %get-tuple-element.23.zp_ref, ...), custom_call_target="tpu_custom_call", output_to_operand_aliasing={{0}: (7, {})} | custom-call | flops 6643777536 | bytes 38535168 | tf_op jit(solution)/shard_map/gdw/pallas_call | solution.py:263
  220.5 19.0 %gdw.10 = (bf16[2,3168,4096]{2,1,0:T(8,128)(2,1)}, f32[528,768]{1,0:T(8,128)}) custom-call(s32[1]{0:T(128)} %bitcast.8.tile_ref, f32[2,8,4096]{2,1,0:T(8,128)} %copy-done, s32[1,8192]{1,0:T(1,128)} %bitcast.21, f32[1,3168,4096]{2,1,0:T(8,128)} %get-tuple-element.23.zp_ref, ...), custom_call_target="tpu_custom_call", output_to_operand_aliasing={{0}: (7, {})} | custom-call | flops 6643777536 | bytes 38535168 | tf_op jit(solution)/shard_map/gdw/pallas_call | solution.py:263
  239.5 19.2 %gdw.11 = (bf16[2,3168,4096]{2,1,0:T(8,128)(2,1)}, f32[528,768]{1,0:T(8,128)}) custom-call(s32[1]{0:T(128)} %bitcast.7.tile_ref, f32[2,8,4096]{2,1,0:T(8,128)} %copy-done, s32[1,8192]{1,0:T(1,128)} %bitcast.22, f32[1,3168,4096]{2,1,0:T(8,128)} %get-tuple-element.23.zp_ref, ...), custom_call_target="tpu_custom_call", output_to_operand_aliasing={{0}: (7, {})} | custom-call | flops 6643777536 | bytes 38535168 | tf_op jit(solution)/shard_map/gdw/pallas_call | solution.py:263
  258.7 27.5 %dx.3 = f32[4096,768]{1,0:T(8,128)} custom-call(bf16[2,3168,4096]{2,1,0:T(8,128)(2,1)} %get-tuple-element.30.g_ref, bf16[3168,768]{1,0:T(8,128)(2,1)} %constant_dynamic-slice_fusion.w_ref), custom_call_target="tpu_custom_call" | custom-call | flops 19931332608 | bytes 38535168 | tf_op jit(solution)/shard_map/dx/pallas_call | solution.py:281
  286.4 27.5 %dx.2 = f32[4096,768]{1,0:T(8,128)} custom-call(bf16[2,3168,4096]{2,1,0:T(8,128)(2,1)} %get-tuple-element.30.g_ref, bf16[3168,768]{1,0:T(8,128)(2,1)} %constant_dynamic-slice_fusion.w_ref), custom_call_target="tpu_custom_call" | custom-call | flops 19931332608 | bytes 38535168 | tf_op jit(solution)/shard_map/dx/pallas_call | solution.py:281
  314.6 24.4 %gather_fusion = bf16[4096,768]{1,0:T(8,128)(2,1)} fusion(bf16[6288,768]{1,0:T(8,128)(2,1)} %param.13, s32[4096]{0:T(1024)S(1)} %fusion), kind=kCustom, calls=%fused_computation | custom fusion | bytes 12599296 | tf_op jit(solution)/shard_map/jit(_take)/gather | solution.py:343
  339.1 8.0 %select_select_fusion = bf16[4096,768]{1,0:T(8,128)(2,1)} fusion(bf16[4096,768]{1,0:T(8,128)(2,1)} %gather_fusion, pred[4096]{0:T(1024)(128)(4,1)S(1)} %get-tuple-element.40, pred[4096]{0:T(1024)(128)(4,1)S(1)} %get-tuple-element.39), kind=kLoop, calls=%fused_computation.1 | loop fusion | flops 6291456 | bytes 12591104 | tf_op jit(solution)/shard_map/jit(_where)/select_n | solution.py:344
  348.9 15.6 %mlp.3.rest_0_ = bf16[4096,768]{1,0:T(8,128)(2,1)} custom-call(bf16[4096,768]{1,0:T(8,128)(2,1)} %a_ref.5, bf16[768,3072]{1,0:T(8,128)(2,1)} %bitcast.23, bf16[3072,768]{1,0:T(8,128)(2,1)} %bitcast.26), custom_call_target="tpu_custom_call" | custom-call | flops 9663676416 | bytes 12582912 | tf_op jit(solution)/shard_map/mlp/pallas_call | solution.py:41
  367.2 21.1 %mlp.4.rest_0_ = bf16[4096,768]{1,0:T(8,128)(2,1)} custom-call(bf16[4096,768]{1,0:T(8,128)(2,1)} %a_ref.5, bf16[768,3072]{1,0:T(8,128)(2,1)} %bitcast.24, bf16[3072,768]{1,0:T(8,128)(2,1)} %bitcast.27, bf16[4096,768]{1,0:T(8,128)(2,1)} %mlp.3.rest_0_), custom_call_target="tpu_custom_call", output_to_operand_aliasing={{}: (3, {})} | custom-call | flops 14495514624 | bytes 14155776 | tf_op jit(solution)/shard_map/mlp/pallas_call | solution.py:41
  394.2 76.3 %collective-permute-start.2 = (f32[1,1]{1,0:T(1,128)}, f32[1,1]{1,0:T(1,128)}, u32[]{:S(2)}, u32[]{:S(2)}) collective-permute-start(f32[1,1]{1,0:T(1,128)} %bitcast.4), channel_id=1, source_target_pairs={{0,24},{8,16},{16,8},{24,0},{1,25},{9,17},{17,9},{25,1},{2,26},{10... | collective-permute-start | bytes 20 | tf_op jit(solution)/shard_map/ppermute | solution.py:319
  470.9 2.1 multiply_convert_fusion.1
  475.3 2.1 multiply_convert_fusion
  479.1 20.8 %mlp.5 = bf16[4096,768]{1,0:T(8,128)(2,1)} custom-call(bf16[4096,768]{1,0:T(8,128)(2,1)} %a_ref.5, bf16[768,3072]{1,0:T(8,128)(2,1)} %bitcast.25, bf16[3072,768]{1,0:T(8,128)(2,1)} %bitcast.28, bf16[4096,768]{1,0:T(8,128)(2,1)} %mlp.4.rest_0_), custom_call_target="tpu_custom_call", output_to_operand_aliasing={{}: (3, {})} | custom-call | flops 14495514624 | bytes 14155776 | tf_op jit(solution)/shard_map/mlp/pallas_call | solution.py:41
  502.1 4.4 broadcast_in_dim.37
  511.8 11.9 %collective-permute-done.7 = bf16[528,768]{1,0:T(8,128)(2,1)} collective-permute-done((bf16[528,768]{1,0:T(8,128)(2,1)S(1)}, bf16[528,768]{1,0:T(8,128)(2,1)}, u32[]{:S(2)}, u32[]{:S(2)}) %collective-permute-start.7) | collective-permute-done | bytes 811040 | tf_op jit(solution)/shard_map/ppermute | solution.py:316
  527.2 2.1 constant_dynamic-update-slice_fusion.6
  531.4 9.7 %collective-permute-done.11 = bf16[528,768]{1,0:T(8,128)(2,1)} collective-permute-done((bf16[528,768]{1,0:T(8,128)(2,1)}, bf16[528,768]{1,0:T(8,128)(2,1)}, u32[]{:S(2)}, u32[]{:S(2)}) %collective-permute-start.11) | collective-permute-done | bytes 811040 | tf_op jit(solution)/shard_map/ppermute | solution.py:316
  541.1 2.1 constant_dynamic-update-slice_fusion.4
  544.1 48.0 %collective-permute-done.13 = bf16[528,768]{1,0:T(8,128)(2,1)S(1)} collective-permute-done((bf16[528,768]{1,0:T(8,128)(2,1)S(1)}, bf16[528,768]{1,0:T(8,128)(2,1)S(1)}, u32[]{:S(2)}, u32[]{:S(2)}) %collective-permute-start.13) | collective-permute-done | bytes 811040 | tf_op jit(solution)/shard_map/ppermute | solution.py:316
  595.1 14.4 %collective-permute-done.15 = bf16[528,768]{1,0:T(8,128)(2,1)S(1)} collective-permute-done((bf16[528,768]{1,0:T(8,128)(2,1)}, bf16[528,768]{1,0:T(8,128)(2,1)S(1)}, u32[]{:S(2)}, u32[]{:S(2)}) %collective-permute-start.15) | collective-permute-done | bytes 811040 | tf_op jit(solution)/shard_map/ppermute | solution.py:316
  610.4 3.2 add.141
  (76 shorter events, 38.1 us)
Async XLA Ops:
  7.2 28.6 %copy-start.8 = (s32[4096]{0:T(1024)S(1)}, s32[4096]{0:T(1024)}, u32[]{:S(2)}) copy-start(s32[4096]{0:T(1024)} %param.11) | copy-start | bytes 49156
  7.2 45.1 %all-gather.5.cloned.1.call-start = ((), (), s32[]{:S(2)}) async-start(), calls=%async_computation.4 | async-start | bytes 7077888 | tf_op jit(solution)/shard_map/all_gather | solution.py:324
  8.0 84.8 %all-gather.3.cloned.1.call-start = ((), (), s32[]{:S(2)}) async-start(), calls=%async_computation.3 | async-start | bytes 7077888 | tf_op jit(solution)/shard_map/all_gather | solution.py:325
  8.1 19.9 %collective-permute-start.1 = (bf16[512,768]{1,0:T(8,128)(2,1)}, bf16[512,768]{1,0:T(8,128)(2,1)S(1)}, u32[]{:S(2)}, u32[]{:S(2)}) collective-permute-start(bf16[512,768]{1,0:T(8,128)(2,1)} %param.9), channel_id=1, source_target_pairs={{0,8},{8,0},{16,24},{24,16},{1,9},{9,1},{17,25},{25,17},{2,10},{10... | collective-permute-start | bytes 2359304 | tf_op jit(solution)/shard_map/ppermute | solution.py:316
  28.0 0.9 copy-start.6
  28.9 473.1 %reduce-scatter.6.cloned.1.call-start = ((), (), s32[]{:S(2)}) async-start(), calls=%async_computation.6 | async-start | bytes 14155776 | tf_op jit(solution)/shard_map/reduce_scatter | solution.py:369
  29.0 6.8 %collective-permute-start = (s32[4096]{0:T(1024)}, s32[4096]{0:T(1024)S(1)}, u32[]{:S(2)}, u32[]{:S(2)}) collective-permute-start(s32[4096]{0:T(1024)} %param.11), channel_id=1, source_target_pairs={{0,8},{8,0},{16,24},{24,16},{1,9},{9,1},{17,25},{25,17},{2,10},{10... | collective-permute-start | bytes 49160 | tf_op jit(solution)/shard_map/ppermute | solution.py:316
  35.8 50.1 %copy-start.4 = (s32[8192]{0:T(1024)}, s32[8192]{0:T(1024)S(1)}, u32[]{:S(2)}) copy-start(s32[8192]{0:T(1024)S(1)} %pad_add_fusion) | copy-start | bytes 98308
  92.8 33.7 %copy-start.1 = (s32[4096]{0:T(1024)S(1)}, s32[4096]{0:T(1024)}, u32[]{:S(2)}) copy-start(s32[4096]{0:T(1024)} %param.12) | copy-start | bytes 49156
  92.8 33.7 %copy-start.2 = (f32[8,4096]{1,0:T(8,128)S(1)}, f32[8,4096]{1,0:T(8,128)}, u32[]{:S(2)}) copy-start(f32[8,4096]{1,0:T(8,128)} %get-tuple-element.22.so_ref) | copy-start | bytes 393220
  126.5 0.9 copy-start.3
  142.3 0.7 copy-start
  286.3 324.1 %reduce-scatter.4.cloned.1.call-start = ((), (), s32[]{:S(2)}) async-start(), calls=%async_computation.5 | async-start | bytes 14155776 | tf_op jit(solution)/shard_map/reduce_scatter | solution.py:371
  313.9 0.7 copy-start.7
  314.0 299.7 %reduce-scatter.8.cloned.1.call-start = ((), (), s32[]{:S(2)}) async-start(), calls=%async_computation.7 | async-start | bytes 7077888 | tf_op jit(solution)/shard_map/reduce_scatter | solution.py:345
  347.2 41.2 %collective-permute-start.4 = (f32[528,768]{1,0:T(8,128)}, f32[528,768]{1,0:T(8,128)}, u32[]{:S(2)}, u32[]{:S(2)}) collective-permute-start(f32[528,768]{1,0:T(8,128)} %get-tuple-element.32), channel_id=1, source_target_pairs={{0,24},{8,16},{16,8},{24,0},{1,25},{9,17},{17,9},{25,1},{2,26},{10... | collective-permute-start | bytes 4866056 | tf_op jit(solution)/shard_map/ppermute | solution.py:319
  364.6 109.6 %collective-permute-start.12 = (f32[528,768]{1,0:T(8,128)}, f32[528,768]{1,0:T(8,128)}, u32[]{:S(2)}, u32[]{:S(2)}) collective-permute-start(f32[528,768]{1,0:T(8,128)} %get-tuple-element.36), channel_id=1, source_target_pairs={{0,24},{8,16},{16,8},{24,0},{1,25},{9,17},{17,9},{25,1},{2,26},{10... | collective-permute-start | bytes 4866056 | tf_op jit(solution)/shard_map/ppermute | solution.py:319
  365.7 22.7 %copy-start.5 = (f32[528,768]{1,0:T(8,128)S(1)}, f32[528,768]{1,0:T(8,128)}, u32[]{:S(2)}) copy-start(f32[528,768]{1,0:T(8,128)} %get-tuple-element.31) | copy-start | bytes 4866052
  365.7 105.2 %collective-permute-start.8 = (f32[528,768]{1,0:T(8,128)}, f32[528,768]{1,0:T(8,128)}, u32[]{:S(2)}, u32[]{:S(2)}) collective-permute-start(f32[528,768]{1,0:T(8,128)} %get-tuple-element.34), channel_id=1, source_target_pairs={{0,24},{8,16},{16,8},{24,0},{1,25},{9,17},{17,9},{25,1},{2,26},{10... | collective-permute-start | bytes 4866056 | tf_op jit(solution)/shard_map/ppermute | solution.py:319
  390.2 88.9 %collective-permute-start.6 = (bf16[528,768]{1,0:T(8,128)(2,1)S(1)}, bf16[528,768]{1,0:T(8,128)(2,1)S(1)}, u32[]{:S(2)}, u32[]{:S(2)}) collective-permute-start(bf16[528,768]{1,0:T(8,128)(2,1)S(1)} %multiply_convert_fusion.2), channel_id=1, source_target_pairs={{0,24},{8,16},{16,8},{24,0},{1,25},{9,17},{17,9},{25,1},{2,26},{10... | collective-permute-start | bytes 2433032 | tf_op jit(solution)/shard_map/ppermute | solution.py:319
  394.2 83.2 %collective-permute-start.2 = (f32[1,1]{1,0:T(1,128)}, f32[1,1]{1,0:T(1,128)}, u32[]{:S(2)}, u32[]{:S(2)}) collective-permute-start(f32[1,1]{1,0:T(1,128)} %bitcast.4), channel_id=1, source_target_pairs={{0,24},{8,16},{16,8},{24,0},{1,25},{9,17},{17,9},{25,1},{2,26},{10... | collective-permute-start | bytes 20 | tf_op jit(solution)/shard_map/ppermute | solution.py:319
  470.5 31.5 %collective-permute-start.5 = (bf16[528,768]{1,0:T(8,128)(2,1)S(1)}, bf16[528,768]{1,0:T(8,128)(2,1)}, u32[]{:S(2)}, u32[]{:S(2)}) collective-permute-start(bf16[528,768]{1,0:T(8,128)(2,1)S(1)} %multiply_convert_fusion.2), channel_id=1, source_target_pairs={{0,8},{8,0},{16,24},{24,16},{1,9},{9,1},{17,25},{25,17},{2,10},{10... | collective-permute-start | bytes 2433032 | tf_op jit(solution)/shard_map/ppermute | solution.py:316
  473.0 54.2 %collective-permute-start.9 = (bf16[528,768]{1,0:T(8,128)(2,1)S(1)}, bf16[528,768]{1,0:T(8,128)(2,1)}, u32[]{:S(2)}, u32[]{:S(2)}) collective-permute-start(bf16[528,768]{1,0:T(8,128)(2,1)S(1)} %multiply_convert_fusion.1), channel_id=1, source_target_pairs={{0,8},{8,0},{16,24},{24,16},{1,9},{9,1},{17,25},{25,17},{2,10},{10... | collective-permute-start | bytes 2433032 | tf_op jit(solution)/shard_map/ppermute | solution.py:316
  474.2 26.2 %collective-permute-start.10 = (bf16[528,768]{1,0:T(8,128)(2,1)S(1)}, bf16[528,768]{1,0:T(8,128)(2,1)}, u32[]{:S(2)}, u32[]{:S(2)}) collective-permute-start(bf16[528,768]{1,0:T(8,128)(2,1)S(1)} %multiply_convert_fusion.1), channel_id=1, source_target_pairs={{0,24},{8,16},{16,8},{24,0},{1,25},{9,17},{17,9},{25,1},{2,26},{10... | collective-permute-start | bytes 2433032 | tf_op jit(solution)/shard_map/ppermute | solution.py:319
  477.4 33.3 %collective-permute-start.14 = (bf16[528,768]{1,0:T(8,128)(2,1)S(1)}, bf16[528,768]{1,0:T(8,128)(2,1)}, u32[]{:S(2)}, u32[]{:S(2)}) collective-permute-start(bf16[528,768]{1,0:T(8,128)(2,1)S(1)} %multiply_convert_fusion), channel_id=1, source_target_pairs={{0,24},{8,16},{16,8},{24,0},{1,25},{9,17},{17,9},{25,1},{2,26},{10... | collective-permute-start | bytes 2433032 | tf_op jit(solution)/shard_map/ppermute | solution.py:319
  479.1 44.6 %collective-permute-start.7 = (bf16[528,768]{1,0:T(8,128)(2,1)S(1)}, bf16[528,768]{1,0:T(8,128)(2,1)}, u32[]{:S(2)}, u32[]{:S(2)}) collective-permute-start(bf16[528,768]{1,0:T(8,128)(2,1)S(1)} %collective-permute-done.6), channel_id=1, source_target_pairs={{0,8},{8,0},{16,24},{24,16},{1,9},{9,1},{17,25},{25,17},{2,10},{10... | collective-permute-start | bytes 2433032 | tf_op jit(solution)/shard_map/ppermute | solution.py:316
  500.4 40.7 %collective-permute-start.11 = (bf16[528,768]{1,0:T(8,128)(2,1)}, bf16[528,768]{1,0:T(8,128)(2,1)}, u32[]{:S(2)}, u32[]{:S(2)}) collective-permute-start(bf16[528,768]{1,0:T(8,128)(2,1)} %collective-permute-done.10), channel_id=1, source_target_pairs={{0,8},{8,0},{16,24},{24,16},{1,9},{9,1},{17,25},{25,17},{2,10},{10... | collective-permute-start | bytes 2433032 | tf_op jit(solution)/shard_map/ppermute | solution.py:316
  502.0 108.4 %collective-permute-start.3 = (f32[512,768]{1,0:T(8,128)}, f32[512,768]{1,0:T(8,128)}, u32[]{:S(2)}, u32[]{:S(2)}) collective-permute-start(f32[512,768]{1,0:T(8,128)} %reduce-scatter.6.cloned.1.call-done), channel_id=1, source_target_pairs={{0,8},{8,0},{16,24},{24,16},{1,9},{9,1},{17,25},{25,17},{2,10},{10... | collective-permute-start | bytes 4718600 | tf_op jit(solution)/shard_map/ppermute | solution.py:316
  510.7 81.4 %collective-permute-start.13 = (bf16[528,768]{1,0:T(8,128)(2,1)S(1)}, bf16[528,768]{1,0:T(8,128)(2,1)S(1)}, u32[]{:S(2)}, u32[]{:S(2)}) collective-permute-start(bf16[528,768]{1,0:T(8,128)(2,1)S(1)} %multiply_convert_fusion), channel_id=1, source_target_pairs={{0,8},{8,0},{16,24},{24,16},{1,9},{9,1},{17,25},{25,17},{2,10},{10... | collective-permute-start | bytes 2433032 | tf_op jit(solution)/shard_map/ppermute | solution.py:316
  523.7 85.7 %collective-permute-start.15 = (bf16[528,768]{1,0:T(8,128)(2,1)}, bf16[528,768]{1,0:T(8,128)(2,1)S(1)}, u32[]{:S(2)}, u32[]{:S(2)}) collective-permute-start(bf16[528,768]{1,0:T(8,128)(2,1)} %collective-permute-done.14), channel_id=1, source_target_pairs={{0,8},{8,0},{16,24},{24,16},{1,9},{9,1},{17,25},{25,17},{2,10},{10... | collective-permute-start | bytes 2433032 | tf_op jit(solution)/shard_map/ppermute | solution.py:316
Sparse Core Ops, SparseCore 0:
  9.6 42.6 all-gather.4
  54.4 38.3 all-gather.2
  286.4 68.6 reduce-scatter.5
  357.3 69.7 reduce-scatter.3
  429.8 39.8 reduce-scatter.7

commit v2 on v1

v2 whole, which is shorter than its diff:
```python
import functools

import jax
import jax.numpy as jnp
from jax import lax
from jax.experimental import pallas as pl
from jax.experimental.pallas import tpu as pltpu
from jax.sharding import PartitionSpec as P

MESH = pl.DeviceIdType.MESH
F32 = jnp.float32
BF16 = jnp.bfloat16
N_TILE = 6


def VT_LOGITS(win):
    return next(v for v in range(352, 0, -16) if win % v == 0 and v <= 288)


LOW = -1e30


def _params(mib=60, **kw):
    return pltpu.CompilerParams(vmem_limit_bytes=mib * 2**20, **kw)


def _cost(flops, nbytes, trans=0):
    return pl.CostEstimate(flops=int(flops), bytes_accessed=int(nbytes), transcendentals=int(trans))


def _mlp_body(a_ref, w1_ref, w2_ref, *rest, chunk):
    o_ref, u_ref = rest[-2:]
    ff = w1_ref.shape[1]
    for c in range(ff // chunk):
        cs = slice(c * chunk, (c + 1) * chunk)
        h = jnp.dot(a_ref[...], w1_ref[:, cs], preferred_element_type=F32)
        u_ref[:, cs] = jax.nn.gelu(h).astype(BF16)
    y = jnp.dot(u_ref[...], w2_ref[...], preferred_element_type=F32)
    o_ref[...] = (a_ref[...].astype(F32) + y).astype(BF16)


def mlp(a, w1, w2, out, first, count, tb=512):
    n, d = a.shape
    ff = w1.shape[1]
    extra = [] if out is None else [out]
    return pl.pallas_call(
        functools.partial(_mlp_body, chunk=512),
        grid=(count,),
        in_specs=[
            pl.BlockSpec((tb, d), lambda i: (first + i, 0)),
            pl.BlockSpec((d, ff), lambda i: (0, 0)),
            pl.BlockSpec((ff, d), lambda i: (0, 0)),
        ] + [pl.BlockSpec(memory_space=pl.ANY)] * len(extra),
        out_specs=pl.BlockSpec((tb, d), lambda i: (first + i, 0)),
        out_shape=jax.ShapeDtypeStruct((n, d), BF16),
        scratch_shapes=[pltpu.VMEM((tb, ff), BF16)],
        input_output_aliases={3: 0} if extra else {},
        compiler_params=_params(),
        cost_estimate=_cost(4 * count * tb * d * ff, 4 * count * tb * d + 4 * d * ff, count * tb * ff),
        name="mlp",
    )(a, w1, w2, *extra)


def _logits_block(z_ref, x, w_ref, lab, lo, vt):
    tb = x.shape[0]
    lab8 = jnp.broadcast_to(lab, (8, tb))
    sub = lax.broadcasted_iota(jnp.int32, (vt // 8, 8, tb), 0) * 8 + lax.broadcasted_iota(jnp.int32, (vt // 8, 8, tb), 1)
    m8 = s8 = t8 = None
    for v in range(w_ref.shape[0] // vt):
        vs = slice(v * vt, (v + 1) * vt)
        z = lax.dot_general(w_ref[vs, :], x, (((1,), (1,)), ((), ())), preferred_element_type=F32)
        if v == 0:
            z = jnp.where(lax.broadcasted_iota(jnp.int32, (vt, tb), 0) >= lo, z, LOW)
        z_ref[vs, :] = z
        zr = z_ref[vs, :].reshape(vt // 8, 8, tb)
        tile_max = jnp.max(zr, axis=0)
        m_new = tile_max if v == 0 else jnp.maximum(m8, tile_max)
        e_sum = jnp.sum(jnp.exp(zr - m_new[None]), axis=0)
        hit = jnp.sum(jnp.where(sub == (lab8 - v * vt)[None], zr, 0.0), axis=0)
        s8 = e_sum if v == 0 else s8 * jnp.exp(m8 - m_new) + e_sum
        t8 = hit if v == 0 else t8 + hit
        m8 = m_new
    m = jnp.max(m8, axis=0, keepdims=True)
    s = jnp.sum(s8 * jnp.exp(m8 - m), axis=0, keepdims=True)
    t = jnp.sum(t8, axis=0, keepdims=True)
    return jnp.concatenate([m, s, t, jnp.zeros((5, tb), F32)], axis=0)


def _head_body(
    x_ref, wh_ref, lab_ref, mask_ref, z_ref, xo_ref, wo_ref, coef_out,
    xbuf, wbuf, zbuf, st, got, mine, coef,
    own_sem, w_sem, wo_sem, z_sem, xo_sem, xs_sem, xr_sem, send1, recv1, send2, recv2, *, n_stage, first_row, over, vt,
):
    y, s = lax.axis_index("data"), lax.axis_index("stage")
    h = lax.rem(y + y // 2, 2)
    n_x = n_stage // 2
    x, c = s // 2, lax.rem(s, 2)
    rows = xbuf.shape[2]
    win = wbuf.shape[0]
    n_blk = 2 * n_stage
    y_a = y + 1 - 2 * lax.rem(y, 2)
    sib = s + 1 - 2 * c

    def at(off, flip=0):
        return 2 * lax.rem(x + off, n_x) + lax.rem(c + flip, 2)

    left, right, far = at(n_x - 1), at(1), at(2)
    here = {"data": y, "stage": s}
    to_a = {"data": y_a, "stage": s}
    to_sib = {"data": y, "stage": sib}
    to_left = {"data": y, "stage": left}
    to_right = {"data": y, "stage": right}

    def slot(f, stage):
        return f * n_stage + stage

    sends = [
        (slot(0, s), slot(0, s), to_right, None),
        (slot(0, s), slot(0, s), to_left, None),
        (slot(0, s), slot(1, s), to_a, None),
        (slot(0, s), slot(0, s), to_sib, None),
        (slot(0, left), slot(0, left), to_right, 0),
        (slot(0, right), slot(0, right), to_left, 1),
        (slot(1, s), slot(1, s), to_right, None),
        (slot(1, s), slot(1, s), to_left, None),
        (slot(1, s), slot(1, s), to_sib, None),
        (slot(0, left), slot(0, left), to_sib, None),
        (slot(0, right), slot(0, right), to_sib, None),
        (slot(0, far), slot(1, far), to_a, None),
        (slot(0, far), slot(0, far), to_sib, None),
        (slot(1, left), slot(1, left), to_sib, None),
        (slot(1, right), slot(1, right), to_sib, None),
        (slot(1, far), slot(1, far), to_sib, None),
    ]

    def copy(k):
        src, dst, to, part = sends[k]
        return pltpu.make_async_remote_copy(
            src_ref=xbuf.at[src] if part is None else xbuf.at[src, part],
            dst_ref=xbuf.at[dst] if part is None else xbuf.at[dst, part],
            send_sem=xs_sem.at[k],
            recv_sem=xr_sem.at[n_blk if part == 1 else dst],
            device_id=to,
            device_id_type=MESH,
        )

    def arrival(ref, sem):
        return pltpu.make_async_remote_copy(
            src_ref=ref, dst_ref=ref, send_sem=xs_sem.at[0], recv_sem=sem, device_id=here, device_id_type=MESH
        )

    def got_block(f, stage):
        arrival(xbuf.at[slot(f, stage)], xr_sem.at[slot(f, stage)]).wait_recv()

    def got_half(part):
        i = slot(0, far)
        arrival(xbuf.at[i, part], xr_sem.at[n_blk if part == 1 else i]).wait_recv()

    own = pltpu.make_async_copy(x_ref, xbuf.at[slot(0, s)], own_sem)
    own.start()
    w_load = pltpu.make_async_copy(wh_ref.at[pl.ds(pl.multiple_of(h * first_row, 16), win), :], wbuf, w_sem)
    w_load.start()

    peers = [(f, k) for f in range(2) for k in range(n_stage) if (f, k) != (0, 0)]

    def peer(f, k):
        return {"data": y if f == 0 else y_a, "stage": lax.rem(s + k, n_stage)}

    barrier = pltpu.get_barrier_semaphore()
    for f, k in peers:
        pl.semaphore_signal(barrier, inc=1, device_id=peer(f, k), device_id_type=MESH)
    pl.semaphore_wait(barrier, len(peers))

    own.wait()
    for k in range(4):
        copy(k).start()
    w_load.wait()
    w_out = pltpu.make_async_copy(wbuf, wo_ref, wo_sem)
    w_out.start()

    def quarter(stage):
        return pl.ds(pl.multiple_of(stage * rows, rows), rows)

    def z_copy(zs, b, f, stage):
        return pltpu.make_async_copy(
            zbuf.at[zs, :, pl.ds(b * rows, rows)],
            z_ref.at[2 * (1 - f) + b, :, quarter(stage)],
            z_sem.at[zs, b],
        )

    def x_copy(f, stage):
        i = slot(f, stage)
        return pltpu.make_async_copy(xbuf.at[i], xo_ref.at[pl.ds(2 * (1 - f), 2), quarter(stage), :], xo_sem.at[i])

    def step(i, carry):
        @pl.when(i == 1)
        def _():
            got_block(0, sib)

        @pl.when(i == 2)
        def _():
            got_block(1, s)
            got_block(0, left)
            got_block(0, right)
            for k in range(4, 11):
                copy(k).start()

        @pl.when(i == 5)
        def _():
            got_half(0)
            got_half(1)
            copy(11).start()
            copy(12).start()
            got_block(1, sib)

        @pl.when(i == 6)
        def _():
            got_block(0, at(n_x - 1, 1))

        @pl.when(i == 7)
        def _():
            got_block(0, at(1, 1))

        @pl.when(i == 9)
        def _():
            got_block(0, at(2, 1))

        @pl.when(i == 10)
        def _():
            got_block(1, left)
            got_block(1, right)
            copy(13).start()
            copy(14).start()

        @pl.when(i == 12)
        def _():
            got_block(1, far)
            copy(15).start()
            got_block(1, at(n_x - 1, 1))

        @pl.when(i == 13)
        def _():
            got_block(1, at(1, 1))

        @pl.when(i == 15)
        def _():
            got_block(1, at(2, 1))

        def among(*ks):
            return functools.reduce(jnp.logical_or, [i == k for k in ks])

        f = jnp.where(jnp.logical_or(among(2, 5), i >= 10), 1, 0)
        flip = jnp.where(among(1, 5, 6, 7, 9, 12, 13, 15), 1, 0)
        off = jnp.where(among(3, 6, 10, 12), n_x - 1, jnp.where(among(4, 7, 11, 13), 1, jnp.where(among(8, 9, 14, 15), 2, 0)))
        stage = at(off, flip)
        blk = slot(f, stage)
        zs = lax.rem(i, 2)

        @pl.when(i >= 2)
        def _():
            for b in range(2):
                z_copy(zs, b, f, stage).wait()

        x_copy(f, stage).start()
        lab = lab_ref[f, :, pl.ds(pl.multiple_of(stage * 2 * rows, 2 * rows), 2 * rows)]
        res = _logits_block(zbuf.at[zs], xbuf[blk].reshape(2 * rows, -1), wbuf, lab, over * h, vt)
        for b in range(2):
            st[2 * (1 - f) + b, :, quarter(stage)] = res[:, b * rows:(b + 1) * rows]
            z_copy(zs, b, f, stage).start()
        return carry

    lax.fori_loop(0, n_blk, step, 0)

    first = []
    for f, k in peers:
        c1 = pltpu.make_async_remote_copy(
            src_ref=st.at[pl.ds(2 * (1 - f), 2), :, quarter(lax.rem(s + k, n_stage))],
            dst_ref=got.at[slot(f, k)],
            send_sem=send1.at[slot(f, k)],
            recv_sem=recv1.at[slot(f, k)],
            device_id=peer(f, k),
            device_id_type=MESH,
        )
        c1.start()
        first.append(c1)
    weight = mask_ref[...].astype(F32)
    denom = jnp.maximum(jnp.sum(weight), 1.0)
    mu = jnp.stack([mask_ref[:, pl.ds(pl.multiple_of((2 * s + b) * rows, rows), rows)].astype(F32) for b in range(2)])
    scale = mu / denom
    for c1 in first:
        c1.wait_recv()
    parts = [st[2:4, :, quarter(s)]] + [got[slot(f, k)] for f, k in peers]
    m = functools.reduce(jnp.maximum, [p[:, 0:1, :] for p in parts])
    z = sum(p[:, 1:2, :] * jnp.exp(p[:, 0:1, :] - m) for p in parts)
    t = sum(p[:, 2:3, :] for p in parts)
    loss = scale * (jnp.log(z) + m - t)
    res = jnp.concatenate([m, scale / z, scale, loss, jnp.zeros((2, 4, rows), F32)], axis=1)
    mine[...] = res
    second = []
    for f, k in peers:
        c2 = pltpu.make_async_remote_copy(
            src_ref=mine,
            dst_ref=coef.at[pl.ds(2 * (1 - f), 2), :, quarter(s)],
            send_sem=send2.at[slot(f, k)],
            recv_sem=recv2.at[slot(f, k)],
            device_id=peer(f, k),
            device_id_type=MESH,
        )
        c2.start()
        second.append(c2)
    coef[2:4, :, quarter(s)] = res
    for zs in range(2):
        for b in range(2):
            z_copy(zs, b, 0, s).wait()
    for i in range(n_blk):
        x_copy(i // n_stage, i % n_stage).wait()
    w_out.wait()
    for k in range(len(sends)):
        copy(k).wait_send()
    for c1 in first:
        c1.wait_send()
    for c2 in second:
        c2.wait_recv()
    coef_out[...] = coef[...]
    for c2 in second:
        c2.wait_send()


def head(x_rows, w_head, lab, mask, n_stage, win, vt):
    rows, d = x_rows.shape
    hr = rows // 2
    shard = w_head.shape[0]
    n = n_stage * hr
    n_blk = 2 * n_stage
    vm = pl.BlockSpec(memory_space=pltpu.VMEM)
    hbm = pl.BlockSpec(memory_space=pl.ANY)
    dma = pltpu.SemaphoreType.DMA
    x3 = x_rows.reshape(2, hr, d)
    total = n_blk * rows
    return pl.pallas_call(
        functools.partial(_head_body, n_stage=n_stage, first_row=shard - win, over=2 * win - shard, vt=vt),
        in_specs=[hbm, hbm, vm, vm],
        out_specs=[hbm, hbm, hbm, vm],
        out_shape=[
            jax.ShapeDtypeStruct((4, win, n), F32),
            jax.ShapeDtypeStruct((4, n, d), BF16),
            jax.ShapeDtypeStruct((win, d), BF16),
            jax.ShapeDtypeStruct((4, 8, n), F32),
        ],
        scratch_shapes=[
            pltpu.VMEM((n_blk, 2, hr, d), BF16),
            pltpu.VMEM((win, d), BF16),
            pltpu.VMEM((2, win, rows), F32),
            pltpu.VMEM((4, 8, n), F32),
            pltpu.VMEM((n_blk, 2, 8, hr), F32),
            pltpu.VMEM((2, 8, hr), F32),
            pltpu.VMEM((4, 8, n), F32),
            dma, dma, dma, dma((2, 2)), dma((n_blk,)), dma((16,)), dma((n_blk + 1,)),
            dma((n_blk,)), dma((n_blk,)), dma((n_blk,)), dma((n_blk,)),
        ],
        compiler_params=_params(56, collective_id=0, has_side_effects=True),
        cost_estimate=_cost(2 * total * d * win, 4 * total * win, total * win),
        name="head",
    )(x3, w_head, lab, mask)


def _gdw_body(tile_ref, coef_ref, lab_ref, z_ref, x_ref, *rest, ch, nv):
    g_ref, dw_refs, acc_ref = rest[-nv - 2], rest[-nv - 1:-1], rest[-1]
    t, v = pl.program_id(0), pl.program_id(1)
    vt, tb = z_ref.shape[1:]
    row0 = (tile_ref[0] + v) * vt
    sub = lax.broadcasted_iota(jnp.int32, (vt // 8, 8, ch), 0) * 8 + lax.broadcasted_iota(jnp.int32, (vt // 8, 8, ch), 1)
    acc = None
    for c in range(tb // ch):
        cs = slice(c * ch, (c + 1) * ch)
        m8 = jnp.broadcast_to(coef_ref[0, 0:1, cs], (8, ch))
        c8 = jnp.broadcast_to(coef_ref[0, 1:2, cs], (8, ch))
        r8 = jnp.broadcast_to(coef_ref[0, 2:3, cs], (8, ch))
        lab8 = jnp.broadcast_to(lab_ref[0, 0:1, cs], (8, ch)) - row0
        zr = z_ref[0, :, cs].reshape(vt // 8, 8, ch)
        e = jnp.exp(zr - m8[None]) * c8[None]
        g = jnp.where(sub == lab8[None], e - r8[None], e)
        gb = g.reshape(vt, ch).astype(BF16)
        g_ref[0, :, cs] = gb
        d = jnp.dot(gb, x_ref[0, cs, :], preferred_element_type=F32)
        acc = d if acc is None else acc + d
    if nv == 1:
        dw_refs[0][...] = jnp.where(t == 0, 0.0, dw_refs[0][...]) + acc
        return
    acc_ref[...] = acc
    for j in range(nv):
        @pl.when(v == j)
        def _(dw_ref=dw_refs[j]):
            dw_ref[...] = jnp.where(t == 0, 0.0, dw_ref[...]) + acc_ref[...]


def gdw(tile, nv, coef, lab, z, x, g, vt, ch=512):
    nq, n, d = x.shape
    win = z.shape[1]
    extra = [] if g is None else [g]
    ch = min(ch, n)
    spec = pltpu.PrefetchScalarGridSpec(
        num_scalar_prefetch=1,
        grid=(nq, nv),
        in_specs=[
            pl.BlockSpec((1, 8, n), lambda t, v, i: (t, 0, 0)),
            pl.BlockSpec((1, 1, n), lambda t, v, i: (t, 0, 0)),
            pl.BlockSpec((1, vt, n), lambda t, v, i: (t, i[0] + v, 0)),
            pl.BlockSpec((1, n, d), lambda t, v, i: (t, 0, 0)),
        ] + [pl.BlockSpec(memory_space=pl.ANY)] * len(extra),
        out_specs=[
            pl.BlockSpec((1, vt, n), lambda t, v, i: (t, i[0] + v, 0)),
        ] + [pl.BlockSpec((vt, d), lambda t, v, i: (0, 0))] * nv,
        scratch_shapes=[pltpu.VMEM((vt if nv > 1 else 8, d), F32)],
    )
    rows = nv * vt
    return pl.pallas_call(
        functools.partial(_gdw_body, ch=ch, nv=nv),
        grid_spec=spec,
        out_shape=[jax.ShapeDtypeStruct((nq, win, n), BF16)] + [jax.ShapeDtypeStruct((vt, d), F32)] * nv,
        input_output_aliases={5: 0} if extra else {},
        compiler_params=_params(62),
        cost_estimate=_cost(2 * nq * n * d * rows, 6 * nq * n * rows + 2 * nq * n * d, nq * n * rows),
        name="gdw",
    )(tile, coef, lab, z, x, *extra)


def _dx_body(g_ref, w_ref, o_ref):
    o_ref[...] = lax.dot_general(g_ref[0], w_ref[...], (((0,), (0,)), ((), ())), preferred_element_type=F32)


def dx(g, w, q, tb=512):
    n = g.shape[2]
    win, d = w.shape
    tb = min(tb, n)
    return pl.pallas_call(
        _dx_body,
        grid=(n // tb,),
        in_specs=[
            pl.BlockSpec((1, win, tb), lambda i: (q, 0, i)),
            pl.BlockSpec((win, d), lambda i: (0, 0)),
        ],
        out_specs=pl.BlockSpec((tb, d), lambda i: (i, 0)),
        out_shape=jax.ShapeDtypeStruct((n, d), F32),
        compiler_params=_params(),
        cost_estimate=_cost(2 * n * d * win, 2 * n * win + 4 * n * d),
        name="dx",
    )(g, w)


def solution(mesh):
    n_data, n_stage = mesh.shape["data"], mesh.shape["stage"]
    tok_spec = P(("pod", "data", "stage"), None)
    rep_spec = P(("pod", "data"))
    vocab_spec = P("stage", None)
    layer_spec = P("stage", None, None)
    swap_a = [(i, i ^ 1) for i in range(n_data)]
    swap_b = [(i, n_data - 1 - i) for i in range(n_data)]

    def local_step(x_rows, w_head, labels, loss_mask, w_embed, tok_ids, act_in, w_up, w_down):
        y, s = lax.axis_index("data"), lax.axis_index("stage")
        shard, d = w_head.shape
        yh = y >> 1
        h = (y ^ yh) & 1
        vt = -(-shard // (2 * N_TILE * 16)) * 16
        win = N_TILE * vt
        first_row = shard - win
        lo = (2 * win - shard) * h

        def over_a(v):
            return lax.ppermute(v, "data", swap_a)

        def over_b(v):
            return lax.ppermute(v, "data", swap_b)

        lab_a = over_a(labels)

        def local(lab):
            lab = lab - (s * shard + h * first_row)
            return jnp.where(lab < lo, -1, lab)

        n_tok = labels.shape[0]
        lab_two = jnp.stack([local(labels), local(lab_a)])
        z, x_all, w_win, coef = head(x_rows, w_head, lab_two.reshape(2, 1, n_tok), loss_mask.reshape(1, -1), n_stage, win, VT_LOGITS(win))
        half_rows = n_tok // n_stage // 2
        lab = lab_two[::-1].reshape(2, n_stage, 2, half_rows).transpose(0, 2, 1, 3).reshape(4, 1, n_tok // 2)

        loss_q = jnp.sum(coef[:, 3, :], axis=1)
        loss_pair = (loss_q[0] + loss_q[1]) + (loss_q[2] + loss_q[3])
        loss_far = over_b(loss_pair.reshape(1, 1))[0, 0]
        mean_loss = (loss_pair + loss_far) / n_data

        half = N_TILE // 2
        far_tile, own_tile = (1 - yh) * half, yh * half
        sent = []
        g, *sent_parts = gdw(far_tile.reshape(1), 1, coef, lab, z, x_all, None, vt)
        g, *more = gdw((far_tile + 1).reshape(1), half - 1, coef, lab, z, x_all, g, vt)
        for part in sent_parts + more:
            sent.append(over_b(part))
        g, *kept = gdw(own_tile.reshape(1), half, coef, lab, z, x_all, g, vt)

        rs = []
        for q in range(4):
            dx_q = dx(g, w_win, q)
            rs.append(lax.psum_scatter(dx_q, "stage", scatter_dimension=0, tiled=True))
        gx = []
        for q in range(2):
            gx.append(over_a(rs[q]))
        grad_x = jnp.concatenate([rs[2] + gx[0], rs[3] + gx[1]], axis=0)

        offset = s * shard
        local_ids = tok_ids - offset
        in_slice = (local_ids >= 0) & (local_ids < shard)
        rows_emb = jnp.take(w_embed, jnp.clip(local_ids, 0, shard - 1), axis=0)
        emb_part = jnp.where(in_slice[:, None], rows_emb, jnp.zeros_like(rows_emb))
        embed_out = lax.psum_scatter(emb_part, "stage", scatter_dimension=0, tiled=True)

        mlp_out = mlp(act_in, w_up[0], w_down[0], None, 0, act_in.shape[0] // 512)

        grad_head = jnp.zeros((shard, d), BF16)
        for j in range(half):
            fin = lax.optimization_barrier(((kept[j] + sent[j]) / n_data).astype(BF16))
            fin_b = over_b(fin)
            fin_a = over_a(fin)
            fin_ab = over_a(fin_b)
            for v, hh, part in ((fin, h, yh), (fin_a, 1 - h, yh), (fin_b, h, 1 - yh), (fin_ab, 1 - h, 1 - yh)):
                row = hh * first_row + (part * half + j) * vt
                grad_head = lax.dynamic_update_slice(grad_head, v, (row, 0))

        return mean_loss.reshape(1), grad_x, grad_head, embed_out, mlp_out

    return jax.shard_map(
        local_step,
        mesh=mesh,
        in_specs=(tok_spec, vocab_spec, rep_spec, rep_spec, vocab_spec, rep_spec, tok_spec, layer_spec, layer_spec),
        out_specs=(P("pod"), tok_spec, P(("pod", "stage"), None), tok_spec, tok_spec),
        check_vma=False,
    )
```

time: 632 us -> 567 us (0.90); the launches traced: 622 us -> 565 us
  waiting for transfers between devices: 126 us -> 90.2 us
  Pallas kernels: 310 us -> 290 us
    ppermute x9, waiting for transfers between devices: 101 us -> 56.9 us  [over_a(): return lax.ppermute(v, 'data', swap_a)]
    ppermute x7, waiting for transfers between devices: 1.11 us -> 33 us  [over_b(): return lax.ppermute(v, 'data', swap_b)]
    all_gather x2 -> x0, waiting for transfers between devices: 22.7 us -> none  [the longest x1 15.8 us: local_step(): x_o = lax.all_gather(x_rows, 'stage', axis=0, tiled=True)]
    pallas_call x9 -> x4, Pallas kernels: 197 us -> 178 us  [the longest x1 89.3 us: head(): pl.pallas_call(functools.partial(_head_body, n_stage=n_stage, first_row=s...]
    pallas_call x3 -> x1, Pallas kernels: 57.4 us -> 47.2 us  [mlp(): pl.pallas_call(functools.partial(_mlp_body, chunk=512), grid=(count,), in...]
    pallas_call x2 -> x4, Pallas kernels: 55.1 us -> 64.4 us  [dx(): pl.pallas_call(_dx_body, grid=(n // tb,), in_specs=[pl.BlockSpec((1, win,...]
  transfers between devices with their start and end apart: 21 -> 21, of which waited for: 8 -> 6; matrix products, arithmetic and copies ran while one was open for 12% -> 11% of each run, Pallas kernels for 19% -> 17%
where the time goes in v2:
time: 567 us; the launch traced here: 565 us
  Pallas kernels  290 us (51%)
  starting transfers between devices  98.9 us (17%)
  waiting for transfers between devices  90.2 us (16%)
  local copies, waits for them, and re-layouts  51.3 us (9%)
  between operations  18.3 us (3%)
  other arithmetic  16.1 us (3%)
    ppermute x7, starting transfers between devices, over_b(): return lax.ppermute(v, 'data', swap_b)  89.7 us
    pallas_call x1, Pallas kernels, head(): pl.pallas_call(functools.partial(_head_body, n_stage=n_stage, first_row=s...  89.3 us
    pallas_call x3, Pallas kernels, gdw(): pl.pallas_call(functools.partial(_gdw_body, ch=ch, nv=nv), grid_spec=spec...  89 us
    pallas_call x4, Pallas kernels, dx(): pl.pallas_call(_dx_body, grid=(n // tb,), in_specs=[pl.BlockSpec((1, win,...  64.4 us
    ppermute x9, waiting for transfers between devices, over_a(): return lax.ppermute(v, 'data', swap_a)  56.9 us
    pallas_call x1, Pallas kernels, mlp(): pl.pallas_call(functools.partial(_mlp_body, chunk=512), grid=(count,), in...  47.2 us
    ppermute x7, waiting for transfers between devices, over_b(): return lax.ppermute(v, 'data', swap_b)  33 us
    gather x1, local copies, waits for them, and re-layouts, local_step(): rows_emb = jnp.take(w_embed, jnp.clip(local_ids, 0, shard - 1), axis=0)  24.3 us
  transfers between devices with their start and end apart: 21, of which 6 were waited for; matrix products, arithmetic and copies ran while one was open for 11% of the time, Pallas kernels for 17%

profile of v2, /device:TPU:97, one launch (start us, length us, event | category | flops | bytes accessed | tf_op | source)
XLA Modules:
  0.0 564.7 jit_solution(1471266597248356911)
XLA Ops:
  7.2 2.8 collective-permute-start
  13.5 89.3 %head.1 = (f32[4,3168,2048]{2,1,0:T(8,128)}, bf16[4,2048,768]{2,1,0:T(8,128)(2,1)}, bf16[3168,768]{1,0:T(8,128)(2,1)}, f32[4,8,2048]{2,1,0:T(8,128)}) custom-call(bf16[2,256,768]{2,1,0:T(8,128)(2,1)} %bitcast.23, bf16[6288,768]{1,0:T(8,128)(2,1)} %wh_ref.1, s32[2,1,4096]{2,1,0:T(1,128)} %reshape.51.lab_ref, s32[1,4096]{1,0:T(1,128)} %bitcast.24), custom_call_target="tpu_custom_call" | custom-call | flops 39862665216 | bytes 103809024 | tf_op jit(solution)/shard_map/head/pallas_call | solution.py:340
  102.8 15.8 %gdw.3 = (bf16[4,3168,2048]{2,1,0:T(8,128)(2,1)}, f32[528,768]{1,0:T(8,128)}) custom-call(s32[1]{0:T(128)} %bitcast.11.tile_ref, f32[4,8,2048]{2,1,0:T(8,128)} %get-tuple-element.18.coef_ref, s32[4,1,2048]{2,1,0:T(1,128)} %reshape.57.lab_ref, f32[4,3168,2048]{2,1,0:T(8,128)} %get-tuple-element.19.z_ref, bf16[4,2048,768]{2,1,0:T(8,128)(2,1)} %get-tuple-element.20.x_ref), custom_call_target="tpu_custom_call" | custom-call | flops 6643777536 | bytes 38535168 | tf_op jit(solution)/shard_map/gdw/pallas_call | solution.py:417
  118.6 32.2 %gdw.4 = (bf16[4,3168,2048]{2,1,0:T(8,128)(2,1)}, f32[528,768]{1,0:T(8,128)}, f32[528,768]{1,0:T(8,128)}) custom-call(s32[1]{0:T(128)} %bitcast.10.tile_ref, f32[4,8,2048]{2,1,0:T(8,128)} %get-tuple-element.18.coef_ref, s32[4,1,2048]{2,1,0:T(1,128)} %reshape.57.lab_ref, f32[4,3168,2048]{2,1,0:T(8,128)} %get-tuple-element.19.z_ref, ...), custom_call_target="tpu_custom_call", output_to_operand_aliasing={{0}: (5, {})} | custom-call | flops 13287555072 | bytes 64487424 | tf_op jit(solution)/shard_map/gdw/pallas_call | solution.py:417
  150.8 41.1 %gdw.5 = (bf16[4,3168,2048]{2,1,0:T(8,128)(2,1)}, f32[528,768]{1,0:T(8,128)}, f32[528,768]{1,0:T(8,128)}, f32[528,768]{1,0:T(8,128)}) custom-call(s32[1]{0:T(128)} %bitcast.8.tile_ref, f32[4,8,2048]{2,1,0:T(8,128)} %get-tuple-element.18.coef_ref, s32[4,1,2048]{2,1,0:T(1,128)} %reshape.57.lab_ref, ...), custom_call_target="tpu_custom_call", output_to_operand_aliasing={{0}: (5, {})} | custom-call | flops 19931332608 | bytes 90439680 | tf_op jit(solution)/shard_map/gdw/pallas_call | solution.py:417
  191.9 16.0 %dx.5 = f32[2048,768]{1,0:T(8,128)} custom-call(bf16[4,3168,2048]{2,1,0:T(8,128)(2,1)} %get-tuple-element.23.g_ref, bf16[3168,768]{1,0:T(8,128)(2,1)} %get-tuple-element.24.w_ref), custom_call_target="tpu_custom_call" | custom-call | flops 9965666304 | bytes 19267584 | tf_op jit(solution)/shard_map/dx/pallas_call | solution.py:436
  208.0 16.1 %dx.7 = f32[2048,768]{1,0:T(8,128)} custom-call(bf16[4,3168,2048]{2,1,0:T(8,128)(2,1)} %get-tuple-element.23.g_ref, bf16[3168,768]{1,0:T(8,128)(2,1)} %get-tuple-element.24.w_ref), custom_call_target="tpu_custom_call" | custom-call | flops 9965666304 | bytes 19267584 | tf_op jit(solution)/shard_map/dx/pallas_call | solution.py:436
  224.2 16.2 %dx.4 = f32[2048,768]{1,0:T(8,128)} custom-call(bf16[4,3168,2048]{2,1,0:T(8,128)(2,1)} %get-tuple-element.23.g_ref, bf16[3168,768]{1,0:T(8,128)(2,1)} %get-tuple-element.24.w_ref), custom_call_target="tpu_custom_call" | custom-call | flops 9965666304 | bytes 19267584 | tf_op jit(solution)/shard_map/dx/pallas_call | solution.py:436
  240.5 16.2 %dx.6 = f32[2048,768]{1,0:T(8,128)} custom-call(bf16[4,3168,2048]{2,1,0:T(8,128)(2,1)} %get-tuple-element.23.g_ref, bf16[3168,768]{1,0:T(8,128)(2,1)} %get-tuple-element.24.w_ref), custom_call_target="tpu_custom_call" | custom-call | flops 9965666304 | bytes 19267584 | tf_op jit(solution)/shard_map/dx/pallas_call | solution.py:436
  257.4 24.3 %gather_fusion = bf16[4096,768]{1,0:T(8,128)(2,1)} fusion(bf16[6288,768]{1,0:T(8,128)(2,1)} %param.13, s32[4096]{0:T(1024)S(1)} %fusion), kind=kCustom, calls=%fused_computation | custom fusion | bytes 12599296 | tf_op jit(solution)/shard_map/jit(_take)/gather | solution.py:514
  281.7 8.0 %select_select_fusion = bf16[4096,768]{1,0:T(8,128)(2,1)} fusion(bf16[4096,768]{1,0:T(8,128)(2,1)} %gather_fusion, pred[4096]{0:T(1024)(128)(4,1)S(1)} %get-tuple-element.32, pred[4096]{0:T(1024)(128)(4,1)S(1)} %get-tuple-element.31), kind=kLoop, calls=%fused_computation.1 | loop fusion | flops 6291456 | bytes 12591104 | tf_op jit(solution)/shard_map/jit(_where)/select_n | solution.py:515
  289.9 2.9 collective-permute-start.4
  292.9 2.6 collective-permute-start.12
  295.5 33.0 %collective-permute-done.4 = f32[528,768]{1,0:T(8,128)S(1)} collective-permute-done((f32[528,768]{1,0:T(8,128)}, f32[528,768]{1,0:T(8,128)S(1)}, u32[]{:S(2)}, u32[]{:S(2)}) %collective-permute-start.4) | collective-permute-done | bytes 1622048 | tf_op jit(solution)/shard_map/ppermute | solution.py:474
  328.7 2.5 collective-permute-start.6
  335.5 78.8 %collective-permute-start.1 = (f32[1,1]{1,0:T(1,128)}, f32[1,1]{1,0:T(1,128)}, u32[]{:S(2)}, u32[]{:S(2)}) collective-permute-start(f32[1,1]{1,0:T(1,128)} %bitcast.5), channel_id=1, source_target_pairs={{0,24},{8,16},{16,8},{24,0},{1,25},{9,17},{17,9},{25,1},{2,26},{10... | collective-permute-start | bytes 20 | tf_op jit(solution)/shard_map/ppermute | solution.py:474
  415.0 1.8 multiply_convert_fusion.1
  418.1 2.6 collective-permute-start.14
  420.7 47.2 %mlp.1 = bf16[4096,768]{1,0:T(8,128)(2,1)} custom-call(bf16[4096,768]{1,0:T(8,128)(2,1)} %a_ref.1, bf16[768,3072]{1,0:T(8,128)(2,1)} %bitcast.21, bf16[3072,768]{1,0:T(8,128)(2,1)} %bitcast.22), custom_call_target="tpu_custom_call" | custom-call | flops 38654705664 | bytes 22020096 | tf_op jit(solution)/shard_map/mlp/pallas_call | solution.py:46
  468.5 1.5 collective-permute-start.11
  470.1 4.4 broadcast_in_dim.33
  476.9 2.1 constant_dynamic-update-slice_fusion.10
  479.0 2.1 constant_dynamic-update-slice_fusion.9
  481.1 2.1 constant_dynamic-update-slice_fusion.8
  484.1 2.1 constant_dynamic-update-slice_fusion.6
  487.7 2.1 constant_dynamic-update-slice_fusion.5
  489.8 2.1 constant_dynamic-update-slice_fusion.4
  492.8 10.8 %collective-permute-done.13 = bf16[528,768]{1,0:T(8,128)(2,1)} collective-permute-done((bf16[528,768]{1,0:T(8,128)(2,1)S(1)}, bf16[528,768]{1,0:T(8,128)(2,1)}, u32[]{:S(2)}, u32[]{:S(2)}) %collective-permute-start.13) | collective-permute-done | bytes 811040 | tf_op jit(solution)/shard_map/ppermute | solution.py:471
  503.6 2.1 constant_dynamic-update-slice_fusion.2
  506.6 14.3 %collective-permute-done.15 = bf16[528,768]{1,0:T(8,128)(2,1)S(1)} collective-permute-done((bf16[528,768]{1,0:T(8,128)(2,1)S(1)}, bf16[528,768]{1,0:T(8,128)(2,1)S(1)}, u32[]{:S(2)}, u32[]{:S(2)}) %collective-permute-start.15) | collective-permute-done | bytes 811040 | tf_op jit(solution)/shard_map/ppermute | solution.py:471
  521.8 16.0 %collective-permute-done.2 = f32[256,768]{1,0:T(8,128)} collective-permute-done((f32[256,768]{1,0:T(8,128)}, f32[256,768]{1,0:T(8,128)}, u32[]{:S(2)}, u32[]{:S(2)}) %collective-permute-start.2) | collective-permute-done | bytes 786464 | tf_op jit(solution)/shard_map/ppermute | solution.py:471
  539.3 15.3 %collective-permute-done.3 = f32[256,768]{1,0:T(8,128)S(1)} collective-permute-done((f32[256,768]{1,0:T(8,128)}, f32[256,768]{1,0:T(8,128)S(1)}, u32[]{:S(2)}, u32[]{:S(2)}) %collective-permute-start.3) | collective-permute-done | bytes 786464 | tf_op jit(solution)/shard_map/ppermute | solution.py:471
  (63 shorter events, 20.3 us)
Async XLA Ops:
  7.2 479.0 %reduce-scatter.8.cloned.1.call-start = ((), (), s32[]{:S(2)}) async-start(), calls=%async_computation.6 | async-start | bytes 7077888 | tf_op jit(solution)/shard_map/reduce_scatter | solution.py:505
  7.2 4.1 collective-permute-start
  207.9 278.4 %reduce-scatter.12.cloned.1.call-start = ((), (), s32[]{:S(2)}) async-start(), calls=%async_computation.8 | async-start | bytes 7077888 | tf_op jit(solution)/shard_map/reduce_scatter | solution.py:505
  224.1 297.7 %reduce-scatter.6.cloned.1.call-start = ((), (), s32[]{:S(2)}) async-start(), calls=%async_computation.5 | async-start | bytes 7077888 | tf_op jit(solution)/shard_map/reduce_scatter | solution.py:505
  240.4 298.9 %reduce-scatter.10.cloned.1.call-start = ((), (), s32[]{:S(2)}) async-start(), calls=%async_computation.7 | async-start | bytes 7077888 | tf_op jit(solution)/shard_map/reduce_scatter | solution.py:505
  256.7 0.7 copy-start.2
  256.8 300.3 %reduce-scatter.14.cloned.1.call-start = ((), (), s32[]{:S(2)}) async-start(), calls=%async_computation.9 | async-start | bytes 7077888 | tf_op jit(solution)/shard_map/reduce_scatter | solution.py:516
  289.8 38.7 %copy-start.1 = (f32[528,768]{1,0:T(8,128)S(1)}, f32[528,768]{1,0:T(8,128)}, u32[]{:S(2)}) copy-start(f32[528,768]{1,0:T(8,128)} %get-tuple-element.25) | copy-start | bytes 4866052
  289.8 128.1 %copy-start = (f32[528,768]{1,0:T(8,128)S(1)}, f32[528,768]{1,0:T(8,128)}, u32[]{:S(2)}) copy-start(f32[528,768]{1,0:T(8,128)} %get-tuple-element.29) | copy-start | bytes 4866052
  289.9 38.6 %collective-permute-start.4 = (f32[528,768]{1,0:T(8,128)}, f32[528,768]{1,0:T(8,128)S(1)}, u32[]{:S(2)}, u32[]{:S(2)}) collective-permute-start(f32[528,768]{1,0:T(8,128)} %get-tuple-element.26), channel_id=1, source_target_pairs={{0,24},{8,16},{16,8},{24,0},{1,25},{9,17},{17,9},{25,1},{2,26},{10... | collective-permute-start | bytes 4866056 | tf_op jit(solution)/shard_map/ppermute | solution.py:474
  292.8 122.2 %collective-permute-start.8 = (f32[528,768]{1,0:T(8,128)}, f32[528,768]{1,0:T(8,128)S(1)}, u32[]{:S(2)}, u32[]{:S(2)}) collective-permute-start(f32[528,768]{1,0:T(8,128)} %get-tuple-element.28), channel_id=1, source_target_pairs={{0,24},{8,16},{16,8},{24,0},{1,25},{9,17},{17,9},{25,1},{2,26},{10... | collective-permute-start | bytes 4866056 | tf_op jit(solution)/shard_map/ppermute | solution.py:474
  292.9 124.8 %collective-permute-start.12 = (f32[528,768]{1,0:T(8,128)}, f32[528,768]{1,0:T(8,128)S(1)}, u32[]{:S(2)}, u32[]{:S(2)}) collective-permute-start(f32[528,768]{1,0:T(8,128)} %get-tuple-element.30), channel_id=1, source_target_pairs={{0,24},{8,16},{16,8},{24,0},{1,25},{9,17},{17,9},{25,1},{2,26},{10... | collective-permute-start | bytes 4866056 | tf_op jit(solution)/shard_map/ppermute | solution.py:474
  328.7 92.0 %collective-permute-start.6 = (bf16[528,768]{1,0:T(8,128)(2,1)S(1)}, bf16[528,768]{1,0:T(8,128)(2,1)}, u32[]{:S(2)}, u32[]{:S(2)}) collective-permute-start(bf16[528,768]{1,0:T(8,128)(2,1)S(1)} %multiply_convert_fusion.2), channel_id=1, source_target_pairs={{0,24},{8,16},{16,8},{24,0},{1,25},{9,17},{17,9},{25,1},{2,26},{10... | collective-permute-start | bytes 2433032 | tf_op jit(solution)/shard_map/ppermute | solution.py:474
  335.5 82.7 %collective-permute-start.1 = (f32[1,1]{1,0:T(1,128)}, f32[1,1]{1,0:T(1,128)}, u32[]{:S(2)}, u32[]{:S(2)}) collective-permute-start(f32[1,1]{1,0:T(1,128)} %bitcast.5), channel_id=1, source_target_pairs={{0,24},{8,16},{16,8},{24,0},{1,25},{9,17},{17,9},{25,1},{2,26},{10... | collective-permute-start | bytes 20 | tf_op jit(solution)/shard_map/ppermute | solution.py:474
  414.3 61.2 %collective-permute-start.5 = (bf16[528,768]{1,0:T(8,128)(2,1)S(1)}, bf16[528,768]{1,0:T(8,128)(2,1)}, u32[]{:S(2)}, u32[]{:S(2)}) collective-permute-start(bf16[528,768]{1,0:T(8,128)(2,1)S(1)} %multiply_convert_fusion.2), channel_id=1, source_target_pairs={{0,8},{8,0},{16,24},{24,16},{1,9},{9,1},{17,25},{25,17},{2,10},{10... | collective-permute-start | bytes 2433032 | tf_op jit(solution)/shard_map/ppermute | solution.py:471
  416.7 67.4 %collective-permute-start.9 = (bf16[528,768]{1,0:T(8,128)(2,1)S(1)}, bf16[528,768]{1,0:T(8,128)(2,1)}, u32[]{:S(2)}, u32[]{:S(2)}) collective-permute-start(bf16[528,768]{1,0:T(8,128)(2,1)S(1)} %multiply_convert_fusion.1), channel_id=1, source_target_pairs={{0,8},{8,0},{16,24},{24,16},{1,9},{9,1},{17,25},{25,17},{2,10},{10... | collective-permute-start | bytes 2433032 | tf_op jit(solution)/shard_map/ppermute | solution.py:471
  417.7 50.8 %collective-permute-start.10 = (bf16[528,768]{1,0:T(8,128)(2,1)S(1)}, bf16[528,768]{1,0:T(8,128)(2,1)}, u32[]{:S(2)}, u32[]{:S(2)}) collective-permute-start(bf16[528,768]{1,0:T(8,128)(2,1)S(1)} %multiply_convert_fusion.1), channel_id=1, source_target_pairs={{0,24},{8,16},{16,8},{24,0},{1,25},{9,17},{17,9},{25,1},{2,26},{10... | collective-permute-start | bytes 2433032 | tf_op jit(solution)/shard_map/ppermute | solution.py:474
  418.1 57.4 %collective-permute-start.14 = (bf16[528,768]{1,0:T(8,128)(2,1)S(1)}, bf16[528,768]{1,0:T(8,128)(2,1)S(1)}, u32[]{:S(2)}, u32[]{:S(2)}) collective-permute-start(bf16[528,768]{1,0:T(8,128)(2,1)S(1)} %multiply_convert_fusion), channel_id=1, source_target_pairs={{0,24},{8,16},{16,8},{24,0},{1,25},{9,17},{17,9},{25,1},{2,26},{10... | collective-permute-start | bytes 2433032 | tf_op jit(solution)/shard_map/ppermute | solution.py:474
  420.7 60.4 %collective-permute-start.7 = (bf16[528,768]{1,0:T(8,128)(2,1)}, bf16[528,768]{1,0:T(8,128)(2,1)}, u32[]{:S(2)}, u32[]{:S(2)}) collective-permute-start(bf16[528,768]{1,0:T(8,128)(2,1)} %collective-permute-done.6), channel_id=1, source_target_pairs={{0,8},{8,0},{16,24},{24,16},{1,9},{9,1},{17,25},{25,17},{2,10},{10... | collective-permute-start | bytes 2433032 | tf_op jit(solution)/shard_map/ppermute | solution.py:471
  468.5 21.2 %collective-permute-start.11 = (bf16[528,768]{1,0:T(8,128)(2,1)}, bf16[528,768]{1,0:T(8,128)(2,1)}, u32[]{:S(2)}, u32[]{:S(2)}) collective-permute-start(bf16[528,768]{1,0:T(8,128)(2,1)} %collective-permute-done.10), channel_id=1, source_target_pairs={{0,8},{8,0},{16,24},{24,16},{1,9},{9,1},{17,25},{25,17},{2,10},{10... | collective-permute-start | bytes 2433032 | tf_op jit(solution)/shard_map/ppermute | solution.py:471
  475.5 28.1 %collective-permute-start.13 = (bf16[528,768]{1,0:T(8,128)(2,1)S(1)}, bf16[528,768]{1,0:T(8,128)(2,1)}, u32[]{:S(2)}, u32[]{:S(2)}) collective-permute-start(bf16[528,768]{1,0:T(8,128)(2,1)S(1)} %multiply_convert_fusion), channel_id=1, source_target_pairs={{0,8},{8,0},{16,24},{24,16},{1,9},{9,1},{17,25},{25,17},{2,10},{10... | collective-permute-start | bytes 2433032 | tf_op jit(solution)/shard_map/ppermute | solution.py:471
  475.5 45.3 %collective-permute-start.15 = (bf16[528,768]{1,0:T(8,128)(2,1)S(1)}, bf16[528,768]{1,0:T(8,128)(2,1)S(1)}, u32[]{:S(2)}, u32[]{:S(2)}) collective-permute-start(bf16[528,768]{1,0:T(8,128)(2,1)S(1)} %collective-permute-done.14), channel_id=1, source_target_pairs={{0,8},{8,0},{16,24},{24,16},{1,9},{9,1},{17,25},{25,17},{2,10},{10... | collective-permute-start | bytes 2433032 | tf_op jit(solution)/shard_map/ppermute | solution.py:471
  486.2 51.6 %collective-permute-start.2 = (f32[256,768]{1,0:T(8,128)}, f32[256,768]{1,0:T(8,128)}, u32[]{:S(2)}, u32[]{:S(2)}) collective-permute-start(f32[256,768]{1,0:T(8,128)} %reduce-scatter.8.cloned.1.call-done), channel_id=1, source_target_pairs={{0,8},{8,0},{16,24},{24,16},{1,9},{9,1},{17,25},{25,17},{2,10},{10... | collective-permute-start | bytes 2359304 | tf_op jit(solution)/shard_map/ppermute | solution.py:471
  486.3 68.2 %collective-permute-start.3 = (f32[256,768]{1,0:T(8,128)}, f32[256,768]{1,0:T(8,128)S(1)}, u32[]{:S(2)}, u32[]{:S(2)}) collective-permute-start(f32[256,768]{1,0:T(8,128)} %reduce-scatter.12.cloned.1.call-done), channel_id=1, source_target_pairs={{0,8},{8,0},{16,24},{24,16},{1,9},{9,1},{17,25},{25,17},{2,10},{10... | collective-permute-start | bytes 2359304 | tf_op jit(solution)/shard_map/ppermute | solution.py:471
Sparse Core Ops, SparseCore 0:
  208.0 39.8 reduce-scatter.7
  250.3 39.6 reduce-scatter.11
  292.3 39.6 reduce-scatter.5
  334.2 39.7 reduce-scatter.9
  376.7 39.7 reduce-scatter.13

commit v3 on v2

v3 whole, which is shorter than its diff:
```python
import functools

import jax
import jax.numpy as jnp
from jax import lax
from jax.experimental import pallas as pl
from jax.experimental.pallas import tpu as pltpu
from jax.sharding import PartitionSpec as P

MESH = pl.DeviceIdType.MESH
F32 = jnp.float32
BF16 = jnp.bfloat16
N_TILE = 6
MLP_EIGHTHS = (3, 3, 2)


def logits_tile(win):
    return next(v for v in range(352, 0, -16) if win % v == 0 and v <= 288)


LOW = -1e30


def _params(mib=60, **kw):
    return pltpu.CompilerParams(vmem_limit_bytes=mib * 2**20, **kw)


def _cost(flops, nbytes, trans=0):
    return pl.CostEstimate(flops=int(flops), bytes_accessed=int(nbytes), transcendentals=int(trans))


def _mlp_body(a_ref, w1_ref, w2_ref, *rest, chunk):
    o_ref, u_ref = rest[-2:]
    ff = w1_ref.shape[1]
    for c in range(ff // chunk):
        cs = slice(c * chunk, (c + 1) * chunk)
        h = jnp.dot(a_ref[...], w1_ref[:, cs], preferred_element_type=F32)
        u_ref[:, cs] = jax.nn.gelu(h).astype(BF16)
    y = jnp.dot(u_ref[...], w2_ref[...], preferred_element_type=F32)
    o_ref[...] = (a_ref[...].astype(F32) + y).astype(BF16)


def mlp(a, w1, w2, out, first, count, tb=512):
    n, d = a.shape
    ff = w1.shape[1]
    extra = [] if out is None else [out]
    return pl.pallas_call(
        functools.partial(_mlp_body, chunk=512),
        grid=(count,),
        in_specs=[
            pl.BlockSpec((tb, d), lambda i: (first + i, 0)),
            pl.BlockSpec((d, ff), lambda i: (0, 0)),
            pl.BlockSpec((ff, d), lambda i: (0, 0)),
        ] + [pl.BlockSpec(memory_space=pl.ANY)] * len(extra),
        out_specs=pl.BlockSpec((tb, d), lambda i: (first + i, 0)),
        out_shape=jax.ShapeDtypeStruct((n, d), BF16),
        scratch_shapes=[pltpu.VMEM((tb, ff), BF16)],
        input_output_aliases={3: 0} if extra else {},
        compiler_params=_params(),
        cost_estimate=_cost(4 * count * tb * d * ff, 4 * count * tb * d + 4 * d * ff, count * tb * ff),
        name="mlp",
    )(a, w1, w2, *extra)


def _logits_block(z_ref, x, w_ref, lab, end, vt):
    tb = x.shape[0]
    lab8 = jnp.broadcast_to(lab, (8, tb))
    sub = lax.broadcasted_iota(jnp.int32, (vt // 8, 8, tb), 0) * 8 + lax.broadcasted_iota(jnp.int32, (vt // 8, 8, tb), 1)
    m8 = s8 = t8 = None
    n_v = w_ref.shape[0] // vt
    for v in range(n_v):
        vs = slice(v * vt, (v + 1) * vt)
        z = lax.dot_general(w_ref[vs, :], x, (((1,), (1,)), ((), ())), preferred_element_type=F32)
        if v == n_v - 1:
            z = jnp.where(lax.broadcasted_iota(jnp.int32, (vt, tb), 0) + v * vt < end, z, LOW)
        z_ref[vs, :] = z
        zr = z_ref[vs, :].reshape(vt // 8, 8, tb)
        tile_max = jnp.max(zr, axis=0)
        m_new = tile_max if v == 0 else jnp.maximum(m8, tile_max)
        e_sum = jnp.sum(jnp.exp(zr - m_new[None]), axis=0)
        hit = jnp.sum(jnp.where(sub == (lab8 - v * vt)[None], zr, 0.0), axis=0)
        s8 = e_sum if v == 0 else s8 * jnp.exp(m8 - m_new) + e_sum
        t8 = hit if v == 0 else t8 + hit
        m8 = m_new
    m = jnp.max(m8, axis=0, keepdims=True)
    s = jnp.sum(s8 * jnp.exp(m8 - m), axis=0, keepdims=True)
    t = jnp.sum(t8, axis=0, keepdims=True)
    return jnp.concatenate([m, s, t, jnp.zeros((5, tb), F32)], axis=0)


def _head_body(
    x_ref, wh_ref, lab_ref, mask_ref, z_ref, xo_ref, wo_ref, coef_out,
    xbuf, wbuf, zbuf, st, got, mine, coef,
    own_sem, w_sem, wo_sem, z_sem, xo_sem, xs_sem, xr_sem, send1, recv1, send2, recv2, *, n_stage, first_row, over, vt,
):
    y, s = lax.axis_index("data"), lax.axis_index("stage")
    h = lax.rem(y + y // 2, 2)
    n_x = n_stage // 2
    x, c = s // 2, lax.rem(s, 2)
    n_q, rows = xbuf.shape[1:3]
    win = wbuf.shape[0]
    n_blk = 2 * n_stage
    y_a = y + 1 - 2 * lax.rem(y, 2)
    sib = s + 1 - 2 * c

    def at(off, flip=0):
        return 2 * lax.rem(x + off, n_x) + lax.rem(c + flip, 2)

    left, right, far = at(n_x - 1), at(1), at(2)
    here = {"data": y, "stage": s}
    to_a = {"data": y_a, "stage": s}
    to_sib = {"data": y, "stage": sib}
    to_left = {"data": y, "stage": left}
    to_right = {"data": y, "stage": right}

    def slot(f, stage):
        return f * n_stage + stage

    sends = [
        (slot(0, s), slot(0, s), to_right, None),
        (slot(0, s), slot(0, s), to_left, None),
        (slot(0, s), slot(1, s), to_a, None),
        (slot(0, s), slot(0, s), to_sib, None),
        (slot(0, left), slot(0, left), to_right, 0),
        (slot(0, right), slot(0, right), to_left, 1),
        (slot(1, s), slot(1, s), to_right, None),
        (slot(1, s), slot(1, s), to_left, None),
        (slot(1, s), slot(1, s), to_sib, None),
        (slot(0, left), slot(0, left), to_sib, None),
        (slot(0, right), slot(0, right), to_sib, None),
        (slot(0, far), slot(1, far), to_a, None),
        (slot(0, far), slot(0, far), to_sib, None),
        (slot(1, left), slot(1, left), to_sib, None),
        (slot(1, right), slot(1, right), to_sib, None),
        (slot(1, far), slot(1, far), to_sib, None),
    ]

    def half(i, part):
        return xbuf.at[i, pl.ds(part * n_q // 2, n_q // 2)]

    def copy(k):
        src, dst, to, part = sends[k]
        return pltpu.make_async_remote_copy(
            src_ref=xbuf.at[src] if part is None else half(src, part),
            dst_ref=xbuf.at[dst] if part is None else half(dst, part),
            send_sem=xs_sem.at[k],
            recv_sem=xr_sem.at[n_blk if part == 1 else dst],
            device_id=to,
            device_id_type=MESH,
        )

    def arrival(ref, sem):
        return pltpu.make_async_remote_copy(
            src_ref=ref, dst_ref=ref, send_sem=xs_sem.at[0], recv_sem=sem, device_id=here, device_id_type=MESH
        )

    def got_block(f, stage):
        arrival(xbuf.at[slot(f, stage)], xr_sem.at[slot(f, stage)]).wait_recv()

    def got_half(part):
        i = slot(0, far)
        arrival(half(i, part), xr_sem.at[n_blk if part == 1 else i]).wait_recv()

    own = pltpu.make_async_copy(x_ref, xbuf.at[slot(0, s)], own_sem)
    own.start()
    w_load = pltpu.make_async_copy(wh_ref.at[pl.ds(pl.multiple_of(h * first_row, 16), win), :], wbuf, w_sem)
    w_load.start()

    peers = [(f, k) for f in range(2) for k in range(n_stage) if (f, k) != (0, 0)]

    def peer(f, k):
        return {"data": y if f == 0 else y_a, "stage": lax.rem(s + k, n_stage)}

    barrier = pltpu.get_barrier_semaphore()
    for f, k in peers:
        pl.semaphore_signal(barrier, inc=1, device_id=peer(f, k), device_id_type=MESH)
    pl.semaphore_wait(barrier, len(peers))

    own.wait()
    for k in range(4):
        copy(k).start()
    w_load.wait()
    w_out = pltpu.make_async_copy(wbuf, wo_ref, wo_sem)
    w_out.start()

    def quarter(stage):
        return pl.ds(pl.multiple_of(stage * rows, rows), rows)

    def z_copy(zs, b, f, stage):
        return pltpu.make_async_copy(
            zbuf.at[zs, :, pl.ds(b * rows, rows)],
            z_ref.at[n_q * (1 - f) + b, stage],
            z_sem.at[zs, b],
        )

    def x_copy(f, stage):
        i = slot(f, stage)
        return pltpu.make_async_copy(xbuf.at[i], xo_ref.at[pl.ds(n_q * (1 - f), n_q), stage], xo_sem.at[i])

    def step(i, carry):
        @pl.when(i == 1)
        def _():
            got_block(0, sib)

        @pl.when(i == 2)
        def _():
            got_block(1, s)
            got_block(0, left)
            got_block(0, right)
            for k in range(4, 11):
                copy(k).start()

        @pl.when(i == 5)
        def _():
            got_half(0)
            got_half(1)
            copy(11).start()
            copy(12).start()
            got_block(1, sib)

        @pl.when(i == 6)
        def _():
            got_block(0, at(n_x - 1, 1))

        @pl.when(i == 7)
        def _():
            got_block(0, at(1, 1))

        @pl.when(i == 9)
        def _():
            got_block(0, at(2, 1))

        @pl.when(i == 10)
        def _():
            got_block(1, left)
            got_block(1, right)
            copy(13).start()
            copy(14).start()

        @pl.when(i == 12)
        def _():
            got_block(1, far)
            copy(15).start()
            got_block(1, at(n_x - 1, 1))

        @pl.when(i == 13)
        def _():
            got_block(1, at(1, 1))

        @pl.when(i == 15)
        def _():
            got_block(1, at(2, 1))

        def among(*ks):
            return functools.reduce(jnp.logical_or, [i == k for k in ks])

        f = jnp.where(jnp.logical_or(among(2, 5), i >= 10), 1, 0)
        flip = jnp.where(among(1, 5, 6, 7, 9, 12, 13, 15), 1, 0)
        off = jnp.where(among(3, 6, 10, 12), n_x - 1, jnp.where(among(4, 7, 11, 13), 1, jnp.where(among(8, 9, 14, 15), 2, 0)))
        stage = at(off, flip)
        blk = slot(f, stage)
        zs = lax.rem(i, 2)

        @pl.when(i >= 2)
        def _():
            for b in range(n_q):
                z_copy(zs, b, f, stage).wait()

        x_copy(f, stage).start()
        lab = lab_ref[f, :, pl.ds(pl.multiple_of(stage * n_q * rows, n_q * rows), n_q * rows)]
        res = _logits_block(zbuf.at[zs], xbuf[blk].reshape(n_q * rows, -1), wbuf, lab, win - over * (1 - h), vt)
        for b in range(n_q):
            st[n_q * (1 - f) + b, :, quarter(stage)] = res[:, b * rows:(b + 1) * rows]
            z_copy(zs, b, f, stage).start()
        return carry

    lax.fori_loop(0, n_blk, step, 0)

    first = []
    for f, k in peers:
        c1 = pltpu.make_async_remote_copy(
            src_ref=st.at[pl.ds(n_q * (1 - f), n_q), :, quarter(lax.rem(s + k, n_stage))],
            dst_ref=got.at[slot(f, k)],
            send_sem=send1.at[slot(f, k)],
            recv_sem=recv1.at[slot(f, k)],
            device_id=peer(f, k),
            device_id_type=MESH,
        )
        c1.start()
        first.append(c1)
    weight = mask_ref[...].astype(F32)
    denom = jnp.maximum(jnp.sum(weight), 1.0)
    mu = jnp.stack([mask_ref[:, pl.ds(pl.multiple_of((n_q * s + b) * rows, rows), rows)].astype(F32) for b in range(n_q)])
    scale = mu / denom
    for c1 in first:
        c1.wait_recv()
    parts = [st[n_q:2 * n_q, :, quarter(s)]] + [got[slot(f, k)] for f, k in peers]
    m = functools.reduce(jnp.maximum, [p[:, 0:1, :] for p in parts])
    z = sum(p[:, 1:2, :] * jnp.exp(p[:, 0:1, :] - m) for p in parts)
    t = sum(p[:, 2:3, :] for p in parts)
    loss = scale * (jnp.log(z) + m - t)
    res = jnp.concatenate([m, scale / z, scale, loss, jnp.zeros((n_q, 4, rows), F32)], axis=1)
    mine[...] = res
    second = []
    for f, k in peers:
        c2 = pltpu.make_async_remote_copy(
            src_ref=mine,
            dst_ref=coef.at[pl.ds(n_q * (1 - f), n_q), :, quarter(s)],
            send_sem=send2.at[slot(f, k)],
            recv_sem=recv2.at[slot(f, k)],
            device_id=peer(f, k),
            device_id_type=MESH,
        )
        c2.start()
        second.append(c2)
    coef[n_q:2 * n_q, :, quarter(s)] = res
    for zs in range(2):
        for b in range(n_q):
            z_copy(zs, b, 0, s).wait()
    for i in range(n_blk):
        x_copy(i // n_stage, i % n_stage).wait()
    w_out.wait()
    for k in range(len(sends)):
        copy(k).wait_send()
    for c1 in first:
        c1.wait_send()
    for c2 in second:
        c2.wait_recv()
    coef_out[...] = coef[...]
    for c2 in second:
        c2.wait_send()


def head(x_rows, w_head, lab, mask, n_stage, win, vt):
    rows, d = x_rows.shape
    n_q = 4
    hr = rows // n_q
    shard = w_head.shape[0]
    n = n_stage * hr
    n_blk = 2 * n_stage
    vm = pl.BlockSpec(memory_space=pltpu.VMEM)
    hbm = pl.BlockSpec(memory_space=pl.ANY)
    dma = pltpu.SemaphoreType.DMA
    x3 = x_rows.reshape(n_q, hr, d)
    total = n_blk * rows
    return pl.pallas_call(
        functools.partial(_head_body, n_stage=n_stage, first_row=shard - win, over=2 * win - shard, vt=vt),
        in_specs=[hbm, hbm, vm, vm],
        out_specs=[hbm, hbm, hbm, vm],
        out_shape=[
            jax.ShapeDtypeStruct((2 * n_q, n_stage, win, hr), F32),
            jax.ShapeDtypeStruct((2 * n_q, n_stage, hr, d), BF16),
            jax.ShapeDtypeStruct((win, d), BF16),
            jax.ShapeDtypeStruct((2 * n_q, 8, n), F32),
        ],
        scratch_shapes=[
            pltpu.VMEM((n_blk, n_q, hr, d), BF16),
            pltpu.VMEM((win, d), BF16),
            pltpu.VMEM((2, win, rows), F32),
            pltpu.VMEM((2 * n_q, 8, n), F32),
            pltpu.VMEM((n_blk, n_q, 8, hr), F32),
            pltpu.VMEM((n_q, 8, hr), F32),
            pltpu.VMEM((2 * n_q, 8, n), F32),
            dma, dma, dma, dma((2, n_q)), dma((n_blk,)), dma((16,)), dma((n_blk + 1,)),
            dma((n_blk,)), dma((n_blk,)), dma((n_blk,)), dma((n_blk,)),
        ],
        compiler_params=_params(56, collective_id=0, has_side_effects=True),
        cost_estimate=_cost(2 * total * d * win, 4 * total * win, total * win),
        name="head",
    )(x3, w_head, lab, mask)


DONE = (12, 17, 27, 31, 38, 41, 44, 47)
N_STEP = 48
AFTER_D, AFTER_1, AFTER_2 = 3, 9, 14
N_SLOT = 4


def _step_of(u):
    phases = (
        (0, 1, 0, 0),
        (8, 5, 1, 0),
        (18, 1, 1, 2),
        (24, 4, 2, 2),
        (32, 1, 2, 4),
        (36, 3, 3, 4),
    )
    tile = group = jnp.int32(0)
    for start, n_tile, tile0, group0 in phases:
        k = jnp.maximum(u - start, 0)
        tile = jnp.where(u >= start, tile0 + k % n_tile, tile)
        group = jnp.where(u >= start, group0 + k // n_tile, group)
    return tile, group


def _grads_body(
    lab_ref, coef_ref, z_ref, x_ref, w_ref, dwo0, dwo1, dwo2, rcv0, rcv1, rcv2, tail_o, tail_r, gx_ref,
    dxb, xb, zb, wb, zt, wt, g, gt, dwb, dwt, rd, r1, r2, ra,
    z_sem, x_sem, w_sem, zt_sem, wt_sem, o_sem, sb_sem, rb_sem, sd_sem, rd_sem, s1_sem, r1_sem, s2_sem, r2_sem, sa_sem, ra_sem,
    *, n_stage,
):
    y, s = lax.axis_index("data"), lax.axis_index("stage")
    n_x = n_stage // 2
    x, c = s // 2, lax.rem(s, 2)
    yh = y // 2
    y_a = y + 1 - 2 * lax.rem(y, 2)
    y_b = lax.axis_size("data") - 1 - y
    x_1, x_3 = x + 1 - 2 * lax.rem(x, 2), n_x - 1 - x
    vt = dwb.shape[1]
    n_own = dwb.shape[0] // 2
    n_t, _, _, rows, d = dxb.shape
    n_tail = dwt.shape[0]
    tail_row = 2 * n_own * vt
    rcv, dwo = (rcv0, rcv1, rcv2), (dwo0, dwo1, dwo2)
    to_sib = {"data": y, "stage": 2 * x + 1 - c}
    to_a = {"data": y_a, "stage": s}
    to_b = {"data": y_b, "stage": s}

    def stage_at(xx):
        return {"data": y, "stage": 2 * xx + c}

    def remote(src, dst, send, recv, to):
        return pltpu.make_async_remote_copy(
            src_ref=src, dst_ref=dst, send_sem=send, recv_sem=recv, device_id=to, device_id_type=MESH
        )

    def row0(tile):
        half = jnp.where(tile < n_own, 1 - yh, yh)
        return pl.multiple_of((half * n_own + tile % n_own) * vt, vt)

    def loads(u):
        tile, t = _step_of(u)
        k = u % 2
        r = pl.ds(row0(tile), vt)
        return (
            pltpu.make_async_copy(z_ref.at[t, :, r, :], zb.at[k], z_sem.at[k]),
            pltpu.make_async_copy(x_ref.at[t], xb.at[k], x_sem.at[k]),
            pltpu.make_async_copy(w_ref.at[r, :], wb.at[k], w_sem.at[k]),
        )

    def tail_load(t):
        return pltpu.make_async_copy(z_ref.at[t, :, pl.ds(tail_row, n_tail), :], zt, zt_sem)

    for cp in loads(jnp.int32(0)):
        cp.start()
    w_tail = pltpu.make_async_copy(w_ref.at[pl.ds(tail_row, n_tail), :], wt, wt_sem)
    w_tail.start()

    peers = (to_sib, to_a, to_b, stage_at(x_1), stage_at(x_3))
    barrier = pltpu.get_barrier_semaphore()
    for p in peers:
        pl.semaphore_signal(barrier, inc=1, device_id=p, device_id_type=MESH)
    pl.semaphore_wait(barrier, len(peers))
    w_tail.wait()

    def send_d(t):
        return remote(dxb.at[t, :, 1 - c], rd.at[t % 2], sd_sem.at[t], rd_sem.at[t], to_sib)

    def order(t):
        even = t % 2 == 0
        return jnp.where(even, x_1, x_3), jnp.where(even, x_3, x_1)

    def send_1(t, k):
        p1, _ = order(t)
        mine = p1 if k == 0 else n_x - 1 - x_1
        return remote(dxb.at[t, mine, c], r1.at[t % N_SLOT, k], s1_sem.at[t, k], r1_sem.at[t, k], stage_at(p1))

    def send_2(t):
        _, p2 = order(t)
        return remote(dxb.at[t, p2, c], r2.at[t % N_SLOT], s2_sem.at[t], r2_sem.at[t], stage_at(p2))

    def send_a(t):
        return remote(dxb.at[t, x, c], ra.at[t], sa_sem.at[t], ra_sem.at[t], to_a)

    def scheduled(u, after):
        t = sum(jnp.where(u == done + after, i, 0) for i, done in enumerate(DONE))
        return functools.reduce(jnp.logical_or, [u == done + after for done in DONE]), t

    def exchanges(u):
        now2, t2 = scheduled(u, AFTER_2)

        @pl.when(now2)
        def _():
            send_2(t2).wait_recv()
            dxb[t2, x, c] = dxb[t2, x, c] + r2[t2 % N_SLOT]

            @pl.when(t2 < n_t // 2)
            def _():
                send_a(t2).start()

        now1, t1 = scheduled(u, AFTER_1)

        @pl.when(now1)
        def _():
            _, p2 = order(t1)
            send_1(t1, 0).wait_recv()
            send_1(t1, 1).wait_recv()
            dxb[t1, p2, c] = dxb[t1, p2, c] + r1[t1 % N_SLOT, 1]
            send_2(t1).start()
            dxb[t1, x, c] = dxb[t1, x, c] + r1[t1 % N_SLOT, 0]

        now, t = scheduled(u, AFTER_D)

        @pl.when(now)
        def _():
            send_d(t).wait_recv()
            for xx in range(n_x):
                dxb[t, xx, c] = dxb[t, xx, c] + rd[t % 2, xx]
            send_1(t, 0).start()
            send_1(t, 1).start()

    def g_tile(z, g_out, t, base):
        n_row = z.shape[1]
        sub = lax.broadcasted_iota(jnp.int32, (n_row // 8, 8, rows), 0) * 8 + lax.broadcasted_iota(jnp.int32, (n_row // 8, 8, rows), 1)
        for i in range(n_stage):
            cs = slice(i * rows, (i + 1) * rows)
            m8 = jnp.broadcast_to(coef_ref[t, 0:1, cs], (8, rows))
            c8 = jnp.broadcast_to(coef_ref[t, 1:2, cs], (8, rows))
            q8 = jnp.broadcast_to(coef_ref[t, 2:3, cs], (8, rows))
            lab8 = jnp.broadcast_to(lab_ref[t, :, cs], (8, rows)) - base
            zr = z[i].reshape(n_row // 8, 8, rows)
            e = jnp.exp(zr - m8[None]) * c8[None]
            gi = jnp.where(sub == lab8[None], e - q8[None], e)
            g_out[:, cs] = gi.reshape(n_row, rows).astype(BF16)

    def step(u, carry):
        tile, t = _step_of(u)
        k = u % 2

        @pl.when(u < N_STEP)
        def _():
            for cp in loads(u):
                cp.wait()

        @pl.when(u < N_STEP - 1)
        def _():
            for cp in loads(u + 1):
                cp.start()

        last = jnp.logical_and(tile == 2 * n_own - 1, u < N_STEP)

        @pl.when(last)
        def _():
            tail_load(t).start()

        exchanges(u)

        @pl.when(u < N_STEP)
        def _():
            g_tile(zb.at[k], g, t, row0(tile))
            xk = xb[k].reshape(n_stage * rows, d)
            dxp = lax.dot_general(g[...], wb[k], (((0,), (0,)), ((), ())), preferred_element_type=F32)
            dxb[t] = jnp.where(tile == 0, 0.0, dxb[t]) + dxp.reshape(n_x, 2, rows, d)
            dwb[tile] = jnp.where(t == 0, 0.0, dwb[tile]) + jnp.dot(g[...], xk, preferred_element_type=F32)

        @pl.when(last)
        def _():
            tail_load(t).wait()
            g_tile(zt, gt, t, tail_row)
            xk = xb[k].reshape(n_stage * rows, d)
            dxp = lax.dot_general(gt[...], wt[...], (((0,), (0,)), ((), ())), preferred_element_type=F32)
            dxb[t] = dxb[t] + dxp.reshape(n_x, 2, rows, d)
            dwt[...] = jnp.where(t == 0, 0.0, dwt[...]) + jnp.dot(gt[...], xk, preferred_element_type=F32)
            send_d(t).start()

        for j, end in enumerate((7, 23, 35)):
            @pl.when(u == end)
            def _(j=j):
                send_b(j).start()

        return carry

    def send_b(j):
        return remote(dwb.at[j], rcv[j], sb_sem.at[j], rb_sem.at[j], to_b)

    lax.fori_loop(0, N_STEP, step, 0)

    outs = [pltpu.make_async_copy(dwb.at[n_own + j], dwo[j], o_sem.at[j]) for j in range(n_own)]
    outs.append(pltpu.make_async_copy(dwt, tail_o, o_sem.at[n_own]))
    for cp in outs:
        cp.start()
    tail = remote(dwt, tail_r, sb_sem.at[n_own], rb_sem.at[n_own], to_b)
    tail.start()

    def drain(u, carry):
        exchanges(u)
        return carry

    lax.fori_loop(N_STEP, DONE[-1] + AFTER_2 + 1, drain, 0)

    for q in range(n_t // 2):
        send_a(q).wait_recv()
        gx_ref[q] = dxb[n_t // 2 + q, x, c] + ra[q]
    for cp in outs:
        cp.wait()
    for j in range(n_own):
        send_b(j).wait()
    tail.wait()
    for t in range(n_t):
        send_d(t).wait_send()
        send_1(t, 0).wait_send()
        send_1(t, 1).wait_send()
        send_2(t).wait_send()
        if t < n_t // 2:
            send_a(t).wait_send()


def grads(lab, coef, z, x, w, vt):
    n_t, n_stage, rows, d = x.shape
    win = w.shape[0]
    n_tail = win - N_TILE * vt
    n = n_stage * rows
    vm = pl.BlockSpec(memory_space=pltpu.VMEM)
    hbm = pl.BlockSpec(memory_space=pl.ANY)
    dma = pltpu.SemaphoreType.DMA
    n_x = n_stage // 2
    tile = jax.ShapeDtypeStruct((vt, d), F32)
    tail = jax.ShapeDtypeStruct((n_tail, d), F32)
    return pl.pallas_call(
        functools.partial(_grads_body, n_stage=n_stage),
        in_specs=[vm, vm, hbm, hbm, hbm],
        out_specs=[hbm] * 8 + [vm],
        out_shape=[tile] * N_TILE + [tail] * 2 + [jax.ShapeDtypeStruct((n_t // 2, rows, d), F32)],
        scratch_shapes=[
            pltpu.VMEM((n_t, n_x, 2, rows, d), F32),
            pltpu.VMEM((2, n_stage, rows, d), BF16),
            pltpu.VMEM((2, n_stage, vt, rows), F32),
            pltpu.VMEM((2, vt, d), BF16),
            pltpu.VMEM((n_stage, n_tail, rows), F32),
            pltpu.VMEM((n_tail, d), BF16),
            pltpu.VMEM((vt, n), BF16),
            pltpu.VMEM((n_tail, n), BF16),
            pltpu.VMEM((N_TILE, vt, d), F32),
            pltpu.VMEM((n_tail, d), F32),
            pltpu.VMEM((2, n_x, rows, d), F32),
            pltpu.VMEM((N_SLOT, 2, rows, d), F32),
            pltpu.VMEM((N_SLOT, rows, d), F32),
            pltpu.VMEM((n_t // 2, rows, d), F32),
            dma((2,)), dma((2,)), dma((2,)), dma, dma, dma((4,)), dma((4,)), dma((4,)),
            dma((n_t,)), dma((n_t,)), dma((n_t, 2)), dma((n_t, 2)), dma((n_t,)), dma((n_t,)), dma((n_t // 2,)), dma((n_t // 2,)),
        ],
        compiler_params=pltpu.CompilerParams(vmem_limit_bytes=67043328, collective_id=1, has_side_effects=True),
        cost_estimate=_cost(4 * n_t * n * d * win, 4 * n_t * n * win, n_t * n * win),
        name="grads",
    )(lab, coef, z, x, w)


def solution(mesh):
    n_data, n_stage = mesh.shape["data"], mesh.shape["stage"]
    tok_spec = P(("pod", "data", "stage"), None)
    rep_spec = P(("pod", "data"))
    vocab_spec = P("stage", None)
    layer_spec = P("stage", None, None)
    swap_a = [(i, i ^ 1) for i in range(n_data)]
    swap_b = [(i, n_data - 1 - i) for i in range(n_data)]

    def local_step(x_rows, w_head, labels, loss_mask, w_embed, tok_ids, act_in, w_up, w_down):
        y, s = lax.axis_index("data"), lax.axis_index("stage")
        shard, d = w_head.shape
        yh = y >> 1
        h = (y ^ yh) & 1
        step_rows = 16 * N_TILE
        win = -(-shard // (2 * step_rows)) * step_rows
        vt = (win // N_TILE - 1) // 16 * 16
        first_row = shard - win
        over = 2 * win - shard

        def over_a(v):
            return lax.ppermute(v, "data", swap_a)

        def over_b(v):
            return lax.ppermute(v, "data", swap_b)

        lab_a = over_a(labels)

        def local(lab):
            lab = lab - (s * shard + h * first_row)
            return jnp.where(lab < win - over * (1 - h), lab, -1)

        n_tok = labels.shape[0]
        lab_two = jnp.stack([local(labels), local(lab_a)])
        z, x_all, w_win, coef = head(x_rows, w_head, lab_two.reshape(2, 1, n_tok), loss_mask.reshape(1, -1), n_stage, win, logits_tile(win))
        n_t, _, rows, _ = x_all.shape
        lab = lab_two[::-1].reshape(2, n_stage, n_t // 2, rows).transpose(0, 2, 1, 3).reshape(n_t, 1, n_stage * rows)
        *parts, tail, tail_far, gx = grads(lab, coef, z, x_all, w_win, vt)
        grad_x = gx.reshape(x_rows.shape)

        loss_t = jnp.sum(coef[:, 3, :], axis=1).reshape(2, n_t // 2).sum(axis=1)
        loss_pair = loss_t[0] + loss_t[1]
        loss_far = over_b(loss_pair.reshape(1, 1))[0, 0]
        mean_loss = (loss_pair + loss_far) / n_data

        offset = s * shard
        local_ids = tok_ids - offset
        in_slice = (local_ids >= 0) & (local_ids < shard)
        rows_emb = jnp.take(w_embed, jnp.clip(local_ids, 0, shard - 1), axis=0)
        emb_part = jnp.where(in_slice[:, None], rows_emb, jnp.zeros_like(rows_emb))
        emb_part, _ = lax.optimization_barrier((emb_part, coef))
        embed_out = lax.psum_scatter(emb_part, "stage", scatter_dimension=0, tiled=True)

        half = N_TILE // 2
        kept, got = parts[:half], parts[half:]
        fins, fas, fbs = [], [], []
        for j in range(half):
            fins.append(lax.optimization_barrier(((kept[j] + got[j]) / n_data).astype(BF16)))
            fbs.append(over_b(fins[j]))
            fas.append(over_a(fins[j]))
        fin_t = lax.optimization_barrier(((tail + tail_far) / n_data).astype(BF16))
        fin_ta = over_a(fin_t)

        mlp_out, done = None, 0
        blocks = n_tok // 512
        for part in MLP_EIGHTHS:
            mlp_out = mlp(act_in, w_up[0], w_down[0], mlp_out, done, blocks * part // 8)
            done += blocks * part // 8

        grad_head = jnp.zeros((shard, d), BF16)
        for j in range(half):
            fin_ab = over_a(fbs[j])
            for v, hh, part in ((fins[j], h, yh), (fas[j], 1 - h, yh), (fbs[j], h, 1 - yh), (fin_ab, 1 - h, 1 - yh)):
                row = hh * first_row + (part * half + j) * vt
                grad_head = lax.dynamic_update_slice(grad_head, v, (row, 0))
        lower = jnp.where(h == 0, fin_t, fin_ta)
        upper = jnp.where(h == 0, fin_ta, fin_t)
        grad_head = lax.dynamic_update_slice(grad_head, lower[: fin_t.shape[0] - over], (N_TILE * vt, 0))
        grad_head = lax.dynamic_update_slice(grad_head, upper, (first_row + N_TILE * vt, 0))

        return mean_loss.reshape(1), grad_x, grad_head, embed_out, mlp_out

    return jax.shard_map(
        local_step,
        mesh=mesh,
        in_specs=(tok_spec, vocab_spec, rep_spec, rep_spec, vocab_spec, rep_spec, tok_spec, layer_spec, layer_spec),
        out_specs=(P("pod"), tok_spec, P(("pod", "stage"), None), tok_spec, tok_spec),
        check_vma=False,
    )
```

time: 567 us -> 507 us (0.89)
  starting transfers between devices: 98.9 us -> 35.8 us
  Pallas kernels: 290 us -> 335 us
  waiting for transfers between devices: 90.2 us -> 47.7 us
    ppermute x7 -> x4, starting transfers between devices: 89.7 us -> 29.6 us  [over_b(): return lax.ppermute(v, 'data', swap_b)]
    pallas_call x7 -> x1, Pallas kernels: 153 us -> 190 us  [grads(): pl.pallas_call(functools.partial(_grads_body, n_stage=n_stage), in_specs=...]
    ppermute x7 -> x4, waiting for transfers between devices: 33 us -> 3.32 us  [over_b(): return lax.ppermute(v, 'data', swap_b)]
    ppermute x9 -> x8, waiting for transfers between devices: 56.9 us -> 44.3 us  [over_a(): return lax.ppermute(v, 'data', swap_a)]
    pallas_call x1 -> x3, Pallas kernels: 47.2 us -> 57.1 us  [mlp(): pl.pallas_call(functools.partial(_mlp_body, chunk=512), grid=(count,), in...]
  transfers between devices with their start and end apart: 21 -> 13, of which waited for: 6 -> 3; matrix products, arithmetic and copies ran while one was open for 11% -> 13% of each run, Pallas kernels for 17% -> 49%
where the time goes in v3:
time: 507 us; the launch traced here: 504 us
  Pallas kernels  335 us (66%)
  local copies, waits for them, and re-layouts  49.3 us (10%)
  waiting for transfers between devices  47.7 us (9%)
  starting transfers between devices  35.8 us (7%)
  other arithmetic  19.4 us (4%)
  between operations  17.3 us (3%)
    pallas_call x1, Pallas kernels, grads(): pl.pallas_call(functools.partial(_grads_body, n_stage=n_stage), in_specs=...  190 us
    pallas_call x1, Pallas kernels, head(): pl.pallas_call(functools.partial(_head_body, n_stage=n_stage, first_row=s...  87.3 us
    pallas_call x3, Pallas kernels, mlp(): pl.pallas_call(functools.partial(_mlp_body, chunk=512), grid=(count,), in...  57.1 us
    ppermute x8, waiting for transfers between devices, over_a(): return lax.ppermute(v, 'data', swap_a)  44.3 us
    ppermute x4, starting transfers between devices, over_b(): return lax.ppermute(v, 'data', swap_b)  29.6 us
    gather x1, local copies, waits for them, and re-layouts, local_step(): rows_emb = jnp.take(w_embed, jnp.clip(local_ids, 0, shard - 1), axis=0)  24 us
    dynamic_update_slice x12, local copies, waits for them, and re-layouts, local_step(): grad_head = lax.dynamic_update_slice(grad_head, v, (row, 0))  16.9 us
  transfers between devices with their start and end apart: 13, of which 3 were waited for; matrix products, arithmetic and copies ran while one was open for 13% of the time, Pallas kernels for 49%

profile of v3, /device:TPU:97, one launch (start us, length us, event | category | flops | bytes accessed | tf_op | source)
XLA Modules:
  0.0 504.1 jit_solution(13838514111685577793)
XLA Ops:
  7.2 2.8 collective-permute-start
  11.5 24.0 %gather_fusion = bf16[4096,768]{1,0:T(8,128)(2,1)} fusion(bf16[6288,768]{1,0:T(8,128)(2,1)} %param.13, s32[4096]{0:T(1024)S(1)} %fusion.1), kind=kCustom, calls=%fused_computation | custom fusion | bytes 12599296 | tf_op jit(solution)/shard_map/jit(_take)/gather | solution.py:696
  35.5 8.0 %select_select_fusion = bf16[4096,768]{1,0:T(8,128)(2,1)} fusion(bf16[4096,768]{1,0:T(8,128)(2,1)} %gather_fusion, pred[4096]{0:T(1024)(128)(4,1)S(1)} %get-tuple-element.34, pred[4096]{0:T(1024)(128)(4,1)S(1)} %get-tuple-element.33), kind=kLoop, calls=%fused_computation.1 | loop fusion | flops 6291456 | bytes 12591104 | tf_op jit(solution)/shard_map/jit(_where)/select_n | solution.py:697
  43.5 20.7 %mlp.3.rest_0_ = bf16[4096,768]{1,0:T(8,128)(2,1)} custom-call(bf16[4096,768]{1,0:T(8,128)(2,1)} %a_ref.5, bf16[768,3072]{1,0:T(8,128)(2,1)} %bitcast.18, bf16[3072,768]{1,0:T(8,128)(2,1)} %bitcast.21), custom_call_target="tpu_custom_call" | custom-call | flops 14495514624 | bytes 14155776 | tf_op jit(solution)/shard_map/mlp/pallas_call | solution.py:47
  64.9 87.3 %head.1 = (f32[8,8,3168,128]{3,2,1,0:T(8,128)}, bf16[8,8,128,768]{3,2,1,0:T(8,128)(2,1)}, bf16[3168,768]{1,0:T(8,128)(2,1)}, f32[8,8,1024]{2,1,0:T(8,128)}) custom-call(bf16[4,128,768]{2,1,0:T(8,128)(2,1)} %bitcast.24, bf16[6288,768]{1,0:T(8,128)(2,1)} %wh_ref.1, s32[2,1,4096]{2,1,0:T(1,128)} %reshape.46.lab_ref, s32[1,4096]{1,0:T(1,128)} %bitcast.25), custom_call_target="tpu_custom_call" | custom-call | flops 39862665216 | bytes 103809024 | tf_op jit(solution)/shard_map/head/pallas_call | solution.py:346
  152.3 20.9 %mlp.4.rest_0_ = bf16[4096,768]{1,0:T(8,128)(2,1)} custom-call(bf16[4096,768]{1,0:T(8,128)(2,1)} %a_ref.5, bf16[768,3072]{1,0:T(8,128)(2,1)} %bitcast.19, bf16[3072,768]{1,0:T(8,128)(2,1)} %bitcast.22, bf16[4096,768]{1,0:T(8,128)(2,1)} %mlp.3.rest_0_), custom_call_target="tpu_custom_call", output_to_operand_aliasing={{}: (3, {})} | custom-call | flops 14495514624 | bytes 14155776 | tf_op jit(solution)/shard_map/mlp/pallas_call | solution.py:47
  174.7 190.2 %grads.1 = (f32[512,768]{1,0:T(8,128)}, f32[512,768]{1,0:T(8,128)}, f32[512,768]{1,0:T(8,128)}, f32[512,768]{1,0:T(8,128)}, f32[512,768]{1,0:T(8,128)}, /*index=...) custom-call(s32[8,1,1024]{2,1,0:T(1,128)} %bitcast.17, ...), custom_call_target="tpu_custom_call" | custom-call | flops 79725330432 | bytes 103809024 | tf_op jit(solution)/shard_map/grads/pallas_call | solution.py:619
  364.9 2.1 multiply_convert_fusion.2
  367.0 3.3 collective-permute-start.3
  370.3 15.4 %mlp.5 = bf16[4096,768]{1,0:T(8,128)(2,1)} custom-call(bf16[4096,768]{1,0:T(8,128)(2,1)} %a_ref.5, bf16[768,3072]{1,0:T(8,128)(2,1)} %bitcast.20, bf16[3072,768]{1,0:T(8,128)(2,1)} %bitcast.23, bf16[4096,768]{1,0:T(8,128)(2,1)} %mlp.4.rest_0_), custom_call_target="tpu_custom_call", output_to_operand_aliasing={{}: (3, {})} | custom-call | flops 9663676416 | bytes 12582912 | tf_op jit(solution)/shard_map/mlp/pallas_call | solution.py:47
  385.7 2.1 multiply_convert_fusion.1
  388.2 2.1 multiply_convert_fusion
  390.3 2.5 collective-permute-start.9
  393.0 1.1 slice_reduce_fusion
  396.2 23.4 %collective-permute-start.1 = (f32[1,1]{1,0:T(1,128)}, f32[1,1]{1,0:T(1,128)}, u32[]{:S(2)}, u32[]{:S(2)}) collective-permute-start(f32[1,1]{1,0:T(1,128)} %bitcast.5), channel_id=1, source_target_pairs={{0,24},{8,16},{16,8},{24,0},{1,25},{9,17},{17,9},{25,1},{2,26},{10... | collective-permute-start | bytes 20 | tf_op jit(solution)/shard_map/ppermute | solution.py:672
  419.6 3.3 collective-permute-done.1
  422.9 1.1 multiply_convert_fusion.3
  424.0 4.4 broadcast_in_dim.33
  428.5 0.9 constant_dynamic-update-slice_fusion.11
  430.1 1.6 collective-permute-start.8
  431.8 2.1 constant_dynamic-update-slice_fusion.10
  434.8 1.3 collective-permute-start.11
  436.3 2.1 constant_dynamic-update-slice_fusion.8
  439.3 2.2 constant_dynamic-update-slice_fusion.6
  441.4 2.1 constant_dynamic-update-slice_fusion.5
  443.5 29.1 %collective-permute-done.7 = bf16[512,768]{1,0:T(8,128)(2,1)S(1)} collective-permute-done((bf16[512,768]{1,0:T(8,128)(2,1)}, bf16[512,768]{1,0:T(8,128)(2,1)S(1)}, u32[]{:S(2)}, u32[]{:S(2)}) %collective-permute-start.7) | collective-permute-done | bytes 786464 | tf_op jit(solution)/shard_map/ppermute | solution.py:669
  472.6 0.9 constant_dynamic-update-slice_fusion.4
  474.5 0.9 constant_dynamic-update-slice_fusion.2
  475.4 2.1 constant_dynamic-update-slice_fusion.1
  477.5 15.2 %collective-permute-done.10 = bf16[512,768]{1,0:T(8,128)(2,1)S(1)} collective-permute-done((bf16[512,768]{1,0:T(8,128)(2,1)}, bf16[512,768]{1,0:T(8,128)(2,1)S(1)}, u32[]{:S(2)}, u32[]{:S(2)}) %collective-permute-start.10) | collective-permute-done | bytes 786464 | tf_op jit(solution)/shard_map/ppermute | solution.py:669
  492.6 0.9 constant_dynamic-update-slice_fusion
  494.9 1.1 copy.34
  (39 shorter events, 9.5 us)
Async XLA Ops:
  7.2 487.8 %reduce-scatter.2.cloned.1.call-start = ((), (), s32[]{:S(2)}) async-start(), calls=%async_computation.1 | async-start | bytes 7077888 | tf_op jit(solution)/shard_map/reduce_scatter | solution.py:699
  7.2 57.0 %collective-permute-start = (s32[4096]{0:T(1024)}, s32[4096]{0:T(1024)S(1)}, u32[]{:S(2)}, u32[]{:S(2)}) collective-permute-start(s32[4096]{0:T(1024)} %param.11), channel_id=1, source_target_pairs={{0,8},{8,0},{16,24},{24,16},{1,9},{9,1},{17,25},{25,17},{2,10},{10... | collective-permute-start | bytes 49160 | tf_op jit(solution)/shard_map/ppermute | solution.py:669
  43.5 20.7 %copy-start.1 = (s32[4096]{0:T(1024)S(1)}, s32[4096]{0:T(1024)}, u32[]{:S(2)}) copy-start(s32[4096]{0:T(1024)} %param.11) | copy-start | bytes 49156
  367.0 25.8 %collective-permute-start.3 = (bf16[512,768]{1,0:T(8,128)(2,1)S(1)}, bf16[512,768]{1,0:T(8,128)(2,1)S(1)}, u32[]{:S(2)}, u32[]{:S(2)}) collective-permute-start(bf16[512,768]{1,0:T(8,128)(2,1)S(1)} %multiply_convert_fusion.2), channel_id=1, source_target_pairs={{0,24},{8,16},{16,8},{24,0},{1,25},{9,17},{17,9},{25,1},{2,26},{10... | collective-permute-start | bytes 2359304 | tf_op jit(solution)/shard_map/ppermute | solution.py:672
  385.7 44.3 %collective-permute-start.2 = (bf16[512,768]{1,0:T(8,128)(2,1)S(1)}, bf16[512,768]{1,0:T(8,128)(2,1)}, u32[]{:S(2)}, u32[]{:S(2)}) collective-permute-start(bf16[512,768]{1,0:T(8,128)(2,1)S(1)} %multiply_convert_fusion.2), channel_id=1, source_target_pairs={{0,8},{8,0},{16,24},{24,16},{1,9},{9,1},{17,25},{25,17},{2,10},{10... | collective-permute-start | bytes 2359304 | tf_op jit(solution)/shard_map/ppermute | solution.py:669
  387.8 43.8 %collective-permute-start.6 = (bf16[512,768]{1,0:T(8,128)(2,1)S(1)}, bf16[512,768]{1,0:T(8,128)(2,1)}, u32[]{:S(2)}, u32[]{:S(2)}) collective-permute-start(bf16[512,768]{1,0:T(8,128)(2,1)S(1)} %multiply_convert_fusion.1), channel_id=1, source_target_pairs={{0,24},{8,16},{16,8},{24,0},{1,25},{9,17},{17,9},{25,1},{2,26},{10... | collective-permute-start | bytes 2359304 | tf_op jit(solution)/shard_map/ppermute | solution.py:672
  390.3 44.5 %collective-permute-start.9 = (bf16[512,768]{1,0:T(8,128)(2,1)S(1)}, bf16[512,768]{1,0:T(8,128)(2,1)}, u32[]{:S(2)}, u32[]{:S(2)}) collective-permute-start(bf16[512,768]{1,0:T(8,128)(2,1)S(1)} %multiply_convert_fusion), channel_id=1, source_target_pairs={{0,24},{8,16},{16,8},{24,0},{1,25},{9,17},{17,9},{25,1},{2,26},{10... | collective-permute-start | bytes 2359304 | tf_op jit(solution)/shard_map/ppermute | solution.py:672
  392.8 43.3 %collective-permute-start.4 = (bf16[512,768]{1,0:T(8,128)(2,1)S(1)}, bf16[512,768]{1,0:T(8,128)(2,1)}, u32[]{:S(2)}, u32[]{:S(2)}) collective-permute-start(bf16[512,768]{1,0:T(8,128)(2,1)S(1)} %collective-permute-done.3), channel_id=1, source_target_pairs={{0,8},{8,0},{16,24},{24,16},{1,9},{9,1},{17,25},{25,17},{2,10},{10... | collective-permute-start | bytes 2359304 | tf_op jit(solution)/shard_map/ppermute | solution.py:669
  396.2 26.7 %collective-permute-start.1 = (f32[1,1]{1,0:T(1,128)}, f32[1,1]{1,0:T(1,128)}, u32[]{:S(2)}, u32[]{:S(2)}) collective-permute-start(f32[1,1]{1,0:T(1,128)} %bitcast.5), channel_id=1, source_target_pairs={{0,24},{8,16},{16,8},{24,0},{1,25},{9,17},{17,9},{25,1},{2,26},{10... | collective-permute-start | bytes 20 | tf_op jit(solution)/shard_map/ppermute | solution.py:672
  422.9 16.3 %collective-permute-start.5 = (bf16[512,768]{1,0:T(8,128)(2,1)S(1)}, bf16[512,768]{1,0:T(8,128)(2,1)}, u32[]{:S(2)}, u32[]{:S(2)}) collective-permute-start(bf16[512,768]{1,0:T(8,128)(2,1)S(1)} %multiply_convert_fusion.1), channel_id=1, source_target_pairs={{0,8},{8,0},{16,24},{24,16},{1,9},{9,1},{17,25},{25,17},{2,10},{10... | collective-permute-start | bytes 2359304 | tf_op jit(solution)/shard_map/ppermute | solution.py:669
  430.1 44.4 %collective-permute-start.8 = (bf16[512,768]{1,0:T(8,128)(2,1)S(1)}, bf16[512,768]{1,0:T(8,128)(2,1)S(1)}, u32[]{:S(2)}, u32[]{:S(2)}) collective-permute-start(bf16[512,768]{1,0:T(8,128)(2,1)S(1)} %multiply_convert_fusion), channel_id=1, source_target_pairs={{0,8},{8,0},{16,24},{24,16},{1,9},{9,1},{17,25},{25,17},{2,10},{10... | collective-permute-start | bytes 2359304 | tf_op jit(solution)/shard_map/ppermute | solution.py:669
  431.7 41.0 %collective-permute-start.7 = (bf16[512,768]{1,0:T(8,128)(2,1)}, bf16[512,768]{1,0:T(8,128)(2,1)S(1)}, u32[]{:S(2)}, u32[]{:S(2)}) collective-permute-start(bf16[512,768]{1,0:T(8,128)(2,1)} %collective-permute-done.6), channel_id=1, source_target_pairs={{0,8},{8,0},{16,24},{24,16},{1,9},{9,1},{17,25},{25,17},{2,10},{10... | collective-permute-start | bytes 2359304 | tf_op jit(solution)/shard_map/ppermute | solution.py:669
  434.8 58.8 %collective-permute-start.11 = (bf16[96,768]{1,0:T(8,128)(2,1)S(1)}, bf16[96,768]{1,0:T(8,128)(2,1)S(1)}, u32[]{:S(2)}, u32[]{:S(2)}) collective-permute-start(bf16[96,768]{1,0:T(8,128)(2,1)S(1)} %multiply_convert_fusion.3), channel_id=1, source_target_pairs={{0,8},{8,0},{16,24},{24,16},{1,9},{9,1},{17,25},{25,17},{2,10},{10... | collective-permute-start | bytes 442376 | tf_op jit(solution)/shard_map/ppermute | solution.py:669
  436.1 56.5 %collective-permute-start.10 = (bf16[512,768]{1,0:T(8,128)(2,1)}, bf16[512,768]{1,0:T(8,128)(2,1)S(1)}, u32[]{:S(2)}, u32[]{:S(2)}) collective-permute-start(bf16[512,768]{1,0:T(8,128)(2,1)} %collective-permute-done.9), channel_id=1, source_target_pairs={{0,8},{8,0},{16,24},{24,16},{1,9},{9,1},{17,25},{25,17},{2,10},{10... | collective-permute-start | bytes 2359304 | tf_op jit(solution)/shard_map/ppermute | solution.py:669
  439.3 55.7 %copy-start = (f32[4,128,768]{2,1,0:T(8,128)S(1)}, f32[4,128,768]{2,1,0:T(8,128)}, u32[]{:S(2)}) copy-start(f32[4,128,768]{2,1,0:T(8,128)} %get-tuple-element.23) | copy-start | bytes 4718596
Sparse Core Ops, SparseCore 0:
  152.5 39.8 reduce-scatter.1

commit v4 on v3

--- a/solution.py
+++ b/solution.py
@@ -11,7 +11,6 @@
 F32 = jnp.float32
 BF16 = jnp.bfloat16
 N_TILE = 6
-MLP_EIGHTHS = (3, 3, 2)
 
 
 def logits_tile(win):
@@ -78,7 +77,7 @@
         tile_max = jnp.max(zr, axis=0)
         m_new = tile_max if v == 0 else jnp.maximum(m8, tile_max)
         e_sum = jnp.sum(jnp.exp(zr - m_new[None]), axis=0)
-        hit = jnp.sum(jnp.where(sub == (lab8 - v * vt)[None], zr, 0.0), axis=0)
+        hit = jnp.sum(jnp.where(sub + v * vt == lab8[None], zr, 0.0), axis=0)
         s8 = e_sum if v == 0 else s8 * jnp.exp(m8 - m_new) + e_sum
         t8 = hit if v == 0 else t8 + hit
         m8 = m_new
@@ -370,10 +369,18 @@
     )(x3, w_head, lab, mask)
 
 
-DONE = (12, 17, 27, 31, 38, 41, 44, 47)
+DONE = (12, 17, 27, 31, 35, 41, 44, 47)
+SENT = (7, 23, 38)
 N_STEP = 48
-AFTER_D, AFTER_1, AFTER_2 = 3, 9, 14
-N_SLOT = 4
+AFTER_D, AFTER_1, AFTER_2 = 3, 12, 18
+SLOTS_1, SLOTS_2 = 6, 4
+
+
+EVENTS = (
+    (48, ("fin", 0)), (49, ("fin", 1)), (51, ("tail", 0)), (54, ("fin", 2)),
+    (62, ("pass", 0)), (66, ("pass", 1)), (67, ("pass", 2)),
+)
+LAST_EVENT = 67
 
 
 def _step_of(u):
@@ -382,8 +389,8 @@
         (8, 5, 1, 0),
         (18, 1, 1, 2),
         (24, 4, 2, 2),
-        (32, 1, 2, 4),
-        (36, 3, 3, 4),
+        (36, 1, 2, 5),
+        (39, 3, 3, 5),
     )
     tile = group = jnp.int32(0)
     for start, n_tile, tile0, group0 in phases:
@@ -394,24 +401,28 @@
 
 
 def _grads_body(
-    lab_ref, coef_ref, z_ref, x_ref, w_ref, dwo0, dwo1, dwo2, rcv0, rcv1, rcv2, tail_o, tail_r, gx_ref,
-    dxb, xb, zb, wb, zt, wt, g, gt, dwb, dwt, rd, r1, r2, ra,
+    lab_ref, coef_ref, z_ref, x_ref, w_ref, gh_ref, rcv0, rcv1, rcv2, gx_ref, loss_ref,
+    dxb, dwb, dwt, tr, rd, r1, r2, ra, ls, lr,
     z_sem, x_sem, w_sem, zt_sem, wt_sem, o_sem, sb_sem, rb_sem, sd_sem, rd_sem, s1_sem, r1_sem, s2_sem, r2_sem, sa_sem, ra_sem,
-    *, n_stage,
+    sf_sem, rf_sem, st_sem, l_sem,
+    *, n_stage, first_row, over,
 ):
     y, s = lax.axis_index("data"), lax.axis_index("stage")
     n_x = n_stage // 2
     x, c = s // 2, lax.rem(s, 2)
     yh = y // 2
     y_a = y + 1 - 2 * lax.rem(y, 2)
-    y_b = lax.axis_size("data") - 1 - y
+    n_data = lax.axis_size("data")
+    y_b = n_data - 1 - y
+    h = lax.rem(y + yh, 2)
     x_1, x_3 = x + 1 - 2 * lax.rem(x, 2), n_x - 1 - x
     vt = dwb.shape[1]
     n_own = dwb.shape[0] // 2
     n_t, _, _, rows, d = dxb.shape
     n_tail = dwt.shape[0]
+    piece = min(rows, vt)
     tail_row = 2 * n_own * vt
-    rcv, dwo = (rcv0, rcv1, rcv2), (dwo0, dwo1, dwo2)
+    rcv = (rcv0, rcv1, rcv2)
     to_sib = {"data": y, "stage": 2 * x + 1 - c}
     to_a = {"data": y_a, "stage": s}
     to_b = {"data": y_b, "stage": s}
@@ -427,31 +438,21 @@
     def row0(tile):
         half = jnp.where(tile < n_own, 1 - yh, yh)
         return pl.multiple_of((half * n_own + tile % n_own) * vt, vt)
-
-    def loads(u):
-        tile, t = _step_of(u)
-        k = u % 2
-        r = pl.ds(row0(tile), vt)
-        return (
-            pltpu.make_async_copy(z_ref.at[t, :, r, :], zb.at[k], z_sem.at[k]),
-            pltpu.make_async_copy(x_ref.at[t], xb.at[k], x_sem.at[k]),
-            pltpu.make_async_copy(w_ref.at[r, :], wb.at[k], w_sem.at[k]),
-        )
-
-    def tail_load(t):
-        return pltpu.make_async_copy(z_ref.at[t, :, pl.ds(tail_row, n_tail), :], zt, zt_sem)
-
-    for cp in loads(jnp.int32(0)):
-        cp.start()
-    w_tail = pltpu.make_async_copy(w_ref.at[pl.ds(tail_row, n_tail), :], wt, wt_sem)
-    w_tail.start()
 
     peers = (to_sib, to_a, to_b, stage_at(x_1), stage_at(x_3))
     barrier = pltpu.get_barrier_semaphore()
     for p in peers:
         pl.semaphore_signal(barrier, inc=1, device_id=p, device_id_type=MESH)
     pl.semaphore_wait(barrier, len(peers))
-    w_tail.wait()
+
+    loss_part = [jnp.sum(coef_ref[i * n_t // 2:(i + 1) * n_t // 2, 3:4, :]) for i in range(2)]
+    loss_pair = loss_part[0] + loss_part[1]
+    ls[...] = jnp.full(ls.shape, loss_pair, F32)
+
+    def send_loss():
+        return remote(ls, lr, l_sem.at[0], l_sem.at[1], to_b)
+
+    send_loss().start()
 
     def send_d(t):
         return remote(dxb.at[t, :, 1 - c], rd.at[t % 2], sd_sem.at[t], rd_sem.at[t], to_sib)
@@ -463,11 +464,11 @@
     def send_1(t, k):
         p1, _ = order(t)
         mine = p1 if k == 0 else n_x - 1 - x_1
-        return remote(dxb.at[t, mine, c], r1.at[t % N_SLOT, k], s1_sem.at[t, k], r1_sem.at[t, k], stage_at(p1))
+        return remote(dxb.at[t, mine, c], r1.at[t % SLOTS_1, k], s1_sem.at[t, k], r1_sem.at[t, k], stage_at(p1))
 
     def send_2(t):
         _, p2 = order(t)
-        return remote(dxb.at[t, p2, c], r2.at[t % N_SLOT], s2_sem.at[t], r2_sem.at[t], stage_at(p2))
+        return remote(dxb.at[t, p2, c], r2.at[t % SLOTS_2], s2_sem.at[t], r2_sem.at[t], stage_at(p2))
 
     def send_a(t):
         return remote(dxb.at[t, x, c], ra.at[t], sa_sem.at[t], ra_sem.at[t], to_a)
@@ -482,7 +483,7 @@
         @pl.when(now2)
         def _():
             send_2(t2).wait_recv()
-            dxb[t2, x, c] = dxb[t2, x, c] + r2[t2 % N_SLOT]
+            dxb[t2, x, c] = dxb[t2, x, c] + r2[t2 % SLOTS_2]
 
             @pl.when(t2 < n_t // 2)
             def _():
@@ -495,17 +496,21 @@
             _, p2 = order(t1)
             send_1(t1, 0).wait_recv()
             send_1(t1, 1).wait_recv()
-            dxb[t1, p2, c] = dxb[t1, p2, c] + r1[t1 % N_SLOT, 1]
+            dxb[t1, p2, c] = dxb[t1, p2, c] + r1[t1 % SLOTS_1, 1]
             send_2(t1).start()
-            dxb[t1, x, c] = dxb[t1, x, c] + r1[t1 % N_SLOT, 0]
+            dxb[t1, x, c] = dxb[t1, x, c] + r1[t1 % SLOTS_1, 0]
 
         now, t = scheduled(u, AFTER_D)
 
         @pl.when(now)
         def _():
             send_d(t).wait_recv()
-            for xx in range(n_x):
+
+            def add(xx, carry):
                 dxb[t, xx, c] = dxb[t, xx, c] + rd[t % 2, xx]
+                return carry
+
+            lax.fori_loop(0, n_x, add, 0)
             send_1(t, 0).start()
             send_1(t, 1).start()
 
@@ -523,89 +528,201 @@
             gi = jnp.where(sub == lab8[None], e - q8[None], e)
             g_out[:, cs] = gi.reshape(n_row, rows).astype(BF16)
 
-    def step(u, carry):
-        tile, t = _step_of(u)
-        k = u % 2
-
-        @pl.when(u < N_STEP)
-        def _():
-            for cp in loads(u):
-                cp.wait()
-
-        @pl.when(u < N_STEP - 1)
-        def _():
-            for cp in loads(u + 1):
-                cp.start()
-
-        last = jnp.logical_and(tile == 2 * n_own - 1, u < N_STEP)
-
-        @pl.when(last)
-        def _():
-            tail_load(t).start()
-
-        exchanges(u)
-
-        @pl.when(u < N_STEP)
-        def _():
-            g_tile(zb.at[k], g, t, row0(tile))
-            xk = xb[k].reshape(n_stage * rows, d)
-            dxp = lax.dot_general(g[...], wb[k], (((0,), (0,)), ((), ())), preferred_element_type=F32)
-            dxb[t] = jnp.where(tile == 0, 0.0, dxb[t]) + dxp.reshape(n_x, 2, rows, d)
-            dwb[tile] = jnp.where(t == 0, 0.0, dwb[tile]) + jnp.dot(g[...], xk, preferred_element_type=F32)
-
-        @pl.when(last)
-        def _():
-            tail_load(t).wait()
-            g_tile(zt, gt, t, tail_row)
-            xk = xb[k].reshape(n_stage * rows, d)
-            dxp = lax.dot_general(gt[...], wt[...], (((0,), (0,)), ((), ())), preferred_element_type=F32)
-            dxb[t] = dxb[t] + dxp.reshape(n_x, 2, rows, d)
-            dwt[...] = jnp.where(t == 0, 0.0, dwt[...]) + jnp.dot(gt[...], xk, preferred_element_type=F32)
-            send_d(t).start()
-
-        for j, end in enumerate((7, 23, 35)):
-            @pl.when(u == end)
-            def _(j=j):
-                send_b(j).start()
-
-        return carry
-
     def send_b(j):
         return remote(dwb.at[j], rcv[j], sb_sem.at[j], rb_sem.at[j], to_b)
 
-    lax.fori_loop(0, N_STEP, step, 0)
-
-    outs = [pltpu.make_async_copy(dwb.at[n_own + j], dwo[j], o_sem.at[j]) for j in range(n_own)]
-    outs.append(pltpu.make_async_copy(dwt, tail_o, o_sem.at[n_own]))
-    for cp in outs:
-        cp.start()
-    tail = remote(dwt, tail_r, sb_sem.at[n_own], rb_sem.at[n_own], to_b)
-    tail.start()
-
-    def drain(u, carry):
-        exchanges(u)
-        return carry
-
-    lax.fori_loop(N_STEP, DONE[-1] + AFTER_2 + 1, drain, 0)
-
-    for q in range(n_t // 2):
-        send_a(q).wait_recv()
-        gx_ref[q] = dxb[n_t // 2 + q, x, c] + ra[q]
-    for cp in outs:
-        cp.wait()
-    for j in range(n_own):
-        send_b(j).wait()
-    tail.wait()
-    for t in range(n_t):
-        send_d(t).wait_send()
-        send_1(t, 0).wait_send()
-        send_1(t, 1).wait_send()
-        send_2(t).wait_send()
-        if t < n_t // 2:
-            send_a(t).wait_send()
-
-
-def grads(lab, coef, z, x, w, vt):
+    def products(zb, xb, wb, zt, wt, g, gt):
+        def loads(u):
+            tile, t = _step_of(u)
+            k = u % 2
+            r = pl.ds(row0(tile), vt)
+            return (
+                pltpu.make_async_copy(z_ref.at[t, :, r, :], zb.at[k], z_sem.at[k]),
+                pltpu.make_async_copy(x_ref.at[t], xb.at[k], x_sem.at[k]),
+                pltpu.make_async_copy(w_ref.at[r, :], wb.at[k], w_sem.at[k]),
+            )
+
+        def tail_load(t):
+            return pltpu.make_async_copy(z_ref.at[t, :, pl.ds(tail_row, n_tail), :], zt, zt_sem)
+
+        for cp in loads(jnp.int32(0)):
+            cp.start()
+        w_tail = pltpu.make_async_copy(w_ref.at[pl.ds(tail_row, n_tail), :], wt, wt_sem)
+        w_tail.start()
+        w_tail.wait()
+
+        def step(u, carry):
+            tile, t = _step_of(u)
+            k = u % 2
+
+            @pl.when(u < N_STEP)
+            def _():
+                for cp in loads(u):
+                    cp.wait()
+
+            @pl.when(u < N_STEP - 1)
+            def _():
+                for cp in loads(u + 1):
+                    cp.start()
+
+            last = jnp.logical_and(tile == 2 * n_own - 1, u < N_STEP)
+
+            @pl.when(last)
+            def _():
+                tail_load(t).start()
+
+            exchanges(u)
+
+            @pl.when(u < N_STEP)
+            def _():
+                g_tile(zb.at[k], g, t, row0(tile))
+                xk = xb[k].reshape(n_stage * rows, d)
+                for xx in range(n_x):
+                    gx = g[:, 2 * xx * rows:2 * (xx + 1) * rows]
+                    dxp = lax.dot_general(gx, wb[k], (((0,), (0,)), ((), ())), preferred_element_type=F32)
+                    dxb[t, xx] = jnp.where(tile == 0, 0.0, dxb[t, xx]) + dxp.reshape(2, rows, d)
+                dwb[tile] = jnp.where(t == 0, 0.0, dwb[tile]) + jnp.dot(g[...], xk, preferred_element_type=F32)
+
+            @pl.when(last)
+            def _():
+                tail_load(t).wait()
+                g_tile(zt, gt, t, tail_row)
+                xk = xb[k].reshape(n_stage * rows, d)
+                dxp = lax.dot_general(gt[...], wt[...], (((0,), (0,)), ((), ())), preferred_element_type=F32)
+                dxb[t] = dxb[t] + dxp.reshape(n_x, 2, rows, d)
+                dwt[...] = jnp.where(t == 0, 0.0, dwt[...]) + jnp.dot(gt[...], xk, preferred_element_type=F32)
+                send_d(t).start()
+
+            for j, end in enumerate(SENT):
+                @pl.when(u == end)
+                def _(j=j):
+                    send_b(j).start()
+
+            return carry
+
+        lax.fori_loop(0, N_STEP, step, 0)
+
+    n_lane = n_stage * rows
+    pl.run_scoped(
+        products,
+        pltpu.VMEM((2, n_stage, vt, rows), F32),
+        pltpu.VMEM((2, n_stage, rows, d), BF16),
+        pltpu.VMEM((2, vt, d), BF16),
+        pltpu.VMEM((n_stage, n_tail, rows), F32),
+        pltpu.VMEM((n_tail, d), BF16),
+        pltpu.VMEM((vt, n_lane), BF16),
+        pltpu.VMEM((n_tail, n_lane), BF16),
+    )
+
+    def rows_of(hh, half, j, n=None):
+        n = vt if n is None else n
+        return gh_ref.at[pl.ds(pl.multiple_of(hh * first_row + (half * n_own + j) * vt, 16), n), :]
+
+    def finish(stage, fin, fint):
+        send_tail = remote(dwt, tr, sb_sem.at[n_own], rb_sem.at[n_own], to_b)
+        send_tail.start()
+
+        def fin_copy(j, way):
+            src, dst = fin.at[j], rows_of(h, yh, j)
+            if way == 0:
+                return remote(src, dst, sf_sem.at[j, 0], rf_sem.at[j, 0], to_a)
+            return remote(src, dst, sf_sem.at[j, 1], rf_sem.at[j, 1], to_b)
+
+        def fin_local(j):
+            return pltpu.make_async_copy(fin.at[j], rows_of(h, yh, j), o_sem.at[j])
+
+        def forward(j):
+            ref = rows_of(h, 1 - yh, j)
+            return remote(ref, ref, sf_sem.at[j, 2], rf_sem.at[j, 2], to_a)
+
+        def arrived(j, way):
+            ref = rows_of(1 - h, yh, j) if way == 0 else rows_of(h, 1 - yh, j) if way == 1 else rows_of(1 - h, 1 - yh, j)
+            return remote(ref, ref, sf_sem.at[j, way], rf_sem.at[j, way], to_a)
+
+        def finish_tile(j):
+            send_b(j).wait_recv()
+            cp = pltpu.make_async_copy(rcv[j], stage, st_sem)
+            cp.start()
+            cp.wait()
+
+            def add(i, carry):
+                r = pl.ds(pl.multiple_of(i * piece, piece), piece)
+                fin[j, r, :] = ((dwb[n_own + j, r, :] + stage[r, :]) * (1.0 / n_data)).astype(BF16)
+                return carry
+
+            lax.fori_loop(0, vt // piece, add, 0)
+            fin_copy(j, 0).start()
+            fin_copy(j, 1).start()
+            fin_local(j).start()
+
+        def tail_copy(hh, remote_copy):
+            n = n_tail - over * (1 - hh)
+            src, dst = fint.at[pl.ds(0, n), :], gh_ref.at[pl.ds(hh * first_row + tail_row, n), :]
+            if remote_copy:
+                return remote(src, dst, sf_sem.at[n_own, 0], rf_sem.at[n_own, 0], to_a)
+            return pltpu.make_async_copy(src, dst, o_sem.at[n_own])
+
+        def events(u, carry):
+            exchanges(u)
+            for at, what in EVENTS:
+                @pl.when(u == at)
+                def _(what=what):
+                    kind, j = what
+                    if kind == "fin":
+                        finish_tile(j)
+                    elif kind == "tail":
+                        send_tail.wait_recv()
+                        fint[...] = ((dwt[...] + tr[...]) * (1.0 / n_data)).astype(BF16)
+                        for hh in range(2):
+                            @pl.when(h == hh)
+                            def _(hh=hh):
+                                tail_copy(hh, True).start()
+                                tail_copy(hh, False).start()
+                    else:
+                        arrived(j, 1).wait_recv()
+                        forward(j).start()
+            return carry
+
+        lax.fori_loop(N_STEP, LAST_EVENT + 1, events, 0)
+
+        for q in range(n_t // 2):
+            send_a(q).wait_recv()
+            gx_ref[q] = dxb[n_t // 2 + q, x, c] + ra[q]
+        send_loss().wait()
+        loss_ref[...] = (ls[...] + lr[...]) * (1.0 / n_data)
+        for j in range(n_own):
+            send_b(j).wait_send()
+        send_tail.wait_send()
+        for t in range(n_t):
+            send_d(t).wait_send()
+            send_1(t, 0).wait_send()
+            send_1(t, 1).wait_send()
+            send_2(t).wait_send()
+            if t < n_t // 2:
+                send_a(t).wait_send()
+        for hh in range(2):
+            @pl.when(h == hh)
+            def _(hh=hh):
+                tail_copy(hh, True).wait_send()
+                tail_copy(hh, False).wait()
+                tail_copy(1 - hh, True).wait_recv()
+        for j in range(n_own):
+            fin_local(j).wait()
+            fin_copy(j, 0).wait_send()
+            fin_copy(j, 1).wait_send()
+            forward(j).wait_send()
+            arrived(j, 0).wait_recv()
+            arrived(j, 2).wait_recv()
+
+    pl.run_scoped(
+        finish,
+        pltpu.VMEM((vt, d), F32),
+        pltpu.VMEM((n_own, vt, d), BF16),
+        pltpu.VMEM((n_tail, d), BF16),
+    )
+
+
+def grads(lab, coef, z, x, w, vt, shard):
     n_t, n_stage, rows, d = x.shape
     win = w.shape[0]
     n_tail = win - N_TILE * vt
@@ -614,30 +731,29 @@
     hbm = pl.BlockSpec(memory_space=pl.ANY)
     dma = pltpu.SemaphoreType.DMA
     n_x = n_stage // 2
-    tile = jax.ShapeDtypeStruct((vt, d), F32)
-    tail = jax.ShapeDtypeStruct((n_tail, d), F32)
+    n_own = N_TILE // 2
     return pl.pallas_call(
-        functools.partial(_grads_body, n_stage=n_stage),
+        functools.partial(_grads_body, n_stage=n_stage, first_row=shard - win, over=2 * win - shard),
         in_specs=[vm, vm, hbm, hbm, hbm],
-        out_specs=[hbm] * 8 + [vm],
-        out_shape=[tile] * N_TILE + [tail] * 2 + [jax.ShapeDtypeStruct((n_t // 2, rows, d), F32)],
+        out_specs=[hbm] * 4 + [vm] * 2,
+        out_shape=[jax.ShapeDtypeStruct((shard, d), BF16)] + [jax.ShapeDtypeStruct((vt, d), F32)] * n_own + [
+            jax.ShapeDtypeStruct((n_t // 2, rows, d), F32),
+            jax.ShapeDtypeStruct((8, 128), F32),
+        ],
         scratch_shapes=[
             pltpu.VMEM((n_t, n_x, 2, rows, d), F32),
-            pltpu.VMEM((2, n_stage, rows, d), BF16),
-            pltpu.VMEM((2, n_stage, vt, rows), F32),
-            pltpu.VMEM((2, vt, d), BF16),
-            pltpu.VMEM((n_stage, n_tail, rows), F32),
-            pltpu.VMEM((n_tail, d), BF16),
-            pltpu.VMEM((vt, n), BF16),
-            pltpu.VMEM((n_tail, n), BF16),
             pltpu.VMEM((N_TILE, vt, d), F32),
             pltpu.VMEM((n_tail, d), F32),
+            pltpu.VMEM((n_tail, d), F32),
             pltpu.VMEM((2, n_x, rows, d), F32),
-            pltpu.VMEM((N_SLOT, 2, rows, d), F32),
-            pltpu.VMEM((N_SLOT, rows, d), F32),
+            pltpu.VMEM((SLOTS_1, 2, rows, d), F32),
+            pltpu.VMEM((SLOTS_2, rows, d), F32),
             pltpu.VMEM((n_t // 2, rows, d), F32),
+            pltpu.VMEM((8, 128), F32),
+            pltpu.VMEM((8, 128), F32),
             dma((2,)), dma((2,)), dma((2,)), dma, dma, dma((4,)), dma((4,)), dma((4,)),
             dma((n_t,)), dma((n_t,)), dma((n_t, 2)), dma((n_t, 2)), dma((n_t,)), dma((n_t,)), dma((n_t // 2,)), dma((n_t // 2,)),
+            dma((4, 3)), dma((4, 3)), dma, dma((2,)),
         ],
         compiler_params=pltpu.CompilerParams(vmem_limit_bytes=67043328, collective_id=1, has_side_effects=True),
         cost_estimate=_cost(4 * n_t * n * d * win, 4 * n_t * n * win, n_t * n * win),
@@ -652,11 +768,10 @@
     vocab_spec = P("stage", None)
     layer_spec = P("stage", None, None)
     swap_a = [(i, i ^ 1) for i in range(n_data)]
-    swap_b = [(i, n_data - 1 - i) for i in range(n_data)]
 
     def local_step(x_rows, w_head, labels, loss_mask, w_embed, tok_ids, act_in, w_up, w_down):
         y, s = lax.axis_index("data"), lax.axis_index("stage")
-        shard, d = w_head.shape
+        shard, _ = w_head.shape
         yh = y >> 1
         h = (y ^ yh) & 1
         step_rows = 16 * N_TILE
@@ -668,9 +783,6 @@
         def over_a(v):
             return lax.ppermute(v, "data", swap_a)
 
-        def over_b(v):
-            return lax.ppermute(v, "data", swap_b)
-
         lab_a = over_a(labels)
 
         def local(lab):
@@ -682,13 +794,9 @@
         z, x_all, w_win, coef = head(x_rows, w_head, lab_two.reshape(2, 1, n_tok), loss_mask.reshape(1, -1), n_stage, win, logits_tile(win))
         n_t, _, rows, _ = x_all.shape
         lab = lab_two[::-1].reshape(2, n_stage, n_t // 2, rows).transpose(0, 2, 1, 3).reshape(n_t, 1, n_stage * rows)
-        *parts, tail, tail_far, gx = grads(lab, coef, z, x_all, w_win, vt)
+        grad_head, _, _, _, gx, loss = grads(lab, coef, z, x_all, w_win, vt, shard)
         grad_x = gx.reshape(x_rows.shape)
-
-        loss_t = jnp.sum(coef[:, 3, :], axis=1).reshape(2, n_t // 2).sum(axis=1)
-        loss_pair = loss_t[0] + loss_t[1]
-        loss_far = over_b(loss_pair.reshape(1, 1))[0, 0]
-        mean_loss = (loss_pair + loss_far) / n_data
+        mean_loss = loss[0, 0]
 
         offset = s * shard
         local_ids = tok_ids - offset
@@ -698,32 +806,7 @@
         emb_part, _ = lax.optimization_barrier((emb_part, coef))
         embed_out = lax.psum_scatter(emb_part, "stage", scatter_dimension=0, tiled=True)
 
-        half = N_TILE // 2
-        kept, got = parts[:half], parts[half:]
-        fins, fas, fbs = [], [], []
-        for j in range(half):
-            fins.append(lax.optimization_barrier(((kept[j] + got[j]) / n_data).astype(BF16)))
-            fbs.append(over_b(fins[j]))
-            fas.append(over_a(fins[j]))
-        fin_t = lax.optimization_barrier(((tail + tail_far) / n_data).astype(BF16))
-        fin_ta = over_a(fin_t)
-
-        mlp_out, done = None, 0
-        blocks = n_tok // 512
-        for part in MLP_EIGHTHS:
-            mlp_out = mlp(act_in, w_up[0], w_down[0], mlp_out, done, blocks * part // 8)
-            done += blocks * part // 8
-
-        grad_head = jnp.zeros((shard, d), BF16)
-        for j in range(half):
-            fin_ab = over_a(fbs[j])
-            for v, hh, part in ((fins[j], h, yh), (fas[j], 1 - h, yh), (fbs[j], h, 1 - yh), (fin_ab, 1 - h, 1 - yh)):
-                row = hh * first_row + (part * half + j) * vt
-                grad_head = lax.dynamic_update_slice(grad_head, v, (row, 0))
-        lower = jnp.where(h == 0, fin_t, fin_ta)
-        upper = jnp.where(h == 0, fin_ta, fin_t)
-        grad_head = lax.dynamic_update_slice(grad_head, lower[: fin_t.shape[0] - over], (N_TILE * vt, 0))
-        grad_head = lax.dynamic_update_slice(grad_head, upper, (first_row + N_TILE * vt, 0))
+        mlp_out = mlp(act_in, w_up[0], w_down[0], None, 0, n_tok // 512)
 
         return mean_loss.reshape(1), grad_x, grad_head, embed_out, mlp_out
 

time: 507 us -> 440 us (0.87)
  waiting for transfers between devices: 47.7 us -> 0.06 us
  Pallas kernels: 335 us -> 374 us
  starting transfers between devices: 35.8 us -> 2.82 us
  local copies, waits for them, and re-layouts: 49.3 us -> 38.1 us
  other arithmetic: 19.4 us -> 9.45 us
    pallas_call x1, Pallas kernels: 190 us -> 243 us  [grads(): pl.pallas_call(functools.partial(_grads_body, n_stage=n_stage, first_row=...]
    ppermute x8 -> x1, waiting for transfers between devices: 44.3 us -> 0.01 us  [over_a(): return lax.ppermute(v, 'data', swap_a)]
    ppermute x4 -> x0, starting transfers between devices: 29.6 us -> none  [over_b(): return lax.ppermute(v, 'data', swap_b)]
    dynamic_update_slice x12 -> x0, local copies, waits for them, and re-layouts: 16.9 us -> none  [local_step(): grad_head = lax.dynamic_update_slice(grad_head, v, (row, 0))]
    pallas_call x3 -> x1, Pallas kernels: 57.1 us -> 47.2 us  [mlp(): pl.pallas_call(functools.partial(_mlp_body, chunk=512), grid=(count,), in...]
    unnamed x5 -> x4, local copies, waits for them, and re-layouts: 1.15 us -> 10.8 us
    convert_element_type x4 -> x0, other arithmetic: 7.33 us -> none  [the longest x3 6.25 us: local_step(): ((kept[j] + got[j]) / n_data).astype(BF16)]
  transfers between devices with their start and end apart: 13 -> 2, of which waited for: 3 -> 0; matrix products, arithmetic and copies ran while one was open for 13% -> 8% of each run, Pallas kernels for 49% -> 66%
where the time goes in v4:
time: 440 us; the launch traced here: 439 us
  Pallas kernels  374 us (85%)
  local copies, waits for them, and re-layouts  38.1 us (9%)
  between operations  14.1 us (3%)
  other arithmetic  9.45 us (2%)
    pallas_call x1, Pallas kernels, grads(): pl.pallas_call(functools.partial(_grads_body, n_stage=n_stage, first_row=...  243 us
    pallas_call x1, Pallas kernels, head(): pl.pallas_call(functools.partial(_head_body, n_stage=n_stage, first_row=s...  84.4 us
    pallas_call x1, Pallas kernels, mlp(): pl.pallas_call(functools.partial(_mlp_body, chunk=512), grid=(count,), in...  47.2 us
    gather x1, local copies, waits for them, and re-layouts, local_step(): rows_emb = jnp.take(w_embed, jnp.clip(local_ids, 0, shard - 1), axis=0)  24 us
    unnamed x4, local copies, waits for them, and re-layouts  10.8 us
  transfers between devices with their start and end apart: 2, of which 0 were waited for; matrix products, arithmetic and copies ran while one was open for 8% of the time, Pallas kernels for 66%

profile of v4, /device:TPU:97, one launch (start us, length us, event | category | flops | bytes accessed | tf_op | source)
XLA Modules:
  0.0 438.7 jit_solution(11479086619464531091)
XLA Ops:
  7.2 0.1 reduce-scatter.2.cloned.1.call-start
  7.2 2.8 collective-permute-start
  10.0 0.7 compare_and_fusion.1
  10.7 0.7 fusion
  11.5 24.0 %gather_fusion = bf16[4096,768]{1,0:T(8,128)(2,1)} fusion(bf16[6288,768]{1,0:T(8,128)(2,1)} %param.13, s32[4096]{0:T(1024)S(1)} %fusion), kind=kCustom, calls=%fused_computation | custom fusion | bytes 12599296 | tf_op jit(solution)/shard_map/jit(_take)/gather | solution.py:804
  35.5 0.0 copy-start
  35.5 7.9 %select_select_fusion = bf16[4096,768]{1,0:T(8,128)(2,1)} fusion(bf16[4096,768]{1,0:T(8,128)(2,1)} %gather_fusion, pred[4096]{0:T(1024)(128)(4,1)S(1)} %get-tuple-element.22, pred[4096]{0:T(1024)(128)(4,1)S(1)} %get-tuple-element.21), kind=kLoop, calls=%fused_computation.1 | loop fusion | flops 6291456 | bytes 12591104 | tf_op jit(solution)/shard_map/jit(_where)/select_n | solution.py:805
  43.5 0.0 copy-done
  43.5 0.0 collective-permute-done
  43.6 0.6 reshape.37.lab_ref
  44.2 84.4 %head.1 = (f32[8,8,3168,128]{3,2,1,0:T(8,128)}, bf16[8,8,128,768]{3,2,1,0:T(8,128)(2,1)}, bf16[3168,768]{1,0:T(8,128)(2,1)}, f32[8,8,1024]{2,1,0:T(8,128)}) custom-call(bf16[4,128,768]{2,1,0:T(8,128)(2,1)} %bitcast.17, bf16[6288,768]{1,0:T(8,128)(2,1)} %wh_ref.1, s32[2,1,4096]{2,1,0:T(1,128)} %reshape.37.lab_ref, s32[1,4096]{1,0:T(1,128)} %bitcast.18), custom_call_target="tpu_custom_call" | custom-call | flops 39862665216 | bytes 103809024 | tf_op jit(solution)/shard_map/head/pallas_call | solution.py:345
  128.6 0.1 reduce-scatter.2.cloned.1.call-update
  128.6 47.2 %mlp.1 = bf16[4096,768]{1,0:T(8,128)(2,1)} custom-call(bf16[4096,768]{1,0:T(8,128)(2,1)} %a_ref.1, bf16[768,3072]{1,0:T(8,128)(2,1)} %bitcast.15, bf16[3072,768]{1,0:T(8,128)(2,1)} %bitcast.16), custom_call_target="tpu_custom_call" | custom-call | flops 38654705664 | bytes 22020096 | tf_op jit(solution)/shard_map/mlp/pallas_call | solution.py:46
  175.8 0.8 rev.3
  176.6 0.6 copy.14
  177.3 242.6 %grads.1 = (bf16[6288,768]{1,0:T(8,128)(2,1)}, f32[512,768]{1,0:T(8,128)}, f32[512,768]{1,0:T(8,128)}, f32[512,768]{1,0:T(8,128)}, f32[4,128,768]{2,1,0:T(8,128)}, /*index=5*/f32[8,128]{1,0:T(8,128)}) custom-call(s32[8,1,1024]{2,1,0:T(1,128)} %bitcast.14, f32[8,8,1024]{2,1,0:T(8,128)} %get-tuple-element.13.coef_ref, ...), custom_call_target="tpu_custom_call" | custom-call | flops 79725330432 | bytes 103809024 | tf_op jit(solution)/shard_map/grads/pallas_call | solution.py:735
  419.9 1.2 slice.3
  421.0 0.0 reduce-scatter.2.cloned.1.call-done
  421.0 2.7 copy.17
  423.7 8.2 %copy.18 = bf16[6288,768]{1,0:T(8,128)(2,1)} copy(bf16[6288,768]{1,0:T(8,128)(2,1)} %get-tuple-element.30) | data formatting | bytes 19316736
  (4 shorter events, 0.1 us)
Async XLA Ops:
  7.2 413.9 %reduce-scatter.2.cloned.1.call-start = ((), (), s32[]{:S(2)}) async-start(), calls=%async_computation.1 | async-start | bytes 7077888 | tf_op jit(solution)/shard_map/reduce_scatter | solution.py:807
  7.2 36.2 %collective-permute-start = (s32[4096]{0:T(1024)}, s32[4096]{0:T(1024)S(1)}, u32[]{:S(2)}, u32[]{:S(2)}) collective-permute-start(s32[4096]{0:T(1024)} %param.11), channel_id=1, source_target_pairs={{0,8},{8,0},{16,24},{24,16},{1,9},{9,1},{17,25},{25,17},{2,10},{10... | collective-permute-start | bytes 49160 | tf_op jit(solution)/shard_map/ppermute | solution.py:784
  35.5 8.0 %copy-start = (s32[4096]{0:T(1024)S(1)}, s32[4096]{0:T(1024)}, u32[]{:S(2)}) copy-start(s32[4096]{0:T(1024)} %param.11) | copy-start | bytes 49156
Sparse Core Ops, SparseCore 0:
  128.7 39.8 reduce-scatter.1

commit v5 on v4

--- a/solution.py
+++ b/solution.py
@@ -26,39 +26,6 @@
 
 def _cost(flops, nbytes, trans=0):
     return pl.CostEstimate(flops=int(flops), bytes_accessed=int(nbytes), transcendentals=int(trans))
-
-
-def _mlp_body(a_ref, w1_ref, w2_ref, *rest, chunk):
-    o_ref, u_ref = rest[-2:]
-    ff = w1_ref.shape[1]
-    for c in range(ff // chunk):
-        cs = slice(c * chunk, (c + 1) * chunk)
-        h = jnp.dot(a_ref[...], w1_ref[:, cs], preferred_element_type=F32)
-        u_ref[:, cs] = jax.nn.gelu(h).astype(BF16)
-    y = jnp.dot(u_ref[...], w2_ref[...], preferred_element_type=F32)
-    o_ref[...] = (a_ref[...].astype(F32) + y).astype(BF16)
-
-
-def mlp(a, w1, w2, out, first, count, tb=512):
-    n, d = a.shape
-    ff = w1.shape[1]
-    extra = [] if out is None else [out]
-    return pl.pallas_call(
-        functools.partial(_mlp_body, chunk=512),
-        grid=(count,),
-        in_specs=[
-            pl.BlockSpec((tb, d), lambda i: (first + i, 0)),
-            pl.BlockSpec((d, ff), lambda i: (0, 0)),
-            pl.BlockSpec((ff, d), lambda i: (0, 0)),
-        ] + [pl.BlockSpec(memory_space=pl.ANY)] * len(extra),
-        out_specs=pl.BlockSpec((tb, d), lambda i: (first + i, 0)),
-        out_shape=jax.ShapeDtypeStruct((n, d), BF16),
-        scratch_shapes=[pltpu.VMEM((tb, ff), BF16)],
-        input_output_aliases={3: 0} if extra else {},
-        compiler_params=_params(),
-        cost_estimate=_cost(4 * count * tb * d * ff, 4 * count * tb * d + 4 * d * ff, count * tb * ff),
-        name="mlp",
-    )(a, w1, w2, *extra)
 
 
 def _logits_block(z_ref, x, w_ref, lab, end, vt):
@@ -376,35 +343,39 @@
 SLOTS_1, SLOTS_2 = 6, 4
 
 
+PHASES = ((0, 1, 0, 0), (8, 5, 1, 0), (18, 1, 1, 2), (24, 4, 2, 2), (36, 1, 2, 5), (39, 3, 3, 5))
 EVENTS = (
-    (48, ("fin", 0)), (49, ("fin", 1)), (51, ("tail", 0)), (54, ("fin", 2)),
-    (62, ("pass", 0)), (66, ("pass", 1)), (67, ("pass", 2)),
+    (48, "2", 3), (48, "fin", 0), (49, "fin", 1), (53, "d", 7), (54, "tail", 0), (59, "2", 4), (60, "1", 5), (65, "fin", 2), (67, "1", 6), (70, "pass", 0),
+    (73, "2", 5), (75, "1", 7), (80, "2", 6), (83, "pass", 1), (87, "2", 7), (98, "pass", 2),
 )
-LAST_EVENT = 67
+MLP_FROM = 50
+MLP_CHUNK = 512
 
 
 def _step_of(u):
-    phases = (
-        (0, 1, 0, 0),
-        (8, 5, 1, 0),
-        (18, 1, 1, 2),
-        (24, 4, 2, 2),
-        (36, 1, 2, 5),
-        (39, 3, 3, 5),
-    )
-    tile = group = jnp.int32(0)
-    for start, n_tile, tile0, group0 in phases:
+    tile = group = xi = wi = jnp.int32(0)
+    new_x = new_w = False
+    x_base = w_base = 0
+    ends = [p[0] for p in PHASES[1:]] + [N_STEP]
+    for (start, n_tile, tile0, group0), end in zip(PHASES, ends):
         k = jnp.maximum(u - start, 0)
-        tile = jnp.where(u >= start, tile0 + k % n_tile, tile)
-        group = jnp.where(u >= start, group0 + k // n_tile, group)
-    return tile, group
+        on = u >= start
+        tile = jnp.where(on, tile0 + k % n_tile, tile)
+        group = jnp.where(on, group0 + k // n_tile, group)
+        xi = jnp.where(on, x_base + k // n_tile, xi)
+        wi = jnp.where(on, w_base + (k if n_tile > 1 else 0), wi)
+        new_x = jnp.where(on, k % n_tile == 0, new_x)
+        new_w = jnp.where(on, True if n_tile > 1 else k == 0, new_w)
+        x_base += (end - start) // n_tile
+        w_base += end - start if n_tile > 1 else 1
+    return tile, group, xi % 2, wi % 2, new_x, new_w
 
 
 def _grads_body(
-    lab_ref, coef_ref, z_ref, x_ref, w_ref, gh_ref, rcv0, rcv1, rcv2, gx_ref, loss_ref,
+    lab_ref, coef_ref, z_ref, x_ref, w_ref, a_ref, w1_ref, w2_ref, gh_ref, mo_ref, rcv0, rcv1, rcv2, gx_ref, loss_ref,
     dxb, dwb, dwt, tr, rd, r1, r2, ra, ls, lr,
     z_sem, x_sem, w_sem, zt_sem, wt_sem, o_sem, sb_sem, rb_sem, sd_sem, rd_sem, s1_sem, r1_sem, s2_sem, r2_sem, sa_sem, ra_sem,
-    sf_sem, rf_sem, st_sem, l_sem,
+    sf_sem, rf_sem, st_sem, l_sem, ai_sem, ao_sem, mw_sem,
     *, n_stage, first_row, over,
 ):
     y, s = lax.axis_index("data"), lax.axis_index("stage")
@@ -473,46 +444,41 @@
     def send_a(t):
         return remote(dxb.at[t, x, c], ra.at[t], sa_sem.at[t], ra_sem.at[t], to_a)
 
-    def scheduled(u, after):
-        t = sum(jnp.where(u == done + after, i, 0) for i, done in enumerate(DONE))
-        return functools.reduce(jnp.logical_or, [u == done + after for done in DONE]), t
+    def exchange_d(t):
+        send_d(t).wait_recv()
+
+        def add(xx, carry):
+            dxb[t, xx, c] = dxb[t, xx, c] + rd[t % 2, xx]
+            return carry
+
+        lax.fori_loop(0, n_x, add, 0)
+        send_1(t, 0).start()
+        send_1(t, 1).start()
+
+    def exchange_1(t):
+        _, p2 = order(t)
+        send_1(t, 0).wait_recv()
+        send_1(t, 1).wait_recv()
+        dxb[t, p2, c] = dxb[t, p2, c] + r1[t % SLOTS_1, 1]
+        send_2(t).start()
+        dxb[t, x, c] = dxb[t, x, c] + r1[t % SLOTS_1, 0]
+
+    def exchange_2(t):
+        send_2(t).wait_recv()
+        dxb[t, x, c] = dxb[t, x, c] + r2[t % SLOTS_2]
+
+        @pl.when(t < n_t // 2)
+        def _():
+            send_a(t).start()
 
     def exchanges(u):
-        now2, t2 = scheduled(u, AFTER_2)
-
-        @pl.when(now2)
-        def _():
-            send_2(t2).wait_recv()
-            dxb[t2, x, c] = dxb[t2, x, c] + r2[t2 % SLOTS_2]
-
-            @pl.when(t2 < n_t // 2)
-            def _():
-                send_a(t2).start()
-
-        now1, t1 = scheduled(u, AFTER_1)
-
-        @pl.when(now1)
-        def _():
-            _, p2 = order(t1)
-            send_1(t1, 0).wait_recv()
-            send_1(t1, 1).wait_recv()
-            dxb[t1, p2, c] = dxb[t1, p2, c] + r1[t1 % SLOTS_1, 1]
-            send_2(t1).start()
-            dxb[t1, x, c] = dxb[t1, x, c] + r1[t1 % SLOTS_1, 0]
-
-        now, t = scheduled(u, AFTER_D)
-
-        @pl.when(now)
-        def _():
-            send_d(t).wait_recv()
-
-            def add(xx, carry):
-                dxb[t, xx, c] = dxb[t, xx, c] + rd[t % 2, xx]
-                return carry
-
-            lax.fori_loop(0, n_x, add, 0)
-            send_1(t, 0).start()
-            send_1(t, 1).start()
+        for after, run in ((AFTER_2, exchange_2), (AFTER_1, exchange_1), (AFTER_D, exchange_d)):
+            done = [d for d in DONE if d + after < N_STEP]
+            t = sum(jnp.where(u == d + after, i, 0) for i, d in enumerate(done))
+
+            @pl.when(functools.reduce(jnp.logical_or, [u == d + after for d in done]))
+            def _(run=run, t=t):
+                run(t)
 
     def g_tile(z, g_out, t, base):
         n_row = z.shape[1]
@@ -532,65 +498,84 @@
         return remote(dwb.at[j], rcv[j], sb_sem.at[j], rb_sem.at[j], to_b)
 
     def products(zb, xb, wb, zt, wt, g, gt):
-        def loads(u):
-            tile, t = _step_of(u)
-            k = u % 2
-            r = pl.ds(row0(tile), vt)
+        def whole(u):
+            tile, t, xk, wk, new_x, new_w = _step_of(u)
             return (
-                pltpu.make_async_copy(z_ref.at[t, :, r, :], zb.at[k], z_sem.at[k]),
-                pltpu.make_async_copy(x_ref.at[t], xb.at[k], x_sem.at[k]),
-                pltpu.make_async_copy(w_ref.at[r, :], wb.at[k], w_sem.at[k]),
+                pltpu.make_async_copy(z_ref.at[t, :, pl.ds(row0(tile), vt), :], zb.at[u % 2], z_sem.at[u % 2]),
+                pltpu.make_async_copy(x_ref.at[t], xb.at[xk], x_sem.at[xk]),
+                pltpu.make_async_copy(w_ref.at[pl.ds(row0(tile), vt), :], wb.at[wk], w_sem.at[wk]),
+                new_x, new_w,
             )
+
+        def load(u):
+            tile, t, xk, wk, new_x, new_w = _step_of(u)
+            r0 = row0(tile)
+            for i in range(n_stage):
+                pltpu.make_async_copy(z_ref.at[t, i, pl.ds(r0, vt), :], zb.at[u % 2, i], z_sem.at[u % 2]).start()
+
+            @pl.when(new_x)
+            def _():
+                for i in range(0, n_stage, 2):
+                    part = pl.ds(i, 2)
+                    pltpu.make_async_copy(x_ref.at[t, part], xb.at[xk, part], x_sem.at[xk]).start()
+
+            @pl.when(new_w)
+            def _():
+                for i in range(2):
+                    src, dst = pl.ds(r0 + i * vt // 2, vt // 2), pl.ds(i * vt // 2, vt // 2)
+                    pltpu.make_async_copy(w_ref.at[src, :], wb.at[wk, dst, :], w_sem.at[wk]).start()
+
+        def arrive(u):
+            z_in, x_in, w_in, new_x, new_w = whole(u)
+            z_in.wait()
+
+            @pl.when(new_x)
+            def _():
+                x_in.wait()
+
+            @pl.when(new_w)
+            def _():
+                w_in.wait()
 
         def tail_load(t):
             return pltpu.make_async_copy(z_ref.at[t, :, pl.ds(tail_row, n_tail), :], zt, zt_sem)
 
-        for cp in loads(jnp.int32(0)):
-            cp.start()
+        load(jnp.int32(0))
         w_tail = pltpu.make_async_copy(w_ref.at[pl.ds(tail_row, n_tail), :], wt, wt_sem)
         w_tail.start()
         w_tail.wait()
 
         def step(u, carry):
-            tile, t = _step_of(u)
-            k = u % 2
-
-            @pl.when(u < N_STEP)
-            def _():
-                for cp in loads(u):
-                    cp.wait()
+            tile, t, xk, wk, _, _ = _step_of(u)
+            arrive(u)
 
             @pl.when(u < N_STEP - 1)
             def _():
-                for cp in loads(u + 1):
-                    cp.start()
-
-            last = jnp.logical_and(tile == 2 * n_own - 1, u < N_STEP)
+                load(u + 1)
+
+            last = tile == 2 * n_own - 1
 
             @pl.when(last)
             def _():
                 tail_load(t).start()
 
             exchanges(u)
-
-            @pl.when(u < N_STEP)
-            def _():
-                g_tile(zb.at[k], g, t, row0(tile))
-                xk = xb[k].reshape(n_stage * rows, d)
-                for xx in range(n_x):
-                    gx = g[:, 2 * xx * rows:2 * (xx + 1) * rows]
-                    dxp = lax.dot_general(gx, wb[k], (((0,), (0,)), ((), ())), preferred_element_type=F32)
-                    dxb[t, xx] = jnp.where(tile == 0, 0.0, dxb[t, xx]) + dxp.reshape(2, rows, d)
-                dwb[tile] = jnp.where(t == 0, 0.0, dwb[tile]) + jnp.dot(g[...], xk, preferred_element_type=F32)
+            g_tile(zb.at[u % 2], g, t, row0(tile))
+            x_t = xb[xk].reshape(n_stage * rows, d)
+            for xx in range(n_x):
+                gx = g[:, 2 * xx * rows:2 * (xx + 1) * rows]
+                dxp = lax.dot_general(gx, wb[wk], (((0,), (0,)), ((), ())), preferred_element_type=F32)
+                dxb[t, xx] = jnp.where(tile == 0, 0.0, dxb[t, xx]) + dxp.reshape(2, rows, d)
+            dwb[tile] = jnp.where(t == 0, 0.0, dwb[tile]) + jnp.dot(g[...], x_t, preferred_element_type=F32)
 
             @pl.when(last)
             def _():
                 tail_load(t).wait()
                 g_tile(zt, gt, t, tail_row)
-                xk = xb[k].reshape(n_stage * rows, d)
+                x_t = xb[xk].reshape(n_stage * rows, d)
                 dxp = lax.dot_general(gt[...], wt[...], (((0,), (0,)), ((), ())), preferred_element_type=F32)
                 dxb[t] = dxb[t] + dxp.reshape(n_x, 2, rows, d)
-                dwt[...] = jnp.where(t == 0, 0.0, dwt[...]) + jnp.dot(gt[...], xk, preferred_element_type=F32)
+                dwt[...] = jnp.where(t == 0, 0.0, dwt[...]) + jnp.dot(gt[...], x_t, preferred_element_type=F32)
                 send_d(t).start()
 
             for j, end in enumerate(SENT):
@@ -618,7 +603,7 @@
         n = vt if n is None else n
         return gh_ref.at[pl.ds(pl.multiple_of(hh * first_row + (half * n_own + j) * vt, 16), n), :]
 
-    def finish(stage, fin, fint):
+    def finish(stage, fin, fint, w1, w2, act, ub):
         send_tail = remote(dwt, tr, sb_sem.at[n_own], rb_sem.at[n_own], to_b)
         send_tail.start()
 
@@ -632,12 +617,78 @@
             return pltpu.make_async_copy(fin.at[j], rows_of(h, yh, j), o_sem.at[j])
 
         def forward(j):
-            ref = rows_of(h, 1 - yh, j)
-            return remote(ref, ref, sf_sem.at[j, 2], rf_sem.at[j, 2], to_a)
+            ref = rows_of(1 - h, yh, j) if j == 0 else rows_of(h, 1 - yh, j)
+            return remote(ref, ref, sf_sem.at[j, 2], rf_sem.at[j, 2], to_b if j == 0 else to_a)
 
         def arrived(j, way):
             ref = rows_of(1 - h, yh, j) if way == 0 else rows_of(h, 1 - yh, j) if way == 1 else rows_of(1 - h, 1 - yh, j)
             return remote(ref, ref, sf_sem.at[j, way], rf_sem.at[j, way], to_a)
+
+        n_rows, ff = act.shape[1], w1_ref.shape[1]
+        n_block, n_chunk = a_ref.shape[0] // n_rows, ff // MLP_CHUNK
+        n_mlp = n_block * n_chunk
+        per_group = n_x * 2 * rows // n_rows
+
+        def act_in(m):
+            r = pl.ds(pl.multiple_of((m % n_block) * n_rows, n_rows), n_rows)
+            return pltpu.make_async_copy(a_ref.at[r, :], act.at[m % 2], ai_sem.at[m % 2])
+
+        def act_out(m):
+            r = pl.ds(pl.multiple_of((m % n_block) * n_rows, n_rows), n_rows)
+            return pltpu.make_async_copy(act.at[m % 2], mo_ref.at[r, :], ao_sem.at[m % 2])
+
+        def weights(chunk):
+            part = pl.ds(pl.multiple_of(chunk * MLP_CHUNK, MLP_CHUNK), MLP_CHUNK)
+            k = chunk % 2
+            return (
+                pltpu.make_async_copy(w1_ref.at[:, part], w1.at[k], mw_sem.at[k, 0]),
+                pltpu.make_async_copy(w2_ref.at[part, :], w2.at[k], mw_sem.at[k, 1]),
+            )
+
+        def mlp_step(m):
+            chunk, block = m // n_block, m % n_block
+            k = m % 2
+
+            @pl.when(block == 0)
+            def _():
+                for cp in weights(chunk):
+                    cp.wait()
+
+                @pl.when(chunk + 1 < n_chunk)
+                def _():
+                    for cp in weights(chunk + 1):
+                        cp.start()
+
+            act_in(m).wait()
+
+            @pl.when(m + 1 < n_mlp)
+            def _():
+                @pl.when(m - 1 >= n_mlp - n_block)
+                def _():
+                    act_out(m - 1).wait()
+
+                act_in(m + 1).start()
+
+            hid = jnp.dot(act[k], w1[chunk % 2], preferred_element_type=F32)
+            ub[...] = jax.nn.gelu(hid).astype(BF16)
+            out = jnp.dot(ub[...], w2[chunk % 2], preferred_element_type=F32)
+            group, part = block // per_group, block % per_group
+            per = n_rows // (2 * rows)
+            xs = pl.ds(part * per, per)
+            total = jnp.where(chunk == 0, 0.0, dxb[group, xs]) + out.reshape(per, 2, rows, d)
+
+            @pl.when(chunk < n_chunk - 1)
+            def _():
+                dxb[group, xs] = total
+
+            @pl.when(chunk == n_chunk - 1)
+            def _():
+                act[k] = (act[k].astype(F32) + total.reshape(n_rows, d)).astype(BF16)
+                act_out(m).start()
+
+        for cp in weights(jnp.int32(0)):
+            cp.start()
+        act_in(jnp.int32(0)).start()
 
         def finish_tile(j):
             send_b(j).wait_recv()
@@ -662,28 +713,51 @@
                 return remote(src, dst, sf_sem.at[n_own, 0], rf_sem.at[n_own, 0], to_a)
             return pltpu.make_async_copy(src, dst, o_sem.at[n_own])
 
-        def events(u, carry):
-            exchanges(u)
-            for at, what in EVENTS:
+        def event(what, j):
+            if what == "fin":
+                finish_tile(j)
+            elif what == "d":
+                exchange_d(j)
+            elif what == "1":
+                exchange_1(j)
+            elif what == "2":
+                exchange_2(j)
+            elif what == "tail":
+                send_tail.wait_recv()
+                fint[...] = ((dwt[...] + tr[...]) * (1.0 / n_data)).astype(BF16)
+                for hh in range(2):
+                    @pl.when(h == hh)
+                    def _(hh=hh):
+                        tail_copy(hh, True).start()
+                        tail_copy(hh, False).start()
+            else:
+                arrived(j, 0 if j == 0 else 1).wait_recv()
+                forward(j).start()
+
+        def after(u, carry):
+            for at, what, j in EVENTS:
                 @pl.when(u == at)
-                def _(what=what):
-                    kind, j = what
-                    if kind == "fin":
-                        finish_tile(j)
-                    elif kind == "tail":
-                        send_tail.wait_recv()
-                        fint[...] = ((dwt[...] + tr[...]) * (1.0 / n_data)).astype(BF16)
-                        for hh in range(2):
-                            @pl.when(h == hh)
-                            def _(hh=hh):
-                                tail_copy(hh, True).start()
-                                tail_copy(hh, False).start()
-                    else:
-                        arrived(j, 1).wait_recv()
-                        forward(j).start()
+                def _(what=what, j=j):
+                    event(what, j)
+
+            for t in range(n_t // 2):
+                @pl.when(u == MLP_FROM + t * per_group)
+                def _(t=t):
+                    send_d(t).wait_send()
+                    send_1(t, 0).wait_send()
+                    send_1(t, 1).wait_send()
+                    send_2(t).wait_send()
+                    send_a(t).wait_send()
+
+            @pl.when(jnp.logical_and(u >= MLP_FROM, u < MLP_FROM + n_mlp))
+            def _():
+                mlp_step(u - MLP_FROM)
+
             return carry
 
-        lax.fori_loop(N_STEP, LAST_EVENT + 1, events, 0)
+        lax.fori_loop(N_STEP, max(MLP_FROM + n_mlp, EVENTS[-1][0] + 1), after, 0)
+        act_out(jnp.int32(n_mlp - 2)).wait()
+        act_out(jnp.int32(n_mlp - 1)).wait()
 
         for q in range(n_t // 2):
             send_a(q).wait_recv()
@@ -693,13 +767,11 @@
         for j in range(n_own):
             send_b(j).wait_send()
         send_tail.wait_send()
-        for t in range(n_t):
+        for t in range(n_t // 2, n_t):
             send_d(t).wait_send()
             send_1(t, 0).wait_send()
             send_1(t, 1).wait_send()
             send_2(t).wait_send()
-            if t < n_t // 2:
-                send_a(t).wait_send()
         for hh in range(2):
             @pl.when(h == hh)
             def _(hh=hh):
@@ -711,7 +783,7 @@
             fin_copy(j, 0).wait_send()
             fin_copy(j, 1).wait_send()
             forward(j).wait_send()
-            arrived(j, 0).wait_recv()
+            arrived(j, 1 if j == 0 else 0).wait_recv()
             arrived(j, 2).wait_recv()
 
     pl.run_scoped(
@@ -719,10 +791,14 @@
         pltpu.VMEM((vt, d), F32),
         pltpu.VMEM((n_own, vt, d), BF16),
         pltpu.VMEM((n_tail, d), BF16),
+        pltpu.VMEM((2, d, MLP_CHUNK), BF16),
+        pltpu.VMEM((2, MLP_CHUNK, d), BF16),
+        pltpu.VMEM((2, min(512, n_lane), d), BF16),
+        pltpu.VMEM((min(512, n_lane), MLP_CHUNK), BF16),
     )
 
 
-def grads(lab, coef, z, x, w, vt, shard):
+def grads(lab, coef, z, x, w, vt, shard, act, w1, w2):
     n_t, n_stage, rows, d = x.shape
     win = w.shape[0]
     n_tail = win - N_TILE * vt
@@ -734,9 +810,9 @@
     n_own = N_TILE // 2
     return pl.pallas_call(
         functools.partial(_grads_body, n_stage=n_stage, first_row=shard - win, over=2 * win - shard),
-        in_specs=[vm, vm, hbm, hbm, hbm],
-        out_specs=[hbm] * 4 + [vm] * 2,
-        out_shape=[jax.ShapeDtypeStruct((shard, d), BF16)] + [jax.ShapeDtypeStruct((vt, d), F32)] * n_own + [
+        in_specs=[vm, vm] + [hbm] * 6,
+        out_specs=[hbm] * 5 + [vm] * 2,
+        out_shape=[jax.ShapeDtypeStruct((shard, d), BF16), jax.ShapeDtypeStruct(act.shape, BF16)] + [jax.ShapeDtypeStruct((vt, d), F32)] * n_own + [
             jax.ShapeDtypeStruct((n_t // 2, rows, d), F32),
             jax.ShapeDtypeStruct((8, 128), F32),
         ],
@@ -753,12 +829,12 @@
             pltpu.VMEM((8, 128), F32),
             dma((2,)), dma((2,)), dma((2,)), dma, dma, dma((4,)), dma((4,)), dma((4,)),
             dma((n_t,)), dma((n_t,)), dma((n_t, 2)), dma((n_t, 2)), dma((n_t,)), dma((n_t,)), dma((n_t // 2,)), dma((n_t // 2,)),
-            dma((4, 3)), dma((4, 3)), dma, dma((2,)),
+            dma((4, 3)), dma((4, 3)), dma, dma((2,)), dma((2,)), dma((2,)), dma((2, 2)),
         ],
         compiler_params=pltpu.CompilerParams(vmem_limit_bytes=67043328, collective_id=1, has_side_effects=True),
         cost_estimate=_cost(4 * n_t * n * d * win, 4 * n_t * n * win, n_t * n * win),
         name="grads",
-    )(lab, coef, z, x, w)
+    )(lab, coef, z, x, w, act, w1, w2)
 
 
 def solution(mesh):
@@ -794,7 +870,7 @@
         z, x_all, w_win, coef = head(x_rows, w_head, lab_two.reshape(2, 1, n_tok), loss_mask.reshape(1, -1), n_stage, win, logits_tile(win))
         n_t, _, rows, _ = x_all.shape
         lab = lab_two[::-1].reshape(2, n_stage, n_t // 2, rows).transpose(0, 2, 1, 3).reshape(n_t, 1, n_stage * rows)
-        grad_head, _, _, _, gx, loss = grads(lab, coef, z, x_all, w_win, vt, shard)
+        grad_head, mlp_out, _, _, _, gx, loss = grads(lab, coef, z, x_all, w_win, vt, shard, act_in, w_up[0], w_down[0])
         grad_x = gx.reshape(x_rows.shape)
         mean_loss = loss[0, 0]
 
@@ -806,8 +882,6 @@
         emb_part, _ = lax.optimization_barrier((emb_part, coef))
         embed_out = lax.psum_scatter(emb_part, "stage", scatter_dimension=0, tiled=True)
 
-        mlp_out = mlp(act_in, w_up[0], w_down[0], None, 0, n_tok // 512)
-
         return mean_loss.reshape(1), grad_x, grad_head, embed_out, mlp_out
 
     return jax.shard_map(

time: 440 us -> 389 us (0.88)
  Pallas kernels: 374 us -> 315 us
  local copies, waits for them, and re-layouts: 38.1 us -> 44 us
    pallas_call x1 -> x0, Pallas kernels: 47.2 us -> none  [mlp(): pl.pallas_call(functools.partial(_mlp_body, chunk=512), grid=(count,), in...]
    pallas_call x1, Pallas kernels: 243 us -> 231 us  [grads(): pl.pallas_call(functools.partial(_grads_body, n_stage=n_stage, first_row=...]
    unnamed x4 -> x5, local copies, waits for them, and re-layouts: 10.8 us -> 16.7 us
  transfers between devices with their start and end apart: 2 -> 2, of which waited for: 0 -> 0; matrix products, arithmetic and copies ran while one was open for 8% -> 9% of each run, Pallas kernels for 66% -> 60%
where the time goes in v5:
time: 389 us; the launch traced here: 386 us
  Pallas kernels  315 us (81%)
  local copies, waits for them, and re-layouts  44 us (11%)
  between operations  14.1 us (4%)
  other arithmetic  9.45 us (2%)
    pallas_call x1, Pallas kernels, grads(): pl.pallas_call(functools.partial(_grads_body, n_stage=n_stage, first_row=...  231 us
    pallas_call x1, Pallas kernels, head(): pl.pallas_call(functools.partial(_head_body, n_stage=n_stage, first_row=s...  84.3 us
    gather x1, local copies, waits for them, and re-layouts, local_step(): rows_emb = jnp.take(w_embed, jnp.clip(local_ids, 0, shard - 1), axis=0)  24 us
    unnamed x5, local copies, waits for them, and re-layouts  16.7 us
    select_n x1, other arithmetic, local_step(): emb_part = jnp.where(in_slice[:, None], rows_emb, jnp.zeros_like(rows_emb))  7.95 us
  transfers between devices with their start and end apart: 2, of which 0 were waited for; matrix products, arithmetic and copies ran while one was open for 9% of the time, Pallas kernels for 60%

profile of v5, /device:TPU:97, one launch (start us, length us, event | category | flops | bytes accessed | tf_op | source)
XLA Modules:
  0.0 385.9 jit_solution(10895386554953797988)
XLA Ops:
  7.2 0.1 reduce-scatter.2.cloned.1.call-start
  7.2 2.8 collective-permute-start
  10.0 0.7 compare_and_fusion.1
  10.7 0.7 fusion
  11.5 24.0 %gather_fusion = bf16[4096,768]{1,0:T(8,128)(2,1)} fusion(bf16[6288,768]{1,0:T(8,128)(2,1)} %param.13, s32[4096]{0:T(1024)S(1)} %fusion), kind=kCustom, calls=%fused_computation | custom fusion | bytes 12599296 | tf_op jit(solution)/shard_map/jit(_take)/gather | solution.py:880
  35.5 0.0 copy-start
  35.5 7.9 %select_select_fusion = bf16[4096,768]{1,0:T(8,128)(2,1)} fusion(bf16[4096,768]{1,0:T(8,128)(2,1)} %gather_fusion, pred[4096]{0:T(1024)(128)(4,1)S(1)} %get-tuple-element.24, pred[4096]{0:T(1024)(128)(4,1)S(1)} %get-tuple-element.23), kind=kLoop, calls=%fused_computation.1 | loop fusion | flops 6291456 | bytes 12591104 | tf_op jit(solution)/shard_map/jit(_where)/select_n | solution.py:881
  43.5 0.0 copy-done
  43.5 0.0 collective-permute-done
  43.6 0.6 reshape.37.lab_ref
  44.2 84.3 %head.1 = (f32[8,8,3168,128]{3,2,1,0:T(8,128)}, bf16[8,8,128,768]{3,2,1,0:T(8,128)(2,1)}, bf16[3168,768]{1,0:T(8,128)(2,1)}, f32[8,8,1024]{2,1,0:T(8,128)}) custom-call(bf16[4,128,768]{2,1,0:T(8,128)(2,1)} %bitcast.17, bf16[6288,768]{1,0:T(8,128)(2,1)} %wh_ref.1, s32[2,1,4096]{2,1,0:T(1,128)} %reshape.37.lab_ref, s32[1,4096]{1,0:T(1,128)} %bitcast.18), custom_call_target="tpu_custom_call" | custom-call | flops 39862665216 | bytes 103809024 | tf_op jit(solution)/shard_map/head/pallas_call | solution.py:312
  128.5 0.1 reduce-scatter.2.cloned.1.call-update
  128.6 0.8 rev.3
  129.4 0.6 copy.14
  130.1 231.0 %grads.1 = (bf16[6288,768]{1,0:T(8,128)(2,1)}, bf16[4096,768]{1,0:T(8,128)(2,1)}, f32[512,768]{1,0:T(8,128)}, f32[512,768]{1,0:T(8,128)}, f32[512,768]{1,0:T(8,1...) custom-call(s32[8,1,1024]{2,1,0:T(1,128)} %bitcast.14, f32[8,8,1024]{2,1,0:T(8,128)} %get-tuple-element.14.coef_ref, ...), custom_call_target="tpu_custom_call" | custom-call | flops 79725330432 | bytes 103809024 | tf_op jit(solution)/shard_map/grads/pallas_call | solution.py:811
  361.1 1.2 slice.3
  362.3 0.0 reduce-scatter.2.cloned.1.call-done
  362.3 2.7 copy.18
  364.9 8.2 %copy.19 = bf16[6288,768]{1,0:T(8,128)(2,1)} copy(bf16[6288,768]{1,0:T(8,128)(2,1)} %get-tuple-element.32) | data formatting | bytes 19316736
  373.1 5.9 %copy.20 = bf16[4096,768]{1,0:T(8,128)(2,1)} copy(bf16[4096,768]{1,0:T(8,128)(2,1)} %get-tuple-element.34) | data formatting | bytes 12582912
  (4 shorter events, 0.1 us)
Async XLA Ops:
  7.2 355.1 %reduce-scatter.2.cloned.1.call-start = ((), (), s32[]{:S(2)}) async-start(), calls=%async_computation.1 | async-start | bytes 7077888 | tf_op jit(solution)/shard_map/reduce_scatter | solution.py:883
  7.2 36.2 %collective-permute-start = (s32[4096]{0:T(1024)}, s32[4096]{0:T(1024)S(1)}, u32[]{:S(2)}, u32[]{:S(2)}) collective-permute-start(s32[4096]{0:T(1024)} %param.11), channel_id=1, source_target_pairs={{0,8},{8,0},{16,24},{24,16},{1,9},{9,1},{17,25},{25,17},{2,10},{10... | collective-permute-start | bytes 49160 | tf_op jit(solution)/shard_map/ppermute | solution.py:860
  35.5 8.0 %copy-start = (s32[4096]{0:T(1024)S(1)}, s32[4096]{0:T(1024)}, u32[]{:S(2)}) copy-start(s32[4096]{0:T(1024)} %param.11) | copy-start | bytes 49156
Sparse Core Ops, SparseCore 0:
  128.7 39.8 reduce-scatter.1

commit v6 on v5

--- a/solution.py
+++ b/solution.py
@@ -55,9 +55,9 @@
 
 
 def _head_body(
-    x_ref, wh_ref, lab_ref, mask_ref, z_ref, xo_ref, wo_ref, coef_out,
-    xbuf, wbuf, zbuf, st, got, mine, coef,
-    own_sem, w_sem, wo_sem, z_sem, xo_sem, xs_sem, xr_sem, send1, recv1, send2, recv2, *, n_stage, first_row, over, vt,
+    x_ref, wh_ref, lab_ref, mask_ref, emb_ref, hit_ref, z_ref, xo_ref, wo_ref, eo_ref, coef_out,
+    xbuf, wbuf, zbuf, st, got, mine, coef, ebuf,
+    ei_sem, eo_sem, own_sem, w_sem, wo_sem, z_sem, xo_sem, xs_sem, xr_sem, send1, recv1, send2, recv2, *, n_stage, first_row, over, vt,
 ):
     y, s = lax.axis_index("data"), lax.axis_index("stage")
     h = lax.rem(y + y // 2, 2)
@@ -132,6 +132,29 @@
     w_load = pltpu.make_async_copy(wh_ref.at[pl.ds(pl.multiple_of(h * first_row, 16), win), :], wbuf, w_sem)
     w_load.start()
 
+    def emb_in(e):
+        return pltpu.make_async_copy(emb_ref.at[e], ebuf.at[e % 2], ei_sem.at[e % 2])
+
+    def emb_out(e):
+        return pltpu.make_async_copy(ebuf.at[e % 2], eo_ref.at[e], eo_sem.at[e % 2])
+
+    def select(e, carry):
+        emb_in(e).wait()
+        hit = jnp.concatenate([hit_ref[e]] * (ebuf.shape[2] // hit_ref.shape[2]), axis=1)
+        v = ebuf[e % 2]
+        ebuf[e % 2] = jnp.where(hit != 0, v, jnp.zeros_like(v))
+        emb_out(e).start()
+
+        @pl.when(jnp.logical_and(e >= 1, e + 1 < n_stage))
+        def _():
+            emb_out(e - 1).wait()
+            emb_in(e + 1).start()
+
+        return carry
+
+    emb_in(0).start()
+    emb_in(1).start()
+
     peers = [(f, k) for f in range(2) for k in range(n_stage) if (f, k) != (0, 0)]
 
     def peer(f, k):
@@ -170,6 +193,7 @@
 
         @pl.when(i == 2)
         def _():
+            lax.fori_loop(0, n_stage, select, 0)
             got_block(1, s)
             got_block(0, left)
             got_block(0, right)
@@ -286,6 +310,8 @@
     for i in range(n_blk):
         x_copy(i // n_stage, i % n_stage).wait()
     w_out.wait()
+    emb_out(n_stage - 2).wait()
+    emb_out(n_stage - 1).wait()
     for k in range(len(sends)):
         copy(k).wait_send()
     for c1 in first:
@@ -297,7 +323,7 @@
         c2.wait_send()
 
 
-def head(x_rows, w_head, lab, mask, n_stage, win, vt):
+def head(x_rows, w_head, lab, mask, emb, hit, n_stage, win, vt):
     rows, d = x_rows.shape
     n_q = 4
     hr = rows // n_q
@@ -311,12 +337,13 @@
     total = n_blk * rows
     return pl.pallas_call(
         functools.partial(_head_body, n_stage=n_stage, first_row=shard - win, over=2 * win - shard, vt=vt),
-        in_specs=[hbm, hbm, vm, vm],
-        out_specs=[hbm, hbm, hbm, vm],
+        in_specs=[hbm, hbm, vm, vm, hbm, vm],
+        out_specs=[hbm, hbm, hbm, hbm, vm],
         out_shape=[
             jax.ShapeDtypeStruct((2 * n_q, n_stage, win, hr), F32),
             jax.ShapeDtypeStruct((2 * n_q, n_stage, hr, d), BF16),
             jax.ShapeDtypeStruct((win, d), BF16),
+            jax.ShapeDtypeStruct(emb.shape, BF16),
             jax.ShapeDtypeStruct((2 * n_q, 8, n), F32),
         ],
         scratch_shapes=[
@@ -327,13 +354,14 @@
             pltpu.VMEM((n_blk, n_q, 8, hr), F32),
             pltpu.VMEM((n_q, 8, hr), F32),
             pltpu.VMEM((2 * n_q, 8, n), F32),
-            dma, dma, dma, dma((2, n_q)), dma((n_blk,)), dma((16,)), dma((n_blk + 1,)),
+            pltpu.VMEM((2, *emb.shape[1:]), BF16),
+            dma((2,)), dma((2,)), dma, dma, dma, dma((2, n_q)), dma((n_blk,)), dma((16,)), dma((n_blk + 1,)),
             dma((n_blk,)), dma((n_blk,)), dma((n_blk,)), dma((n_blk,)),
         ],
         compiler_params=_params(56, collective_id=0, has_side_effects=True),
         cost_estimate=_cost(2 * total * d * win, 4 * total * win, total * win),
         name="head",
-    )(x3, w_head, lab, mask)
+    )(x3, w_head, lab, mask, emb, hit)
 
 
 DONE = (12, 17, 27, 31, 35, 41, 44, 47)
@@ -345,8 +373,8 @@
 
 PHASES = ((0, 1, 0, 0), (8, 5, 1, 0), (18, 1, 1, 2), (24, 4, 2, 2), (36, 1, 2, 5), (39, 3, 3, 5))
 EVENTS = (
-    (48, "2", 3), (48, "fin", 0), (49, "fin", 1), (53, "d", 7), (54, "tail", 0), (59, "2", 4), (60, "1", 5), (65, "fin", 2), (67, "1", 6), (70, "pass", 0),
-    (73, "2", 5), (75, "1", 7), (80, "2", 6), (83, "pass", 1), (87, "2", 7), (98, "pass", 2),
+    (48, "2", 3), (48, "fin", 0), (49, "d", 7), (49, "fin", 1), (53, "1", 5), (53, "fin", 2), (53, "fb", 0), (54, "2", 4), (56, "tail", 0),
+    (60, "1", 6), (61, "2", 5), (62, "pass", 0), (65, "1", 7), (68, "2", 6), (70, "pass", 1), (72, "2", 7), (83, "pass", 2),
 )
 MLP_FROM = 50
 MLP_CHUNK = 512
@@ -358,13 +386,15 @@
     x_base = w_base = 0
     ends = [p[0] for p in PHASES[1:]] + [N_STEP]
     for (start, n_tile, tile0, group0), end in zip(PHASES, ends):
-        k = jnp.maximum(u - start, 0)
+        k = u - start
         on = u >= start
-        tile = jnp.where(on, tile0 + k % n_tile, tile)
-        group = jnp.where(on, group0 + k // n_tile, group)
-        xi = jnp.where(on, x_base + k // n_tile, xi)
+        turn = k if n_tile == 1 else sum(jnp.where(k >= i, 1, 0) for i in range(n_tile, end - start, n_tile))
+        place = k - n_tile * turn
+        tile = jnp.where(on, tile0 + place, tile)
+        group = jnp.where(on, group0 + turn, group)
+        xi = jnp.where(on, x_base + turn, xi)
         wi = jnp.where(on, w_base + (k if n_tile > 1 else 0), wi)
-        new_x = jnp.where(on, k % n_tile == 0, new_x)
+        new_x = jnp.where(on, place == 0, new_x)
         new_w = jnp.where(on, True if n_tile > 1 else k == 0, new_w)
         x_base += (end - start) // n_tile
         w_base += end - start if n_tile > 1 else 1
@@ -407,8 +437,9 @@
         )
 
     def row0(tile):
-        half = jnp.where(tile < n_own, 1 - yh, yh)
-        return pl.multiple_of((half * n_own + tile % n_own) * vt, vt)
+        far = tile < n_own
+        half = jnp.where(far, 1 - yh, yh)
+        return pl.multiple_of((half * n_own + tile - jnp.where(far, 0, n_own)) * vt, vt)
 
     peers = (to_sib, to_a, to_b, stage_at(x_1), stage_at(x_3))
     barrier = pltpu.get_barrier_semaphore()
@@ -703,7 +734,8 @@
 
             lax.fori_loop(0, vt // piece, add, 0)
             fin_copy(j, 0).start()
-            fin_copy(j, 1).start()
+            if j > 0:
+                fin_copy(j, 1).start()
             fin_local(j).start()
 
         def tail_copy(hh, remote_copy):
@@ -716,6 +748,8 @@
         def event(what, j):
             if what == "fin":
                 finish_tile(j)
+            elif what == "fb":
+                fin_copy(j, 1).start()
             elif what == "d":
                 exchange_d(j)
             elif what == "1":
@@ -847,7 +881,7 @@
 
     def local_step(x_rows, w_head, labels, loss_mask, w_embed, tok_ids, act_in, w_up, w_down):
         y, s = lax.axis_index("data"), lax.axis_index("stage")
-        shard, _ = w_head.shape
+        shard, d = w_head.shape
         yh = y >> 1
         h = (y ^ yh) & 1
         step_rows = 16 * N_TILE
@@ -867,19 +901,20 @@
 
         n_tok = labels.shape[0]
         lab_two = jnp.stack([local(labels), local(lab_a)])
-        z, x_all, w_win, coef = head(x_rows, w_head, lab_two.reshape(2, 1, n_tok), loss_mask.reshape(1, -1), n_stage, win, logits_tile(win))
+        local_ids = tok_ids - s * shard
+        in_slice = (local_ids >= 0) & (local_ids < shard)
+        rows_emb = w_embed.at[jnp.clip(local_ids, 0, shard - 1)].get(mode="promise_in_bounds").reshape(n_stage, -1, d)
+        hit = jnp.broadcast_to(in_slice[:, None], (n_tok, 128)).astype(BF16).reshape(n_stage, -1, 128)
+        z, x_all, w_win, emb_part, coef = head(
+            x_rows, w_head, lab_two.reshape(2, 1, n_tok), loss_mask.reshape(1, -1), rows_emb, hit, n_stage, win, logits_tile(win)
+        )
+        emb_part = emb_part.reshape(n_tok, d)
         n_t, _, rows, _ = x_all.shape
         lab = lab_two[::-1].reshape(2, n_stage, n_t // 2, rows).transpose(0, 2, 1, 3).reshape(n_t, 1, n_stage * rows)
         grad_head, mlp_out, _, _, _, gx, loss = grads(lab, coef, z, x_all, w_win, vt, shard, act_in, w_up[0], w_down[0])
         grad_x = gx.reshape(x_rows.shape)
         mean_loss = loss[0, 0]
 
-        offset = s * shard
-        local_ids = tok_ids - offset
-        in_slice = (local_ids >= 0) & (local_ids < shard)
-        rows_emb = jnp.take(w_embed, jnp.clip(local_ids, 0, shard - 1), axis=0)
-        emb_part = jnp.where(in_slice[:, None], rows_emb, jnp.zeros_like(rows_emb))
-        emb_part, _ = lax.optimization_barrier((emb_part, coef))
         embed_out = lax.psum_scatter(emb_part, "stage", scatter_dimension=0, tiled=True)
 
         return mean_loss.reshape(1), grad_x, grad_head, embed_out, mlp_out

time: 389 us -> 375 us (0.964)
  other arithmetic: 9.45 us -> 2.21 us
  Pallas kernels: 315 us -> 308 us
    pallas_call x1, Pallas kernels: 231 us -> 222 us  [grads(): pl.pallas_call(functools.partial(_grads_body, n_stage=n_stage, first_row=...]
    select_n x1 -> x0, other arithmetic: 7.95 us -> none  [local_step(): emb_part = jnp.where(in_slice[:, None], rows_emb, jnp.zeros_like(rows_emb))]
    unnamed x5 -> x3, local copies, waits for them, and re-layouts: 16.7 us -> 16.7 us
  transfers between devices with their start and end apart: 2 -> 2, of which waited for: 0 -> 0; matrix products, arithmetic and copies ran while one was open for 9% -> 8% of each run, Pallas kernels for 60% -> 60%
where the time goes in v6:
time: 375 us; the launch traced here: 372 us
  Pallas kernels  308 us (82%)
  local copies, waits for them, and re-layouts  45.6 us (12%)
  between operations  14.1 us (4%)
    pallas_call x1, Pallas kernels, grads(): pl.pallas_call(functools.partial(_grads_body, n_stage=n_stage, first_row=...  222 us
    pallas_call x1, Pallas kernels, head(): pl.pallas_call(functools.partial(_head_body, n_stage=n_stage, first_row=s...  85.1 us
    gather x1, local copies, waits for them, and re-layouts, local_step(): w_embed.at[jnp.clip(local_ids, 0, shard - 1)].get(mode='promise_in_bounds')  24 us
    unnamed x3, local copies, waits for them, and re-layouts  16.7 us
  transfers between devices with their start and end apart: 2, of which 0 were waited for; matrix products, arithmetic and copies ran while one was open for 8% of the time, Pallas kernels for 60%

profile of v6, /device:TPU:97, one launch (start us, length us, event | category | flops | bytes accessed | tf_op | source)
XLA Modules:
  0.0 372.4 jit_solution(51541219932704276)
XLA Ops:
  7.2 0.1 reduce-scatter.2.cloned.1.call-start
  7.2 2.8 collective-permute-start
  10.0 0.7 fusion
  10.7 0.7 compare_select_fusion.2
  11.5 0.7 and_convert_fusion
  12.2 24.0 %gather_fusion = bf16[4096,768]{1,0:T(8,128)(2,1)} fusion(bf16[6288,768]{1,0:T(8,128)(2,1)} %param.13, s32[4096]{0:T(1024)S(1)} %fusion), kind=kCustom, calls=%fused_computation | custom fusion | bytes 12599296 | tf_op jit(solution)/shard_map/gather | solution.py:906
  36.3 0.0 collective-permute-done
  36.3 0.6 reshape.44.lab_ref
  36.9 1.6 broadcast_in_dim.22.hit_ref
  38.5 85.1 %head.1 = (f32[8,8,3168,128]{3,2,1,0:T(8,128)}, bf16[8,8,128,768]{3,2,1,0:T(8,128)(2,1)}, bf16[3168,768]{1,0:T(8,128)(2,1)}, bf16[8,512,768]{2,1,0:T(8,128)(2,1)}, f32[8,8,1024]{2,1,0:T(8,128)}) custom-call(bf16[4,128,768]{2,1,0:T(8,128)(2,1)} %bitcast.21, bf16[6288,768]{1,0:T(8,128)(2,1)} %wh_ref.1, s32[2,1,4096]{2,1,0:T(1,128)} %reshape.44.lab_ref, ...), custom_call_target="tpu_custom_call" | custom-call | flops 39862665216 | bytes 103809024 | tf_op jit(solution)/shard_map/head/pallas_call | solution.py:338
  123.6 0.1 reduce-scatter.2.cloned.1.call-update
  123.7 0.8 rev.3
  124.5 0.6 copy.14
  125.1 222.4 %grads.1 = (bf16[6288,768]{1,0:T(8,128)(2,1)}, bf16[4096,768]{1,0:T(8,128)(2,1)}, f32[512,768]{1,0:T(8,128)}, f32[512,768]{1,0:T(8,128)}, f32[512,768]{1,0:T(8,1...) custom-call(s32[8,1,1024]{2,1,0:T(1,128)} %bitcast.18, f32[8,8,1024]{2,1,0:T(8,128)} %get-tuple-element.14.coef_ref, ...), custom_call_target="tpu_custom_call" | custom-call | flops 79725330432 | bytes 103809024 | tf_op jit(solution)/shard_map/grads/pallas_call | solution.py:845
  347.6 1.2 slice.3
  348.8 0.0 reduce-scatter.2.cloned.1.call-done
  348.8 2.7 copy.18
  351.4 8.2 %copy.19 = bf16[6288,768]{1,0:T(8,128)(2,1)} copy(bf16[6288,768]{1,0:T(8,128)(2,1)} %get-tuple-element.30) | data formatting | bytes 19316736
  359.6 5.9 %copy.20 = bf16[4096,768]{1,0:T(8,128)(2,1)} copy(bf16[4096,768]{1,0:T(8,128)(2,1)} %get-tuple-element.32) | data formatting | bytes 12582912
  (4 shorter events, 0.1 us)
Async XLA Ops:
  7.2 341.6 %reduce-scatter.2.cloned.1.call-start = ((), (), s32[]{:S(2)}) async-start(), calls=%async_computation.1 | async-start | bytes 7077888 | tf_op jit(solution)/shard_map/reduce_scatter | solution.py:918
  7.2 29.0 %collective-permute-start = (s32[4096]{0:T(1024)}, s32[4096]{0:T(1024)S(1)}, u32[]{:S(2)}, u32[]{:S(2)}) collective-permute-start(s32[4096]{0:T(1024)} %param.11), channel_id=1, source_target_pairs={{0,8},{8,0},{16,24},{24,16},{1,9},{9,1},{17,25},{25,17},{2,10},{10... | collective-permute-start | bytes 49160 | tf_op jit(solution)/shard_map/ppermute | solution.py:894
Sparse Core Ops, SparseCore 0:
  123.8 39.8 reduce-scatter.1

commit v7 on v6

--- a/solution.py
+++ b/solution.py
@@ -367,6 +367,7 @@
 DONE = (12, 17, 27, 31, 35, 41, 44, 47)
 SENT = (7, 23, 38)
 N_STEP = 48
+Z_SLOTS = 3
 AFTER_D, AFTER_1, AFTER_2 = 3, 12, 18
 SLOTS_1, SLOTS_2 = 6, 4
 
@@ -441,20 +442,21 @@
         half = jnp.where(far, 1 - yh, yh)
         return pl.multiple_of((half * n_own + tile - jnp.where(far, 0, n_own)) * vt, vt)
 
-    peers = (to_sib, to_a, to_b, stage_at(x_1), stage_at(x_3))
-    barrier = pltpu.get_barrier_semaphore()
-    for p in peers:
-        pl.semaphore_signal(barrier, inc=1, device_id=p, device_id_type=MESH)
-    pl.semaphore_wait(barrier, len(peers))
-
-    loss_part = [jnp.sum(coef_ref[i * n_t // 2:(i + 1) * n_t // 2, 3:4, :]) for i in range(2)]
-    loss_pair = loss_part[0] + loss_part[1]
-    ls[...] = jnp.full(ls.shape, loss_pair, F32)
-
     def send_loss():
         return remote(ls, lr, l_sem.at[0], l_sem.at[1], to_b)
 
-    send_loss().start()
+    def meet():
+        peers = (to_sib, to_a, to_b, stage_at(x_1), stage_at(x_3))
+        barrier = pltpu.get_barrier_semaphore()
+        for p in peers:
+            pl.semaphore_signal(barrier, inc=1, device_id=p, device_id_type=MESH)
+        pl.semaphore_wait(barrier, len(peers))
+
+        loss_part = [jnp.sum(coef_ref[i * n_t // 2:(i + 1) * n_t // 2, 3:4, :]) for i in range(2)]
+        loss_pair = loss_part[0] + loss_part[1]
+        ls[...] = jnp.full(ls.shape, loss_pair, F32)
+
+        send_loss().start()
 
     def send_d(t):
         return remote(dxb.at[t, :, 1 - c], rd.at[t % 2], sd_sem.at[t], rd_sem.at[t], to_sib)
@@ -529,10 +531,20 @@
         return remote(dwb.at[j], rcv[j], sb_sem.at[j], rb_sem.at[j], to_b)
 
     def products(zb, xb, wb, zt, wt, g, gt):
+        def z_whole(u):
+            tile, t = _step_of(u)[:2]
+            return pltpu.make_async_copy(z_ref.at[t, :, pl.ds(row0(tile), vt), :], zb.at[u % Z_SLOTS], z_sem.at[u % Z_SLOTS])
+
+        def z_load(u):
+            tile, t = _step_of(u)[:2]
+            for i in range(0, n_stage, 2):
+                part = pl.ds(i, 2)
+                pltpu.make_async_copy(z_ref.at[t, part, pl.ds(row0(tile), vt), :], zb.at[u % Z_SLOTS, part], z_sem.at[u % Z_SLOTS]).start()
+
         def whole(u):
             tile, t, xk, wk, new_x, new_w = _step_of(u)
             return (
-                pltpu.make_async_copy(z_ref.at[t, :, pl.ds(row0(tile), vt), :], zb.at[u % 2], z_sem.at[u % 2]),
+                z_whole(u),
                 pltpu.make_async_copy(x_ref.at[t], xb.at[xk], x_sem.at[xk]),
                 pltpu.make_async_copy(w_ref.at[pl.ds(row0(tile), vt), :], wb.at[wk], w_sem.at[wk]),
                 new_x, new_w,
@@ -541,8 +553,6 @@
         def load(u):
             tile, t, xk, wk, new_x, new_w = _step_of(u)
             r0 = row0(tile)
-            for i in range(n_stage):
-                pltpu.make_async_copy(z_ref.at[t, i, pl.ds(r0, vt), :], zb.at[u % 2, i], z_sem.at[u % 2]).start()
 
             @pl.when(new_x)
             def _():
@@ -571,9 +581,12 @@
         def tail_load(t):
             return pltpu.make_async_copy(z_ref.at[t, :, pl.ds(tail_row, n_tail), :], zt, zt_sem)
 
+        z_load(jnp.int32(0))
         load(jnp.int32(0))
+        z_load(jnp.int32(1))
         w_tail = pltpu.make_async_copy(w_ref.at[pl.ds(tail_row, n_tail), :], wt, wt_sem)
         w_tail.start()
+        meet()
         w_tail.wait()
 
         def step(u, carry):
@@ -584,6 +597,10 @@
             def _():
                 load(u + 1)
 
+            @pl.when(u < N_STEP - 2)
+            def _():
+                z_load(u + 2)
+
             last = tile == 2 * n_own - 1
 
             @pl.when(last)
@@ -591,7 +608,7 @@
                 tail_load(t).start()
 
             exchanges(u)
-            g_tile(zb.at[u % 2], g, t, row0(tile))
+            g_tile(zb.at[u % Z_SLOTS], g, t, row0(tile))
             x_t = xb[xk].reshape(n_stage * rows, d)
             for xx in range(n_x):
                 gx = g[:, 2 * xx * rows:2 * (xx + 1) * rows]
@@ -604,8 +621,10 @@
                 tail_load(t).wait()
                 g_tile(zt, gt, t, tail_row)
                 x_t = xb[xk].reshape(n_stage * rows, d)
-                dxp = lax.dot_general(gt[...], wt[...], (((0,), (0,)), ((), ())), preferred_element_type=F32)
-                dxb[t] = dxb[t] + dxp.reshape(n_x, 2, rows, d)
+                for xx in range(n_x):
+                    gx = gt[:, 2 * xx * rows:2 * (xx + 1) * rows]
+                    dxp = lax.dot_general(gx, wt[...], (((0,), (0,)), ((), ())), preferred_element_type=F32)
+                    dxb[t, xx] = dxb[t, xx] + dxp.reshape(2, rows, d)
                 dwt[...] = jnp.where(t == 0, 0.0, dwt[...]) + jnp.dot(gt[...], x_t, preferred_element_type=F32)
                 send_d(t).start()
 
@@ -621,7 +640,7 @@
     n_lane = n_stage * rows
     pl.run_scoped(
         products,
-        pltpu.VMEM((2, n_stage, vt, rows), F32),
+        pltpu.VMEM((Z_SLOTS, n_stage, vt, rows), F32),
         pltpu.VMEM((2, n_stage, rows, d), BF16),
         pltpu.VMEM((2, vt, d), BF16),
         pltpu.VMEM((n_stage, n_tail, rows), F32),
@@ -861,7 +880,7 @@
             pltpu.VMEM((n_t // 2, rows, d), F32),
             pltpu.VMEM((8, 128), F32),
             pltpu.VMEM((8, 128), F32),
-            dma((2,)), dma((2,)), dma((2,)), dma, dma, dma((4,)), dma((4,)), dma((4,)),
+            dma((Z_SLOTS,)), dma((2,)), dma((2,)), dma, dma, dma((4,)), dma((4,)), dma((4,)),
             dma((n_t,)), dma((n_t,)), dma((n_t, 2)), dma((n_t, 2)), dma((n_t,)), dma((n_t,)), dma((n_t // 2,)), dma((n_t // 2,)),
             dma((4, 3)), dma((4, 3)), dma, dma((2,)), dma((2,)), dma((2,)), dma((2, 2)),
         ],

time: 375 us -> 373 us (level)
  no operation moved by 1% of the time
where the time goes in v7:
time: 373 us; the launch traced here: 372 us
  Pallas kernels  307 us (82%)
  local copies, waits for them, and re-layouts  45.6 us (12%)
  between operations  14.1 us (4%)
    pallas_call x1, Pallas kernels, grads(): pl.pallas_call(functools.partial(_grads_body, n_stage=n_stage, first_row=...  222 us
    pallas_call x1, Pallas kernels, head(): pl.pallas_call(functools.partial(_head_body, n_stage=n_stage, first_row=s...  85.1 us
    gather x1, local copies, waits for them, and re-layouts, local_step(): w_embed.at[jnp.clip(local_ids, 0, shard - 1)].get(mode='promise_in_bounds')  24 us
    unnamed x3, local copies, waits for them, and re-layouts  16.7 us
  transfers between devices with their start and end apart: 2, of which 0 were waited for; matrix products, arithmetic and copies ran while one was open for 8% of the time, Pallas kernels for 60%

profile of v7, /device:TPU:97, one launch (start us, length us, event | category | flops | bytes accessed | tf_op | source)
XLA Modules:
  0.0 371.7 jit_solution(10478448561148585992)
XLA Ops:
  7.2 0.1 reduce-scatter.2.cloned.1.call-start
  7.2 2.8 collective-permute-start
  10.0 0.7 fusion
  10.7 0.7 compare_select_fusion.2
  11.5 0.7 and_convert_fusion
  12.2 24.0 %gather_fusion = bf16[4096,768]{1,0:T(8,128)(2,1)} fusion(bf16[6288,768]{1,0:T(8,128)(2,1)} %param.13, s32[4096]{0:T(1024)S(1)} %fusion), kind=kCustom, calls=%fused_computation | custom fusion | bytes 12599296 | tf_op jit(solution)/shard_map/gather | solution.py:925
  36.3 0.0 collective-permute-done
  36.3 0.6 reshape.44.lab_ref
  36.9 1.6 broadcast_in_dim.22.hit_ref
  38.5 85.1 %head.1 = (f32[8,8,3168,128]{3,2,1,0:T(8,128)}, bf16[8,8,128,768]{3,2,1,0:T(8,128)(2,1)}, bf16[3168,768]{1,0:T(8,128)(2,1)}, bf16[8,512,768]{2,1,0:T(8,128)(2,1)}, f32[8,8,1024]{2,1,0:T(8,128)}) custom-call(bf16[4,128,768]{2,1,0:T(8,128)(2,1)} %bitcast.21, bf16[6288,768]{1,0:T(8,128)(2,1)} %wh_ref.1, s32[2,1,4096]{2,1,0:T(1,128)} %reshape.44.lab_ref, ...), custom_call_target="tpu_custom_call" | custom-call | flops 39862665216 | bytes 103809024 | tf_op jit(solution)/shard_map/head/pallas_call | solution.py:338
  123.6 0.1 reduce-scatter.2.cloned.1.call-update
  123.7 0.8 rev.3
  124.5 0.6 copy.14
  125.1 221.8 %grads.1 = (bf16[6288,768]{1,0:T(8,128)(2,1)}, bf16[4096,768]{1,0:T(8,128)(2,1)}, f32[512,768]{1,0:T(8,128)}, f32[512,768]{1,0:T(8,128)}, f32[512,768]{1,0:T(8,1...) custom-call(s32[8,1,1024]{2,1,0:T(1,128)} %bitcast.18, f32[8,8,1024]{2,1,0:T(8,128)} %get-tuple-element.14.coef_ref, ...), custom_call_target="tpu_custom_call" | custom-call | flops 79725330432 | bytes 103809024 | tf_op jit(solution)/shard_map/grads/pallas_call | solution.py:864
  346.9 1.2 slice.3
  348.1 0.0 reduce-scatter.2.cloned.1.call-done
  348.1 2.7 copy.18
  350.8 8.2 %copy.19 = bf16[6288,768]{1,0:T(8,128)(2,1)} copy(bf16[6288,768]{1,0:T(8,128)(2,1)} %get-tuple-element.30) | data formatting | bytes 19316736
  359.0 5.9 %copy.20 = bf16[4096,768]{1,0:T(8,128)(2,1)} copy(bf16[4096,768]{1,0:T(8,128)(2,1)} %get-tuple-element.32) | data formatting | bytes 12582912
  (4 shorter events, 0.1 us)
Async XLA Ops:
  7.2 340.9 %reduce-scatter.2.cloned.1.call-start = ((), (), s32[]{:S(2)}) async-start(), calls=%async_computation.1 | async-start | bytes 7077888 | tf_op jit(solution)/shard_map/reduce_scatter | solution.py:937
  7.2 29.0 %collective-permute-start = (s32[4096]{0:T(1024)}, s32[4096]{0:T(1024)S(1)}, u32[]{:S(2)}, u32[]{:S(2)}) collective-permute-start(s32[4096]{0:T(1024)} %param.11), channel_id=1, source_target_pairs={{0,8},{8,0},{16,24},{24,16},{1,9},{9,1},{17,25},{25,17},{2,10},{10... | collective-permute-start | bytes 49160 | tf_op jit(solution)/shard_map/ppermute | solution.py:913
Sparse Core Ops, SparseCore 0:
  123.8 39.8 reduce-scatter.1
